TPU v7x, 32 devices: a 4x4x1 block of a 4x4x8 slice. The times are simulated.
32 devices in a mesh: dp: 1 (over z), tp: 32 (over y, x, core).
Axes of the slice: x: 4, y: 4, z: 1, core: 2. Of those that a mesh axis runs over, the one named last changes fastest.
The devices are a block of a 4x4x8 slice.
Arguments:
- q_hidden: bfloat16 [512, 8, 4096], P(('dp', 'tp'))
- d_hidden: bfloat16 [64, 32, 4096], P(('dp', 'tp'))
- q_mask: int32 [512, 8], P(('dp', 'tp'))
- d_mask: int32 [64, 32], P(('dp', 'tp'))
- positive: int32 [512], P(('dp', 'tp'))
- w_head: bfloat16 [4096, 32768], P(None, 'tp')
- b_head: float32 [32768], P('tp')
Outputs:
- output 1: float32 [1], P('dp')
- output 2: bfloat16 [4096, 32768], P('dp', 'tp')
- output 3: float32 [32768], P(('dp', 'tp'))
- output 4: bfloat16 [512, 8, 4096], P(('dp', 'tp'))
- output 5: bfloat16 [64, 32, 4096], P(('dp', 'tp'))
All inputs are finite; a program needn't handle non-finite values.
Results may differ from a plain program's by a relative error of at most 0.0125692.
Values are sent between devices in bfloat16 or wider.
A program may use at most 768 MiB of HBM per device.

v0:
```python
import math
import jax
import jax.numpy as jnp
from jax import lax
from jax.sharding import PartitionSpec as P


def solution(mesh):
    n_group = mesh.shape['tp']
    highest = lax.Precision.HIGHEST
    row_spec = P(('dp', 'tp'))
    mask_spec = P(('dp', 'tp'), None)
    hid_spec = P(('dp', 'tp'), None, None)
    contract_first = (((0,), (0,)), ((), ()))
    contract_last = (((1,), (1,)), ((), ()))

    def head_logits(gathered, w_head, b_head):
        return jnp.einsum('pld,dv->plv', gathered, w_head, preferred_element_type=jnp.float32) + b_head

    def side_reps(hidden, mask_all, w_head, b_head):
        def one_row(row_in):
            hid_row, mask_rows = row_in
            gathered = lax.all_gather(hid_row, 'tp')
            logits = head_logits(gathered, w_head, b_head)
            active = jnp.log1p(jnp.maximum(logits, 0.0)) * mask_rows[:, :, None].astype(jnp.float32)
            return jnp.sum(active, axis=1)
        row_reps = lax.map(one_row, (hidden, jnp.swapaxes(mask_all, 0, 1)))
        return jnp.swapaxes(row_reps, 0, 1).reshape((-1, row_reps.shape[-1]))

    def side_grads(hidden, mask_all, grad_rep, w_head, b_head, acc_init):
        grad_rows = jnp.swapaxes(grad_rep.reshape((n_group, hidden.shape[0], -1)), 0, 1)

        def one_row(acc_pair, row_in):
            acc_w, acc_b = acc_pair
            hid_row, mask_rows, grad_row = row_in
            gathered = lax.all_gather(hid_row, 'tp')
            logits = head_logits(gathered, w_head, b_head)
            relu_slope = jnp.where(logits > 0.0, 1.0 / (1.0 + jnp.maximum(logits, 0.0)), 0.0)
            grad_logits = grad_row[:, None, :] * relu_slope * mask_rows[:, :, None].astype(jnp.float32)
            grad_low = grad_logits.astype(jnp.bfloat16)
            acc_w = acc_w + jnp.einsum('pld,plv->dv', gathered, grad_low, preferred_element_type=jnp.float32)
            acc_b = acc_b + jnp.sum(grad_logits, axis=(0, 1))
            part_hid = jnp.einsum('plv,dv->pld', grad_low, w_head, preferred_element_type=jnp.float32).astype(jnp.bfloat16)
            own_hid = lax.psum_scatter(part_hid, 'tp', scatter_dimension=0, tiled=True)
            return (acc_w, acc_b), own_hid[0]
        return lax.scan(one_row, acc_init, (hidden, jnp.swapaxes(mask_all, 0, 1), grad_rows))

    def local_step(q_hidden, d_hidden, q_mask, d_mask, positive, w_head, b_head):
        hidden_size, vocab_loc = w_head.shape
        vocab_size = vocab_loc * n_group
        q_len = q_hidden.shape[1]
        d_len = d_hidden.shape[1]
        q_batch = q_hidden.shape[0] * n_group
        d_batch = d_hidden.shape[0] * n_group
        value_a11 = q_len * math.sqrt(vocab_size * d_len) / 16.0
        lam_q = 4.0 / (vocab_size * q_len * q_len)
        lam_d = 4.0 / (vocab_size * d_len * d_len)
        q_masks = lax.all_gather(q_mask, 'tp')
        d_masks = lax.all_gather(d_mask, 'tp')
        q_rep = side_reps(q_hidden, q_masks, w_head, b_head)
        d_rep = side_reps(d_hidden, d_masks, w_head, b_head)
        q_mean = jnp.mean(q_rep, axis=0)
        d_mean = jnp.mean(d_rep, axis=0)
        score_part = lax.dot_general(q_rep, d_rep, contract_last, precision=highest, preferred_element_type=jnp.float32)
        reg_part = jnp.stack([jnp.sum(q_mean * q_mean), jnp.sum(d_mean * d_mean)])
        score_sum, reg_sum = lax.psum((score_part, reg_part), 'tp')
        scores = score_sum / value_a11
        pos_all = lax.all_gather(positive, 'tp', tiled=True)
        target = (pos_all[:, None] == jnp.arange(d_batch)[None, :]).astype(jnp.float32)
        log_norm = jax.nn.logsumexp(scores, axis=1)
        loss_val = (jnp.mean(log_norm - jnp.sum(scores * target, axis=1))
                    + lam_q * reg_sum[0] + lam_d * reg_sum[1])
        grad_scores = (jnp.exp(scores - log_norm[:, None]) - target) / (q_batch * value_a11)
        grad_q = (jnp.dot(grad_scores, d_rep, precision=highest, preferred_element_type=jnp.float32)
                  + (2.0 * lam_q / q_batch) * q_mean)
        grad_d = (lax.dot_general(grad_scores, q_rep, contract_first, precision=highest, preferred_element_type=jnp.float32)
                  + (2.0 * lam_d / d_batch) * d_mean)
        acc_init = (jnp.zeros((hidden_size, vocab_loc), jnp.float32), jnp.zeros((vocab_loc,), jnp.float32))
        acc_mid, grad_qh = side_grads(q_hidden, q_masks, grad_q, w_head, b_head, acc_init)
        (acc_w, acc_b), grad_dh = side_grads(d_hidden, d_masks, grad_d, w_head, b_head, acc_mid)
        return jnp.reshape(loss_val, (1,)), acc_w.astype(jnp.bfloat16), acc_b, grad_qh, grad_dh

    return jax.shard_map(local_step, mesh=mesh,
                         in_specs=(hid_spec, hid_spec, mask_spec, mask_spec, row_spec, P(None, 'tp'), P('tp')),
                         out_specs=(P('dp'), P('dp', 'tp'), row_spec, hid_spec, hid_spec),
                         check_vma=False)
```

profile of v0, /device:TPU:97, one launch (start us, length us, event | category | flops | bytes accessed | tf_op | source)
XLA Modules:
  0.0 3478.2 jit_solution(12799293382230350234)
XLA Ops:
  73.0 136.6 %while.50 = (s32[]{:T(128)}, f32[2,32,1024]{2,1,0:T(8,128)S(1)}, bf16[2,32,4096]{2,1,0:T(8,128)(2,1)}, bf16[4096,1024]{1,0:T(8,128)(2,1)}, f32[1024]{0:T(1024)}, /*index=5*/s32[2,32,32]{2,1,0:T(8,128)S(1)}, s32[]{:T(128)}) while((s32[]{:T(128)}, f32[2,32,1024]{2,1,0:T(8,128)S(1)}, bf16[2,32,4096]{2,1,0:T(8,128)(2,1)}, ...), condition=%wide.region_5.6_spmd, body=%wide.region_3.5_spmd.sunk | while | flops 8594097152 | bytes 43663496 | solution.py:27
  74.9 53.7 %all-gather.11.cloned.1.call-done = bf16[32,32,4096]{2,1,0:T(8,128)(2,1)} async-done(((bf16[1,32,4096]{2,1,0:T(8,128)(2,1)}), bf16[32,32,4096]{2,1,0:T(8,128)(2,1)}) %all-gather.11.cloned.1.call-update) | async-done | bytes 8388624 | tf_op jit(solution)/shard_map/while/body/eval_jaxpr/all_gather | solution.py:23
  145.7 48.5 %all-gather.11.cloned.1.call-done = bf16[32,32,4096]{2,1,0:T(8,128)(2,1)} async-done(((bf16[1,32,4096]{2,1,0:T(8,128)(2,1)}), bf16[32,32,4096]{2,1,0:T(8,128)(2,1)}) %all-gather.11.cloned.1.call-update) | async-done | bytes 8388624 | tf_op jit(solution)/shard_map/while/body/eval_jaxpr/all_gather | solution.py:23
  210.3 774.4 %while.49 = (s32[]{:T(128)}, f32[16,32,1024]{2,1,0:T(8,128)}, bf16[16,8,4096]{2,1,0:T(8,128)(2,1)}, bf16[4096,1024]{1,0:T(8,128)(2,1)}, f32[1024]{0:T(1024)}, /*index=5*/s32[16,32,8]{2,1,0:T(8,128)S(1)}, s32[]{:T(128)}) while((s32[]{:T(128)}, f32[16,32,1024]{2,1,0:T(8,128)}, bf16[16,8,4096]{2,1,0:T(8,128)(2,1)}, bf16[4096,1024]{1,0:T(8,128)(2,1)}, ...), condition=%wide.region_2.3_spmd, body=%wide.region_0.2_spmd.sunk | while | flops 2148499712 | bytes 17505416 | solution.py:27
  1006.4 45.0 %psum.15 = f32[2]{0:T(128)S(1)} all-reduce(f32[2]{0:T(128)S(1)} %pad_maximum_fusion), channel_id=1, replica_groups=mesh['dp'=1,'tp'=32] {'tp'}, use_global_device_ids=true, to_apply=%region_15.16 | all-reduce | flops 2 | bytes 16 | tf_op jit(solution)/shard_map/psum | solution.py:66
  1053.5 43.9 %all-reduce = s32[512]{0:T(512)S(1)} all-reduce(s32[512]{0:T(512)S(1)} %dynamic-update-slice), channel_id=1, replica_groups=mesh['dp'=1,'tp'=32] {'tp'}, use_global_device_ids=true, to_apply=%add | all-reduce | flops 512 | bytes 4096
  1108.5 2016.3 %while.52 = (s32[]{:T(128)}, f32[4096,1024]{1,0:T(8,128)}, f32[1024]{0:T(1024)S(1)}, bf16[16,8,4096]{2,1,0:T(8,128)(2,1)}, bf16[16,8,4096]{2,1,0:T(8,128)(2,1)},...) while((s32[]{:T(128)}, f32[4096,1024]{1,0:T(8,128)}, ...), condition=%wide.region_19.20_spmd.clone, body=%wide.region_16.19_spmd.clone.sunk | while | flops 6461056000 | bytes 74867936 | solution.py:46
  1171.2 59.4 %reduce-scatter.5.cloned.1.call-done = bf16[1,8,4096]{2,1,0:T(8,128)(2,1)} async-done(((bf16[32,8,4096]{2,1,0:T(8,128)(2,1)}), bf16[1,8,4096]{2,1,0:T(8,128)(2,1)}) %reduce-scatter.5.cloned.1.call-update) | async-done | bytes 65552 | tf_op jit(solution)/shard_map/while/body/eval_jaxpr/reduce_scatter | solution.py:44
  1234.6 40.1 %all-gather.15.cloned.1.call-done = bf16[32,8,4096]{2,1,0:T(8,128)(2,1)} async-done(((bf16[1,8,4096]{2,1,0:T(8,128)(2,1)}), bf16[32,8,4096]{2,1,0:T(8,128)(2,1)}) %all-gather.15.cloned.1.call-update) | async-done | bytes 2097168 | tf_op jit(solution)/shard_map/while/body/eval_jaxpr/all_gather | solution.py:36
  1299.9 57.1 %reduce-scatter.5.cloned.1.call-done = bf16[1,8,4096]{2,1,0:T(8,128)(2,1)} async-done(((bf16[32,8,4096]{2,1,0:T(8,128)(2,1)}), bf16[1,8,4096]{2,1,0:T(8,128)(2,1)}) %reduce-scatter.5.cloned.1.call-update) | async-done | bytes 65552 | tf_op jit(solution)/shard_map/while/body/eval_jaxpr/reduce_scatter | solution.py:44
  1426.2 57.1 %reduce-scatter.5.cloned.1.call-done = bf16[1,8,4096]{2,1,0:T(8,128)(2,1)} async-done(((bf16[32,8,4096]{2,1,0:T(8,128)(2,1)}), bf16[1,8,4096]{2,1,0:T(8,128)(2,1)}) %reduce-scatter.5.cloned.1.call-update) | async-done | bytes 65552 | tf_op jit(solution)/shard_map/while/body/eval_jaxpr/reduce_scatter | solution.py:44
  1487.3 40.1 %all-gather.15.cloned.1.call-done = bf16[32,8,4096]{2,1,0:T(8,128)(2,1)} async-done(((bf16[1,8,4096]{2,1,0:T(8,128)(2,1)}), bf16[32,8,4096]{2,1,0:T(8,128)(2,1)}) %all-gather.15.cloned.1.call-update) | async-done | bytes 2097168 | tf_op jit(solution)/shard_map/while/body/eval_jaxpr/all_gather | solution.py:36
  1552.6 57.1 %reduce-scatter.5.cloned.1.call-done = bf16[1,8,4096]{2,1,0:T(8,128)(2,1)} async-done(((bf16[32,8,4096]{2,1,0:T(8,128)(2,1)}), bf16[1,8,4096]{2,1,0:T(8,128)(2,1)}) %reduce-scatter.5.cloned.1.call-update) | async-done | bytes 65552 | tf_op jit(solution)/shard_map/while/body/eval_jaxpr/reduce_scatter | solution.py:44
  1678.6 57.1 %reduce-scatter.5.cloned.1.call-done = bf16[1,8,4096]{2,1,0:T(8,128)(2,1)} async-done(((bf16[32,8,4096]{2,1,0:T(8,128)(2,1)}), bf16[1,8,4096]{2,1,0:T(8,128)(2,1)}) %reduce-scatter.5.cloned.1.call-update) | async-done | bytes 65552 | tf_op jit(solution)/shard_map/while/body/eval_jaxpr/reduce_scatter | solution.py:44
  1739.7 40.1 %all-gather.15.cloned.1.call-done = bf16[32,8,4096]{2,1,0:T(8,128)(2,1)} async-done(((bf16[1,8,4096]{2,1,0:T(8,128)(2,1)}), bf16[32,8,4096]{2,1,0:T(8,128)(2,1)}) %all-gather.15.cloned.1.call-update) | async-done | bytes 2097168 | tf_op jit(solution)/shard_map/while/body/eval_jaxpr/all_gather | solution.py:36
  1805.0 57.1 %reduce-scatter.5.cloned.1.call-done = bf16[1,8,4096]{2,1,0:T(8,128)(2,1)} async-done(((bf16[32,8,4096]{2,1,0:T(8,128)(2,1)}), bf16[1,8,4096]{2,1,0:T(8,128)(2,1)}) %reduce-scatter.5.cloned.1.call-update) | async-done | bytes 65552 | tf_op jit(solution)/shard_map/while/body/eval_jaxpr/reduce_scatter | solution.py:44
  1931.3 57.1 %reduce-scatter.5.cloned.1.call-done = bf16[1,8,4096]{2,1,0:T(8,128)(2,1)} async-done(((bf16[32,8,4096]{2,1,0:T(8,128)(2,1)}), bf16[1,8,4096]{2,1,0:T(8,128)(2,1)}) %reduce-scatter.5.cloned.1.call-update) | async-done | bytes 65552 | tf_op jit(solution)/shard_map/while/body/eval_jaxpr/reduce_scatter | solution.py:44
  2057.3 57.1 %reduce-scatter.5.cloned.1.call-done = bf16[1,8,4096]{2,1,0:T(8,128)(2,1)} async-done(((bf16[32,8,4096]{2,1,0:T(8,128)(2,1)}), bf16[1,8,4096]{2,1,0:T(8,128)(2,1)}) %reduce-scatter.5.cloned.1.call-update) | async-done | bytes 65552 | tf_op jit(solution)/shard_map/while/body/eval_jaxpr/reduce_scatter | solution.py:44
  2118.5 40.1 %all-gather.15.cloned.1.call-done = bf16[32,8,4096]{2,1,0:T(8,128)(2,1)} async-done(((bf16[1,8,4096]{2,1,0:T(8,128)(2,1)}), bf16[32,8,4096]{2,1,0:T(8,128)(2,1)}) %all-gather.15.cloned.1.call-update) | async-done | bytes 2097168 | tf_op jit(solution)/shard_map/while/body/eval_jaxpr/all_gather | solution.py:36
  2183.7 57.1 %reduce-scatter.5.cloned.1.call-done = bf16[1,8,4096]{2,1,0:T(8,128)(2,1)} async-done(((bf16[32,8,4096]{2,1,0:T(8,128)(2,1)}), bf16[1,8,4096]{2,1,0:T(8,128)(2,1)}) %reduce-scatter.5.cloned.1.call-update) | async-done | bytes 65552 | tf_op jit(solution)/shard_map/while/body/eval_jaxpr/reduce_scatter | solution.py:44
  2309.7 57.1 %reduce-scatter.5.cloned.1.call-done = bf16[1,8,4096]{2,1,0:T(8,128)(2,1)} async-done(((bf16[32,8,4096]{2,1,0:T(8,128)(2,1)}), bf16[1,8,4096]{2,1,0:T(8,128)(2,1)}) %reduce-scatter.5.cloned.1.call-update) | async-done | bytes 65552 | tf_op jit(solution)/shard_map/while/body/eval_jaxpr/reduce_scatter | solution.py:44
  2435.8 57.1 %reduce-scatter.5.cloned.1.call-done = bf16[1,8,4096]{2,1,0:T(8,128)(2,1)} async-done(((bf16[32,8,4096]{2,1,0:T(8,128)(2,1)}), bf16[1,8,4096]{2,1,0:T(8,128)(2,1)}) %reduce-scatter.5.cloned.1.call-update) | async-done | bytes 65552 | tf_op jit(solution)/shard_map/while/body/eval_jaxpr/reduce_scatter | solution.py:44
  2562.1 57.1 %reduce-scatter.5.cloned.1.call-done = bf16[1,8,4096]{2,1,0:T(8,128)(2,1)} async-done(((bf16[32,8,4096]{2,1,0:T(8,128)(2,1)}), bf16[1,8,4096]{2,1,0:T(8,128)(2,1)}) %reduce-scatter.5.cloned.1.call-update) | async-done | bytes 65552 | tf_op jit(solution)/shard_map/while/body/eval_jaxpr/reduce_scatter | solution.py:44
  2688.2 57.1 %reduce-scatter.5.cloned.1.call-done = bf16[1,8,4096]{2,1,0:T(8,128)(2,1)} async-done(((bf16[32,8,4096]{2,1,0:T(8,128)(2,1)}), bf16[1,8,4096]{2,1,0:T(8,128)(2,1)}) %reduce-scatter.5.cloned.1.call-update) | async-done | bytes 65552 | tf_op jit(solution)/shard_map/while/body/eval_jaxpr/reduce_scatter | solution.py:44
  2814.2 57.1 %reduce-scatter.5.cloned.1.call-done = bf16[1,8,4096]{2,1,0:T(8,128)(2,1)} async-done(((bf16[32,8,4096]{2,1,0:T(8,128)(2,1)}), bf16[1,8,4096]{2,1,0:T(8,128)(2,1)}) %reduce-scatter.5.cloned.1.call-update) | async-done | bytes 65552 | tf_op jit(solution)/shard_map/while/body/eval_jaxpr/reduce_scatter | solution.py:44
  2940.2 57.1 %reduce-scatter.5.cloned.1.call-done = bf16[1,8,4096]{2,1,0:T(8,128)(2,1)} async-done(((bf16[32,8,4096]{2,1,0:T(8,128)(2,1)}), bf16[1,8,4096]{2,1,0:T(8,128)(2,1)}) %reduce-scatter.5.cloned.1.call-update) | async-done | bytes 65552 | tf_op jit(solution)/shard_map/while/body/eval_jaxpr/reduce_scatter | solution.py:44
  3066.3 57.1 %reduce-scatter.5.cloned.1.call-done = bf16[1,8,4096]{2,1,0:T(8,128)(2,1)} async-done(((bf16[32,8,4096]{2,1,0:T(8,128)(2,1)}), bf16[1,8,4096]{2,1,0:T(8,128)(2,1)}) %reduce-scatter.5.cloned.1.call-update) | async-done | bytes 65552 | tf_op jit(solution)/shard_map/while/body/eval_jaxpr/reduce_scatter | solution.py:44
  3124.9 334.7 %while.51 = (s32[]{:T(128)}, f32[4096,1024]{1,0:T(8,128)}, f32[1024]{0:T(1024)S(1)}, bf16[2,32,4096]{2,1,0:T(8,128)(2,1)}, bf16[2,32,4096]{2,1,0:T(8,128)(2,1)S(...) while((s32[]{:T(128)}, f32[4096,1024]{1,0:T(8,128)}, ...), condition=%wide.region_23.24_spmd, body=%wide.region_20.23_spmd.sunk | while | flops 25818005504 | bytes 180015376 | solution.py:46
  3126.0 51.0 %all-gather.13.cloned.1.call-done = bf16[32,32,4096]{2,1,0:T(8,128)(2,1)} async-done(((bf16[1,32,4096]{2,1,0:T(8,128)(2,1)}), bf16[32,32,4096]{2,1,0:T(8,128)(2,1)}) %all-gather.13.cloned.1.call-update) | async-done | bytes 8388624 | tf_op jit(solution)/shard_map/while/body/eval_jaxpr/all_gather | solution.py:36
  3230.4 60.2 %reduce-scatter.3.cloned.1.call-done = bf16[1,32,4096]{2,1,0:T(8,128)(2,1)} async-done(((bf16[32,32,4096]{2,1,0:T(8,128)(2,1)}), bf16[1,32,4096]{2,1,0:T(8,128)(2,1)}) %reduce-scatter.3.cloned.1.call-update) | async-done | bytes 262160 | tf_op jit(solution)/shard_map/while/body/eval_jaxpr/reduce_scatter | solution.py:44
  3293.2 51.1 %all-gather.13.cloned.1.call-done = bf16[32,32,4096]{2,1,0:T(8,128)(2,1)} async-done(((bf16[1,32,4096]{2,1,0:T(8,128)(2,1)}), bf16[32,32,4096]{2,1,0:T(8,128)(2,1)}) %all-gather.13.cloned.1.call-update) | async-done | bytes 8388624 | tf_op jit(solution)/shard_map/while/body/eval_jaxpr/all_gather | solution.py:36
  3397.7 60.2 %reduce-scatter.3.cloned.1.call-done = bf16[1,32,4096]{2,1,0:T(8,128)(2,1)} async-done(((bf16[32,32,4096]{2,1,0:T(8,128)(2,1)}), bf16[1,32,4096]{2,1,0:T(8,128)(2,1)}) %reduce-scatter.3.cloned.1.call-update) | async-done | bytes 262160 | tf_op jit(solution)/shard_map/while/body/eval_jaxpr/reduce_scatter | solution.py:44
  (427 shorter events, 1967.3 us)
Async XLA Ops:
  73.0 55.5 %all-gather.11.cloned.1.call-start = ((), (), s32[]{:S(2)}) async-start(), calls=%async_computation.4 | async-start | bytes 8650752 | tf_op jit(solution)/shard_map/while/body/eval_jaxpr/all_gather | solution.py:23
  143.9 50.4 %all-gather.11.cloned.1.call-start = ((), (), s32[]{:S(2)}) async-start(), calls=%async_computation.4 | async-start | bytes 8650752 | tf_op jit(solution)/shard_map/while/body/eval_jaxpr/all_gather | solution.py:23
  984.6 112.8 %all-reduce.3.cloned.1.call-start = ((), (), s32[]{:S(2)}) async-start(), calls=%async_computation.2 | async-start | bytes 262144 | tf_op jit(solution)/shard_map/psum | solution.py:66
  1110.2 120.4 %reduce-scatter.5.cloned.1.call-start = ((), (), s32[]{:S(2)}) async-start(), calls=%async_computation.8 | async-start | bytes 2162688 | tf_op jit(solution)/shard_map/while/body/eval_jaxpr/reduce_scatter | solution.py:44
  1232.1 42.7 %all-gather.15.cloned.1.call-start = ((), (), s32[]{:S(2)}) async-start(), calls=%async_computation.7 | async-start | bytes 2162688 | tf_op jit(solution)/shard_map/while/body/eval_jaxpr/all_gather | solution.py:36
  1233.6 123.4 %reduce-scatter.5.cloned.1.call-start = ((), (), s32[]{:S(2)}) async-start(), calls=%async_computation.8 | async-start | bytes 2162688 | tf_op jit(solution)/shard_map/while/body/eval_jaxpr/reduce_scatter | solution.py:44
  1358.5 42.6 %all-gather.15.cloned.1.call-start = ((), (), s32[]{:S(2)}) async-start(), calls=%async_computation.7 | async-start | bytes 2162688 | tf_op jit(solution)/shard_map/while/body/eval_jaxpr/all_gather | solution.py:36
  1360.0 123.3 %reduce-scatter.5.cloned.1.call-start = ((), (), s32[]{:S(2)}) async-start(), calls=%async_computation.8 | async-start | bytes 2162688 | tf_op jit(solution)/shard_map/while/body/eval_jaxpr/reduce_scatter | solution.py:44
  1484.8 42.6 %all-gather.15.cloned.1.call-start = ((), (), s32[]{:S(2)}) async-start(), calls=%async_computation.7 | async-start | bytes 2162688 | tf_op jit(solution)/shard_map/while/body/eval_jaxpr/all_gather | solution.py:36
  1486.3 123.4 %reduce-scatter.5.cloned.1.call-start = ((), (), s32[]{:S(2)}) async-start(), calls=%async_computation.8 | async-start | bytes 2162688 | tf_op jit(solution)/shard_map/while/body/eval_jaxpr/reduce_scatter | solution.py:44
  1612.7 123.0 %reduce-scatter.5.cloned.1.call-start = ((), (), s32[]{:S(2)}) async-start(), calls=%async_computation.8 | async-start | bytes 2162688 | tf_op jit(solution)/shard_map/while/body/eval_jaxpr/reduce_scatter | solution.py:44
  1737.2 42.6 %all-gather.15.cloned.1.call-start = ((), (), s32[]{:S(2)}) async-start(), calls=%async_computation.7 | async-start | bytes 2162688 | tf_op jit(solution)/shard_map/while/body/eval_jaxpr/all_gather | solution.py:36
  1738.7 123.4 %reduce-scatter.5.cloned.1.call-start = ((), (), s32[]{:S(2)}) async-start(), calls=%async_computation.8 | async-start | bytes 2162688 | tf_op jit(solution)/shard_map/while/body/eval_jaxpr/reduce_scatter | solution.py:44
  1863.6 42.6 %all-gather.15.cloned.1.call-start = ((), (), s32[]{:S(2)}) async-start(), calls=%async_computation.7 | async-start | bytes 2162688 | tf_op jit(solution)/shard_map/while/body/eval_jaxpr/all_gather | solution.py:36
  1865.1 123.3 %reduce-scatter.5.cloned.1.call-start = ((), (), s32[]{:S(2)}) async-start(), calls=%async_computation.8 | async-start | bytes 2162688 | tf_op jit(solution)/shard_map/while/body/eval_jaxpr/reduce_scatter | solution.py:44
  1991.4 123.0 %reduce-scatter.5.cloned.1.call-start = ((), (), s32[]{:S(2)}) async-start(), calls=%async_computation.8 | async-start | bytes 2162688 | tf_op jit(solution)/shard_map/while/body/eval_jaxpr/reduce_scatter | solution.py:44
  2115.9 42.6 %all-gather.15.cloned.1.call-start = ((), (), s32[]{:S(2)}) async-start(), calls=%async_computation.7 | async-start | bytes 2162688 | tf_op jit(solution)/shard_map/while/body/eval_jaxpr/all_gather | solution.py:36
  2117.4 123.4 %reduce-scatter.5.cloned.1.call-start = ((), (), s32[]{:S(2)}) async-start(), calls=%async_computation.8 | async-start | bytes 2162688 | tf_op jit(solution)/shard_map/while/body/eval_jaxpr/reduce_scatter | solution.py:44
  2243.8 123.0 %reduce-scatter.5.cloned.1.call-start = ((), (), s32[]{:S(2)}) async-start(), calls=%async_computation.8 | async-start | bytes 2162688 | tf_op jit(solution)/shard_map/while/body/eval_jaxpr/reduce_scatter | solution.py:44
  2368.3 42.3 %all-gather.15.cloned.1.call-start = ((), (), s32[]{:S(2)}) async-start(), calls=%async_computation.7 | async-start | bytes 2162688 | tf_op jit(solution)/shard_map/while/body/eval_jaxpr/all_gather | solution.py:36
  2369.8 123.0 %reduce-scatter.5.cloned.1.call-start = ((), (), s32[]{:S(2)}) async-start(), calls=%async_computation.8 | async-start | bytes 2162688 | tf_op jit(solution)/shard_map/while/body/eval_jaxpr/reduce_scatter | solution.py:44
  2494.3 42.6 %all-gather.15.cloned.1.call-start = ((), (), s32[]{:S(2)}) async-start(), calls=%async_computation.7 | async-start | bytes 2162688 | tf_op jit(solution)/shard_map/while/body/eval_jaxpr/all_gather | solution.py:36
  2495.9 123.4 %reduce-scatter.5.cloned.1.call-start = ((), (), s32[]{:S(2)}) async-start(), calls=%async_computation.8 | async-start | bytes 2162688 | tf_op jit(solution)/shard_map/while/body/eval_jaxpr/reduce_scatter | solution.py:44
  2622.3 123.0 %reduce-scatter.5.cloned.1.call-start = ((), (), s32[]{:S(2)}) async-start(), calls=%async_computation.8 | async-start | bytes 2162688 | tf_op jit(solution)/shard_map/while/body/eval_jaxpr/reduce_scatter | solution.py:44
  2748.3 123.0 %reduce-scatter.5.cloned.1.call-start = ((), (), s32[]{:S(2)}) async-start(), calls=%async_computation.8 | async-start | bytes 2162688 | tf_op jit(solution)/shard_map/while/body/eval_jaxpr/reduce_scatter | solution.py:44
  2872.8 42.3 %all-gather.15.cloned.1.call-start = ((), (), s32[]{:S(2)}) async-start(), calls=%async_computation.7 | async-start | bytes 2162688 | tf_op jit(solution)/shard_map/while/body/eval_jaxpr/all_gather | solution.py:36
  2874.3 123.1 %reduce-scatter.5.cloned.1.call-start = ((), (), s32[]{:S(2)}) async-start(), calls=%async_computation.8 | async-start | bytes 2162688 | tf_op jit(solution)/shard_map/while/body/eval_jaxpr/reduce_scatter | solution.py:44
  3000.4 123.0 %reduce-scatter.5.cloned.1.call-start = ((), (), s32[]{:S(2)}) async-start(), calls=%async_computation.8 | async-start | bytes 2162688 | tf_op jit(solution)/shard_map/while/body/eval_jaxpr/reduce_scatter | solution.py:44
  3125.0 52.0 %all-gather.13.cloned.1.call-start = ((), (), s32[]{:S(2)}) async-start(), calls=%async_computation.5 | async-start | bytes 8650752 | tf_op jit(solution)/shard_map/while/body/eval_jaxpr/all_gather | solution.py:36
  3125.9 164.7 %reduce-scatter.3.cloned.1.call-start = ((), (), s32[]{:S(2)}) async-start(), calls=%async_computation.6 | async-start | bytes 8650752 | tf_op jit(solution)/shard_map/while/body/eval_jaxpr/reduce_scatter | solution.py:44
  3292.3 52.0 %all-gather.13.cloned.1.call-start = ((), (), s32[]{:S(2)}) async-start(), calls=%async_computation.5 | async-start | bytes 8650752 | tf_op jit(solution)/shard_map/while/body/eval_jaxpr/all_gather | solution.py:36
  3293.1 164.8 %reduce-scatter.3.cloned.1.call-start = ((), (), s32[]{:S(2)}) async-start(), calls=%async_computation.6 | async-start | bytes 8650752 | tf_op jit(solution)/shard_map/while/body/eval_jaxpr/reduce_scatter | solution.py:44
  (34 other events, 7079.6 us)
Sparse Core Ops, SparseCore 0:
  76.5 51.9 all-gather.10
  147.4 46.8 all-gather.10
  1162.1 68.4 reduce-scatter.4
  1234.9 39.7 all-gather.14
  1288.5 68.4 reduce-scatter.4
  1361.4 39.6 all-gather.14
  1414.8 68.4 reduce-scatter.4
  1487.7 39.7 all-gather.14
  1541.2 68.4 reduce-scatter.4
  1667.2 68.4 reduce-scatter.4
  1740.1 39.7 all-gather.14
  1793.5 68.4 reduce-scatter.4
  1919.9 68.4 reduce-scatter.4
  1992.5 39.6 all-gather.14
  2045.9 68.4 reduce-scatter.4
  2118.8 39.7 all-gather.14
  2172.3 68.4 reduce-scatter.4
  2244.8 39.7 all-gather.14
  2298.3 68.4 reduce-scatter.4
  2370.9 39.7 all-gather.14
  2424.4 68.4 reduce-scatter.4
  2497.2 39.7 all-gather.14
  2550.7 68.4 reduce-scatter.4
  2676.7 68.4 reduce-scatter.4
  2802.8 68.4 reduce-scatter.4
  2875.3 39.7 all-gather.14
  2928.8 68.4 reduce-scatter.4
  3054.9 68.4 reduce-scatter.4
  3128.2 48.7 all-gather.12
  3208.2 82.3 reduce-scatter.2
  3295.5 48.7 all-gather.12
  3375.5 82.3 reduce-scatter.2
  (22 shorter events, 834.4 us)
Sparse Core Ops, SparseCore 1:
  1002.1 90.8 all-reduce.2
where the time goes:
time: 3490 us; the launch traced here: 3480 us
  waiting for transfers between devices  2510 us (72%)
  matrix products  638 us (18%)
  blocking collectives  154 us (4%)
  local copies, waits for them, and re-layouts  116 us (3%)
    all_gather x36, waiting for transfers between devices, one_row(): gathered = lax.all_gather(hid_row, 'tp')  1470 us
    reduce_scatter x18, waiting for transfers between devices, one_row(): own_hid = lax.psum_scatter(part_hid, 'tp', scatter_dimension=0, tiled=True)  1040 us
    dot_general x36, matrix products, head_logits(): jnp.einsum('pld,dv->plv', gathered, w_head, preferred_element_type=jnp.fl...  271 us
    dot_general x18, matrix products, one_row(): jnp.einsum('pld,plv->dv', gathered, grad_low, preferred_element_type=jnp....  215 us
    dot_general x18, matrix products, one_row(): jnp.einsum('plv,dv->pld', grad_low, w_head, preferred_element_type=jnp.fl...  145 us
  transfers between devices with their start and end apart: 55, of which 54 were waited for; matrix products, arithmetic and copies ran while one was open for 7% of the time, Pallas kernels for 0%

commit v1 on v0

v1 whole, which is shorter than its diff:
```python
import functools
import math

import jax
import jax.numpy as jnp
from jax import lax
from jax.experimental import pallas as pl
from jax.experimental.pallas import tpu as pltpu
from jax.sharding import PartitionSpec as P

MESH = pl.DeviceIdType.MESH
F32 = jnp.float32
BF16 = jnp.bfloat16
VMEM_LIMIT = 67043328
HIGHEST = lax.Precision.HIGHEST


class Geometry:
    def __init__(self, n_group, rows, hidden, vocab, unit):
        self.side = math.isqrt(n_group // 2)
        self.nd = 2 * (self.side.bit_length() - 1)
        self.chips = 1 << self.nd
        assert self.side == 4 and self.chips * 2 == n_group
        self.rows = rows
        self.steps = rows + self.nd
        self.unit = unit
        self.slab = 2 * unit
        self.tokens = self.slab * self.chips
        self.half = hidden // 2
        self.width = self.half // self.nd
        self.vocab = vocab

    def hops(self, rel):
        return bin(rel).count("1")

    def slot(self, rel, lane):
        return ((rel >> lane) | (rel << (self.nd - lane))) & (self.chips - 1)

    def peer(self, me, dim, core):
        chip = lax.div(me, 2)
        x, y = lax.rem(chip, self.side), lax.div(chip, self.side)
        if dim == 0:
            x = x + 1 - 2 * lax.rem(x, 2)
        elif dim == 1:
            x = self.side - 1 - x
        elif dim == 2:
            y = y + 1 - 2 * lax.rem(y, 2)
        else:
            y = self.side - 1 - y
        return {"tp": (y * self.side + x) * 2 + core}


def entry_barrier(peers):
    barrier = pltpu.get_barrier_semaphore()
    for device in peers:
        pl.semaphore_signal(barrier, inc=1, device_id=device, device_id_type=MESH)
    pl.semaphore_wait(barrier, len(peers))


class Gather:
    def __init__(self, geo, me, xo, xs, stage, ownx, sems):
        (self.ici_send, self.ici_recv, self.share_send, self.share_recv, self.piece_send, self.piece_recv,
         self.free_ici, self.free_piece, self.free_xs) = sems
        self.geo, self.xo, self.xs, self.stage, self.ownx = geo, xo, xs, stage, ownx
        self.core = lax.rem(me, 2)
        self.sib = {"tp": me + 1 - 2 * self.core}
        self.cross = [geo.peer(me, dim, 1 - self.core) for dim in range(geo.nd)]

    def ici(self, lane, pos):
        count = (1 << pos) * self.geo.slab
        return pltpu.make_async_remote_copy(
            src_ref=self.xs.at[lane, pl.ds(0, count)], dst_ref=self.xo.at[lane, pl.ds(count, count)],
            send_sem=self.ici_send.at[lane, pos], recv_sem=self.ici_recv.at[lane, pos],
            device_id=self.cross[(lane + pos) % self.geo.nd], device_id_type=MESH)

    def share(self, lane):
        return pltpu.make_async_remote_copy(
            src_ref=self.xo.at[lane], dst_ref=self.xs.at[lane],
            send_sem=self.share_send.at[lane], recv_sem=self.share_recv.at[lane],
            device_id=self.sib, device_id_type=MESH)

    def piece(self, lane, row):
        width = self.geo.width
        return pltpu.make_async_remote_copy(
            src_ref=self.ownx.at[1, row, :, pl.ds(lane * width, width)], dst_ref=self.stage.at[lane],
            send_sem=self.piece_send.at[lane], recv_sem=self.piece_recv.at[lane],
            device_id=self.sib, device_id_type=MESH)

    def arrive(self, s, lane):
        geo = self.geo
        width = geo.width

        @pl.when(s < geo.rows)
        def _():
            self.piece(lane, s).wait()
            mine = self.ownx[0, s, :, lane * width:(lane + 1) * width].astype(F32)
            theirs = self.stage[lane].astype(F32)
            first = jnp.where(self.core == 0, mine, theirs)
            second = jnp.where(self.core == 0, theirs, mine)
            self.xo[lane, 0:geo.slab, :] = jnp.concatenate([first, second], axis=0).astype(BF16)

        @pl.when(s > 0)
        def _():
            for pos in range(geo.nd):
                self.ici(lane, pos).wait_recv()
            pl.semaphore_wait(self.free_xs.at[lane], 1)

        self.share(lane).start()

    def release_own(self, s, lane):
        geo = self.geo
        self.share(lane).wait_send()

        @pl.when(s < geo.steps - 1)
        def _():
            for pos in range(geo.nd):
                pl.semaphore_signal(self.free_ici.at[lane, pos], inc=1,
                                    device_id=self.cross[(lane + pos) % geo.nd], device_id_type=MESH)

        @pl.when(s < geo.rows - 1)
        def _():
            pl.semaphore_signal(self.free_piece.at[lane], inc=1, device_id=self.sib, device_id_type=MESH)

    def forward(self, s, lane):
        geo = self.geo

        @pl.when(s < geo.rows - 1)
        def _():
            pl.semaphore_wait(self.free_piece.at[lane], 1)
            self.piece(lane, s + 1).start()

        @pl.when(s < geo.steps - 1)
        def _():
            for pos in reversed(range(geo.nd)):
                pl.semaphore_wait(self.free_ici.at[lane, pos], 1)
                self.ici(lane, pos).start()

    def release_sib(self, s, lane):
        geo = self.geo

        @pl.when(s < geo.steps - 1)
        def _():
            for pos in range(geo.nd):
                self.ici(lane, pos).wait_send()
            pl.semaphore_signal(self.free_xs.at[lane], inc=1, device_id=self.sib, device_id_type=MESH)

    def tokens_of(self, ref, lane):
        geo = self.geo
        if lane == 0:
            return ref[lane]
        places = [geo.slot(rel, lane) * geo.slab for rel in range(geo.chips)]
        return jnp.concatenate([ref[lane, at:at + geo.slab, :] for at in places], axis=0)


def gather_scratch(geo):
    nd = geo.nd
    lane = pltpu.VMEM((nd, geo.tokens, geo.width), BF16)
    bufs = [lane, lane, pltpu.VMEM((nd, geo.unit, geo.width), BF16),
            pltpu.VMEM((2, geo.rows, geo.unit, geo.half), BF16)]
    dma, reg = pltpu.SemaphoreType.DMA, pltpu.SemaphoreType.REGULAR
    sems = [dma((nd, nd)), dma((nd, nd)), dma((nd,)), dma((nd,)), dma((nd,)), dma((nd,)),
            reg((nd, nd)), reg((nd,)), reg((nd,))]
    return bufs, sems


def start_loads(geo, core, q_hbm, d_hbm, w_hbm, ownx, wv, own_sem, w_sem):
    n_q, n_d = q_hbm.shape[0], d_hbm.shape[0]
    own_loads, w_loads = [], []
    for plane in range(2):
        column = pl.multiple_of((core if plane == 0 else 1 - core) * geo.half, geo.half)
        own_loads.append(pltpu.make_async_copy(
            q_hbm.at[:, :, pl.ds(column, geo.half)], ownx.at[plane, pl.ds(0, n_q)], own_sem.at[2 * plane]))
        own_loads.append(pltpu.make_async_copy(
            d_hbm.at[:, :, pl.ds(column, geo.half)], ownx.at[plane, pl.ds(n_q, n_d)], own_sem.at[2 * plane + 1]))
        for lane in range(geo.nd):
            w_loads.append(pltpu.make_async_copy(
                w_hbm.at[pl.ds(pl.multiple_of(column + lane * geo.width, geo.width), geo.width), :],
                wv.at[plane, lane], w_sem.at[plane, lane]))
    for copy in own_loads + w_loads:
        copy.start()
    return own_loads, w_loads


def loss_kernel(geo, q_hbm, d_hbm, w_hbm, bias, mask, rep, xo, xs, stage, ownx, wv, z, own_sem, w_sem, *sems):
    me = lax.axis_index("tp")
    net = Gather(geo, me, xo, xs, stage, ownx, sems)
    own_loads, w_loads = start_loads(geo, net.core, q_hbm, d_hbm, w_hbm, ownx, wv, own_sem, w_sem)
    xo[...] = jnp.zeros_like(xo)
    entry_barrier([net.sib] + net.cross)
    for copy in own_loads:
        copy.wait()
    for lane in range(geo.nd):
        net.piece(lane, 0).start()
    for copy in w_loads:
        copy.wait()

    def own_part(s, lane):
        net.arrive(s, lane)
        part = jnp.dot(net.tokens_of(xo, lane), wv[0, lane], preferred_element_type=F32)
        par = lax.rem(s, 2)
        if lane == 0:
            z[par] = part
        else:
            z[par] = z[par] + part

    def sib_part(s, lane):
        net.release_own(s, lane)
        net.share(lane).wait_recv()
        par = lax.rem(s, 2)
        z[par] = z[par] + jnp.dot(net.tokens_of(xs, lane), wv[1, lane], preferred_element_type=F32)

    def reps(s):
        par = lax.rem(s, 2)
        for rel in range(geo.chips):
            logits = z[par, rel * geo.slab:(rel + 1) * geo.slab, :] + bias[...]
            active = jnp.log1p(jnp.maximum(logits, 0.0))
            row = s + geo.nd - geo.hops(rel)
            for core in range(2):
                at = 2 * rel + core
                part = active[core * geo.unit:(core + 1) * geo.unit, :] * mask[s, :, at:at + 1]
                rep[row, at:at + 1, :] = jnp.sum(part, axis=0, keepdims=True)

    def body(s, carry):
        for lane in range(geo.nd):
            @pl.when(s > 0)
            def _():
                net.release_sib(s - 1, lane)

            own_part(s, lane)
            if lane == 0:
                @pl.when(s > 0)
                def _():
                    reps(s - 1)
                    net.forward(s - 1, geo.nd - 1)
            else:
                net.forward(s, lane - 1)
            sib_part(s, lane)
        return carry

    lax.fori_loop(0, geo.steps, body, 0)
    reps(geo.steps - 1)


def grad_kernel(geo, q_hbm, d_hbm, w_hbm, bias, mask, drep, gw_hbm, gb, gh_hbm,
                xo, xs, stage, ownx, wv, wt, acc, z, dz, dzt, dho, sibout, sibin, dlo, dhi, m1, m2, m3,
                r1, r2, r3, r4, ost, gout, own_sem, w_sem, sd_send, sd_recv, rs_send, rs_recv, out_send, out_recv,
                wout_sem, hout_sem, *sems):
    nd, slab, unit, width, steps, rows = geo.nd, geo.slab, geo.unit, geo.width, geo.steps, geo.rows
    me = lax.axis_index("tp")
    net = Gather(geo, me, xo, xs, stage, ownx, sems)
    core = net.core
    same = [geo.peer(me, dim, core) for dim in range(nd)]
    own_loads, w_loads = start_loads(geo, core, q_hbm, d_hbm, w_hbm, ownx, wv, own_sem, w_sem)
    xo[...] = jnp.zeros_like(xo)
    entry_barrier([net.sib] + net.cross + same)
    for copy in own_loads:
        copy.wait()
    for lane in range(nd):
        net.piece(lane, 0).start()
    gb[...] = jnp.zeros_like(gb)
    for copy in w_loads:
        copy.wait()

    def prepare(k, carry):
        acc[k] = jnp.zeros(acc.shape[1:], F32)
        wt[k] = wv[lax.div(k, nd), lax.rem(k, nd)].T
        return carry

    lax.fori_loop(0, 2 * nd, prepare, 0)

    def sib_dh(lane):
        return pltpu.make_async_remote_copy(
            src_ref=sibout.at[lane], dst_ref=sibin.at[lane], send_sem=sd_send.at[lane], recv_sem=sd_recv.at[lane],
            device_id=net.sib, device_id_type=MESH)

    def rs_copy(stage_no, lane, s):
        parity, ring = lax.rem(s, 2), lax.rem(s, 3)
        n_low = geo.tokens >> stage_no
        src = dhi.at[lane]
        if stage_no > 1:
            src = (m1, m2, m3)[stage_no - 2].at[ring, lane, pl.ds(n_low, n_low)]
        dst = (r1, r2, r3, r4)[stage_no - 1].at[parity, lane]
        return pltpu.make_async_remote_copy(
            src_ref=src, dst_ref=dst, send_sem=rs_send.at[stage_no - 1, lane],
            recv_sem=rs_recv.at[stage_no - 1, lane, parity],
            device_id=same[(lane + nd - stage_no) % nd], device_id_type=MESH)

    def out_copy(s):
        parity = lax.rem(s, 2)
        return pltpu.make_async_remote_copy(
            src_ref=ost.at[parity], dst_ref=gout.at[1, s - 9], send_sem=out_send.at[parity],
            recv_sem=out_recv.at[parity], device_id=net.sib, device_id_type=MESH)

    def scatter(s):
        ring, back, prev = lax.rem(s, 3), lax.rem(s + 1, 3), lax.rem(s + 2, 3)
        was = lax.rem(s + 1, 2)
        low1, low2, low3, low4 = (geo.tokens >> k for k in range(1, 5))
        for lane in range(nd):
            cols = slice(lane * width, (lane + 1) * width)

            @pl.when((s >= 3) & (s <= steps + 1))
            def _():
                rs_copy(1, lane, s - 1).wait()
                m1[ring, lane] = (r1[was, lane].astype(F32) + dlo[ring, lane].astype(F32)).astype(BF16)

            @pl.when((s >= 5) & (s <= steps + 2))
            def _():
                rs_copy(2, lane, s - 1).wait()
                m2[ring, lane] = (r2[was, lane].astype(F32) + m1[back, lane, 0:low2].astype(F32)).astype(BF16)

            @pl.when((s >= 7) & (s <= steps + 3))
            def _():
                rs_copy(3, lane, s - 1).wait()
                m3[ring, lane] = (r3[was, lane].astype(F32) + m2[back, lane, 0:low3].astype(F32)).astype(BF16)

            @pl.when((s >= 9) & (s <= steps + 4))
            def _():
                rs_copy(4, lane, s - 1).wait()
                done = r4[was, lane].astype(F32) + m3[back, lane, 0:low4].astype(F32)
                first, second = done[0:unit], done[unit:slab]
                gout[0, s - 9, :, cols] = jnp.where(core == 0, first, second).astype(BF16)
                ost[lax.rem(s, 2), :, cols] = jnp.where(core == 0, second, first).astype(BF16)

            @pl.when((s >= 1) & (s <= steps))
            def _():
                sib_dh(lane).wait()
                both = dho[lane] + sibin[lane].astype(F32)
                dlo[prev, lane] = both[0:low1].astype(BF16)
                dhi[lane] = both[low1:].astype(BF16)

            @pl.when((s >= 2) & (s <= steps))
            def _():
                rs_copy(1, lane, s).start()

            @pl.when((s >= 4) & (s <= steps + 1))
            def _():
                rs_copy(2, lane, s).start()

            @pl.when((s >= 6) & (s <= steps + 2))
            def _():
                rs_copy(3, lane, s).start()

            @pl.when((s >= 8) & (s <= steps + 3))
            def _():
                rs_copy(4, lane, s).start()

        @pl.when((s >= 10) & (s <= steps + 4))
        def _():
            out_copy(s - 1).wait()

        @pl.when((s >= 9) & (s <= steps + 4))
        def _():
            out_copy(s).start()

    def logits_grad(s):
        total = gb[...]
        for rel in range(geo.chips):
            logits = z[rel * slab:(rel + 1) * slab, :] + bias[...]
            slope = jnp.where(logits > 0.0, 1.0 / (1.0 + jnp.maximum(logits, 0.0)), 0.0)
            row = s + nd - geo.hops(rel)
            parts = []
            for cr in range(2):
                at = 2 * rel + cr
                grad_row = drep[row, at:at + 1, :]
                part = grad_row * slope[cr * unit:(cr + 1) * unit, :] * mask[s, :, at:at + 1]
                total = total + part
                parts.append(part)
            dz[rel * slab:(rel + 1) * slab, :] = jnp.concatenate(parts, axis=0).astype(BF16)
        gb[...] = total
        dzt[...] = dz[...].T

    def compute(s):
        def sib_part(lane):
            net.share(lane).wait_recv()
            z[...] += jnp.dot(net.tokens_of(xs, lane), wv[1, lane], preferred_element_type=F32)

        for lane in range(nd):
            @pl.when(s > 0)
            def _():
                net.release_sib(s - 1, lane)

            net.arrive(s, lane)
            part = jnp.dot(net.tokens_of(xo, lane), wv[0, lane], preferred_element_type=F32)
            if lane == 0:
                z[...] = part
            else:
                z[...] += part
                sib_part(lane - 1)
        sib_part(nd - 1)
        logits_grad(s)
        for lane in range(nd):
            acc[lane] += jnp.dot(dzt[...], net.tokens_of(xo, lane), preferred_element_type=F32)
            net.release_own(s, lane)
        for lane in range(nd):
            acc[nd + lane] += jnp.dot(dzt[...], net.tokens_of(xs, lane), preferred_element_type=F32)
            if lane >= 1:
                net.forward(s, lane - 1)
        for lane in range(nd):
            part = jnp.dot(dz[...], wt[nd + lane], preferred_element_type=F32)
            for rel in range(geo.chips):
                at = geo.slot(rel, lane) * slab
                sibout[lane, at:at + slab, :] = part[rel * slab:(rel + 1) * slab, :].astype(BF16)
            sib_dh(lane).start()
            if lane == 0:
                net.forward(s, nd - 1)
        for lane in range(nd):
            part = jnp.dot(dz[...], wt[lane], preferred_element_type=F32)
            for rel in range(geo.chips):
                at = geo.slot(rel, lane) * slab
                dho[lane, at:at + slab, :] = part[rel * slab:(rel + 1) * slab, :]

    def wout(plane, lane):
        column = (core if plane == 0 else 1 - core) * geo.half + lane * width
        return pltpu.make_async_copy(
            wv.at[plane, lane], gw_hbm.at[pl.ds(pl.multiple_of(column, width), width), :], wout_sem.at[plane, lane])

    def body(s, carry):
        scatter(s)

        @pl.when(s < steps)
        def _():
            compute(s)

        for plane in range(2):
            for lane in range(nd):
                k = plane * nd + lane

                @pl.when(s == steps + k // 2)
                def _():
                    wv[plane, lane] = acc[k].astype(BF16).T
                    wout(plane, lane).start()
        return carry

    lax.fori_loop(0, steps + 5, body, 0)
    out_copy(steps + 4).wait()
    stores = []
    for plane in range(2):
        column = pl.multiple_of((core if plane == 0 else 1 - core) * geo.half, geo.half)
        stores.append(pltpu.make_async_copy(gout.at[plane], gh_hbm.at[:, :, pl.ds(column, geo.half)],
                                            hout_sem.at[plane]))
    for copy in stores:
        copy.start()
    for copy in stores:
        copy.wait()
    for plane in range(2):
        for lane in range(nd):
            wout(plane, lane).wait()


def call_loss(geo, q_rows, d_rows, w_head, bias, mask):
    bufs, sems = gather_scratch(geo)
    dma = pltpu.SemaphoreType.DMA
    hbm, vmem = pl.BlockSpec(memory_space=pl.ANY), pl.BlockSpec(memory_space=pltpu.VMEM)
    slots = 2 * geo.chips
    return pl.pallas_call(
        functools.partial(loss_kernel, geo),
        name="loss_pass",
        out_shape=jax.ShapeDtypeStruct((geo.steps + geo.nd, slots, geo.vocab), F32),
        in_specs=[hbm, hbm, hbm, vmem, vmem],
        out_specs=vmem,
        scratch_shapes=bufs + [pltpu.VMEM((2, geo.nd, geo.width, geo.vocab), BF16),
                               pltpu.VMEM((2, geo.tokens, geo.vocab), F32), dma((4,)), dma((2, geo.nd))] + sems,
        compiler_params=pltpu.CompilerParams(collective_id=0, has_side_effects=True, vmem_limit_bytes=VMEM_LIMIT),
    )(q_rows, d_rows, w_head, bias, mask)


def call_grad(geo, q_rows, d_rows, w_head, bias, mask, drep):
    bufs, sems = gather_scratch(geo)
    dma = pltpu.SemaphoreType.DMA
    nd, tok, width, vocab = geo.nd, geo.tokens, geo.width, geo.vocab
    hbm, vmem = pl.BlockSpec(memory_space=pl.ANY), pl.BlockSpec(memory_space=pltpu.VMEM)
    lane_b = functools.partial(pltpu.VMEM, dtype=BF16)
    scratch = bufs + [
        pltpu.VMEM((2, nd, width, vocab), BF16), pltpu.VMEM((2 * nd, vocab, width), BF16),
        pltpu.VMEM((2 * nd, vocab, width), F32), pltpu.VMEM((tok, vocab), F32), pltpu.VMEM((tok, vocab), BF16),
        pltpu.VMEM((vocab, tok), BF16), pltpu.VMEM((nd, tok, width), F32), pltpu.VMEM((nd, tok, width), BF16),
        pltpu.VMEM((nd, tok, width), BF16), pltpu.VMEM((3, nd, tok // 2, width), BF16),
        pltpu.VMEM((nd, tok // 2, width), BF16), pltpu.VMEM((3, nd, tok // 2, width), BF16),
        pltpu.VMEM((3, nd, tok // 4, width), BF16), pltpu.VMEM((3, nd, tok // 8, width), BF16),
        pltpu.VMEM((2, nd, tok // 2, width), BF16), pltpu.VMEM((2, nd, tok // 4, width), BF16),
        pltpu.VMEM((2, nd, tok // 8, width), BF16), pltpu.VMEM((2, nd, tok // 16, width), BF16),
        pltpu.VMEM((2, geo.unit, geo.half), BF16), pltpu.VMEM((2, geo.rows, geo.unit, geo.half), BF16),
        dma((4,)), dma((2, nd)), dma((nd,)), dma((nd,)), dma((4, nd)), dma((4, nd, 2)), dma((2,)), dma((2,)),
        dma((2, nd)), dma((2,))] + sems
    return pl.pallas_call(
        functools.partial(grad_kernel, geo),
        name="grad_pass",
        out_shape=[jax.ShapeDtypeStruct(w_head.shape, BF16), jax.ShapeDtypeStruct((geo.unit, vocab), F32),
                   jax.ShapeDtypeStruct((geo.rows, geo.unit, 2 * geo.half), BF16)],
        in_specs=[hbm, hbm, hbm, vmem, vmem, vmem],
        out_specs=[hbm, vmem, hbm],
        scratch_shapes=scratch,
        compiler_params=pltpu.CompilerParams(collective_id=1, has_side_effects=True, vmem_limit_bytes=VMEM_LIMIT),
    )(q_rows, d_rows, w_head, bias, mask, drep)


def solution(mesh):
    n_group = mesh.shape['tp']
    row_spec = P(('dp', 'tp'))
    mask_spec = P(('dp', 'tp'), None)
    hid_spec = P(('dp', 'tp'), None, None)
    contract_first = (((0,), (0,)), ((), ()))
    contract_last = (((1,), (1,)), ((), ()))

    def local_step(q_hidden, d_hidden, q_mask, d_mask, positive, w_head, b_head):
        hidden_size, vocab_loc = w_head.shape
        vocab_size = vocab_loc * n_group
        n_q, q_len, _ = q_hidden.shape
        n_d, d_len, _ = d_hidden.shape
        pieces = d_len // q_len
        q_batch, d_batch = n_q * n_group, n_d * n_group
        tau = q_len * math.sqrt(vocab_size * d_len) / 16.0
        lam_q = 4.0 / (vocab_size * q_len * q_len)
        lam_d = 4.0 / (vocab_size * d_len * d_len)
        rows = n_q + n_d * pieces
        geo = Geometry(n_group, rows, hidden_size, vocab_loc, q_len)
        nd, side, slots = geo.nd, geo.side, 2 * geo.chips

        me = lax.axis_index('tp')
        rel = jnp.arange(geo.chips)
        flip = jnp.array([0, 1, 3, 2])
        chip = me // 2
        chip_of = ((chip // side) ^ flip[rel // side]) * side + ((chip % side) ^ flip[rel % side])
        device_of = (chip_of[:, None] * 2 + jnp.arange(2)[None, :]).reshape((slots,))
        place = (device_of[:, None] == jnp.arange(n_group)[None, :]).astype(F32)
        hop_of = [geo.hops(s // 2) for s in range(slots)]

        unit_mask = jnp.concatenate([q_mask, d_mask.reshape((n_d * pieces, q_len))], axis=0)
        own_ints = jnp.concatenate([unit_mask, positive.reshape((-1, q_len))], axis=0)
        all_ints = lax.all_gather(own_ints, 'tp')
        all_mask = all_ints[:, :rows].astype(F32).reshape((n_group, rows * q_len))
        pos_all = all_ints[:, rows:].reshape((q_batch,))
        slot_mask = jnp.dot(place, all_mask, precision=HIGHEST).reshape((slots, rows, q_len))
        padded = jnp.pad(slot_mask, ((0, 0), (nd, nd), (0, 0)))
        hop_vec = jnp.array(hop_of)[:, None, None]
        skewed = jnp.zeros((slots, geo.steps, q_len), F32)
        for h in range(nd + 1):
            skewed = jnp.where(hop_vec == h, padded[:, nd - h:nd - h + geo.steps, :], skewed)
        mask = jnp.pad(jnp.transpose(skewed, (1, 2, 0)), ((0, 0), (0, 0), (0, 128 - slots)))

        bias = b_head.reshape((1, vocab_loc))
        d_units = d_hidden.reshape((n_d * pieces, q_len, hidden_size))
        rep = call_loss(geo, q_hidden, d_units, w_head, bias, mask)
        q_rep = rep[nd:nd + n_q].reshape((n_q * slots, vocab_loc))
        d_rep = jnp.sum(rep[nd + n_q:nd + rows].reshape((n_d, pieces, slots, vocab_loc)), axis=1)
        d_rep = d_rep.reshape((n_d * slots, vocab_loc))

        q_mean = jnp.mean(q_rep, axis=0)
        d_mean = jnp.mean(d_rep, axis=0)
        part = lax.dot_general(q_rep, d_rep, contract_last, precision=HIGHEST, preferred_element_type=F32)
        part = part.reshape((n_q, slots, n_d, slots))
        score_part = jnp.einsum('rjik,je,kf->erfi', part, place, place, precision=HIGHEST)
        score_part = score_part.reshape((q_batch, d_batch))
        reg_part = jnp.stack([jnp.sum(q_mean * q_mean), jnp.sum(d_mean * d_mean)])
        reg_part = jnp.pad(reg_part[None, :], ((0, 7), (0, d_batch - 2)))
        summed = lax.psum(jnp.concatenate([score_part, reg_part], axis=0), 'tp')
        scores, reg_sum = summed[:q_batch] / tau, summed[q_batch]
        target = (pos_all[:, None] == jnp.arange(d_batch)[None, :]).astype(F32)
        log_norm = jax.nn.logsumexp(scores, axis=1)
        loss_val = (jnp.mean(log_norm - jnp.sum(scores * target, axis=1))
                    + lam_q * reg_sum[0] + lam_d * reg_sum[1])
        grad_scores = (jnp.exp(scores - log_norm[:, None]) - target) / (q_batch * tau)
        grad_part = grad_scores.reshape((n_group, n_q, n_group, n_d))
        grad_part = jnp.einsum('erfi,je,kf->rjik', grad_part, place, place, precision=HIGHEST)
        grad_part = grad_part.reshape((n_q * slots, n_d * slots))
        grad_q = (jnp.dot(grad_part, d_rep, precision=HIGHEST, preferred_element_type=F32)
                  + (2.0 * lam_q / q_batch) * q_mean).reshape((n_q, slots, vocab_loc))
        grad_d = (lax.dot_general(grad_part, q_rep, contract_first, precision=HIGHEST, preferred_element_type=F32)
                  + (2.0 * lam_d / d_batch) * d_mean).reshape((n_d, 1, slots, vocab_loc))
        grad_d = jnp.broadcast_to(grad_d, (n_d, pieces, slots, vocab_loc)).reshape((n_d * pieces, slots, vocab_loc))
        blank = jnp.zeros((nd, slots, vocab_loc), F32)
        drep = jnp.concatenate([blank, grad_q, grad_d, blank], axis=0)

        grad_w, grad_b, grad_h = call_grad(geo, q_hidden, d_units, w_head, bias, mask, drep)
        return (jnp.reshape(loss_val, (1,)), grad_w, jnp.sum(grad_b, axis=0), grad_h[:n_q],
                grad_h[n_q:].reshape(d_hidden.shape))

    return jax.shard_map(local_step, mesh=mesh,
                         in_specs=(hid_spec, hid_spec, mask_spec, mask_spec, row_spec, P(None, 'tp'), P('tp')),
                         out_specs=(P('dp'), P('dp', 'tp'), row_spec, hid_spec, hid_spec),
                         check_vma=False)
```

time: 3490 us -> 865 us (0.25)
  waiting for transfers between devices: 2510 us -> 90.4 us
  Pallas kernels: 0 us -> 672 us
  matrix products: 638 us -> 8.85 us
  blocking collectives: 154 us -> 32.4 us
  local copies, waits for them, and re-layouts: 116 us -> 25.4 us
    all_gather x36 -> x0, waiting for transfers between devices: 1470 us -> none  [one_row(): gathered = lax.all_gather(hid_row, 'tp')]
    reduce_scatter x18 -> x0, waiting for transfers between devices: 1040 us -> none  [one_row(): own_hid = lax.psum_scatter(part_hid, 'tp', scatter_dimension=0, tiled=True)]
    pallas_call x0 -> x2, Pallas kernels: none -> 672 us  [the longest x1 422 us: call_grad(): pl.pallas_call(functools.partial(grad_kernel, geo), name='grad_pass', out...]
    dot_general x75 -> x8, matrix products: 638 us -> 8.85 us  [the longest x2 1.87 us: local_step(): jnp.einsum('erfi,je,kf->rjik', grad_part, place, place, precision=HIGHEST)]
    psum x1, waiting for transfers between devices: 0.01 us -> 90.4 us  [local_step(): summed = lax.psum(jnp.concatenate([score_part, reg_part], axis=0), 'tp')]
    dynamic_slice x36 -> x0, local copies, waits for them, and re-layouts: 51.9 us -> none  [side_reps(): row_reps = lax.map(one_row, (hidden, jnp.swapaxes(mask_all, 0, 1)))]
    psum x1 -> x0, blocking collectives: 45 us -> none  [local_step(): score_sum, reg_sum = lax.psum((score_part, reg_part), 'tp')]
    unnamed x1 -> x0, blocking collectives: 43.9 us -> none
  transfers between devices with their start and end apart: 55 -> 1, of which waited for: 54 -> 1; matrix products, arithmetic and copies ran while one was open for 7% -> 0% of each run, Pallas kernels for 0% -> 0%
where the time goes in v1:
time: 865 us; the launch traced here: 864 us
  Pallas kernels  672 us (78%)
  waiting for transfers between devices  90.4 us (10%)
  blocking collectives  32.4 us (4%)
  local copies, waits for them, and re-layouts  25.4 us (3%)
  other arithmetic  17.8 us (2%)
  between operations  17.3 us (2%)
  matrix products  8.85 us (1%)
    pallas_call x1, Pallas kernels, call_grad(): pl.pallas_call(functools.partial(grad_kernel, geo), name='grad_pass', out...  422 us
    pallas_call x1, Pallas kernels, call_loss(): pl.pallas_call(functools.partial(loss_kernel, geo), name='loss_pass', out...  250 us
    psum x1, waiting for transfers between devices, local_step(): summed = lax.psum(jnp.concatenate([score_part, reg_part], axis=0), 'tp')  90.4 us
    all_gather x1, blocking collectives, local_step(): all_ints = lax.all_gather(own_ints, 'tp')  32.4 us
  transfers between devices with their start and end apart: 1, of which 1 were waited for; matrix products, arithmetic and copies ran while one was open for 0% of the time, Pallas kernels for 0%

profile of v1, /device:TPU:97, one launch (start us, length us, event | category | flops | bytes accessed | tf_op | source)
XLA Modules:
  0.0 864.5 jit_solution(2292614452526451460)
XLA Ops:
  7.3 0.7 reshape.195
  8.2 1.3 gather_fusion.1
  9.5 1.3 gather_fusion
  10.8 0.8 reshape.194
  11.8 0.8 add_bitcast_fusion
  12.6 32.4 %all-gather.1 = s32[32,26,8]{1,2,0:T(8,128)S(1)} all-gather(s32[1,26,8]{1,2,0:T(8,128)S(1)} %add_bitcast_fusion), channel_id=2, replica_groups=mesh['dp'=1,'tp'=32] {'tp'}, dimensions={0}, use_global_device_ids=true | all-gather | bytes 27456 | tf_op jit(solution)/shard_map/all_gather | solution.py:530
  46.1 0.8 fusion.4
  47.5 250.0 %loss_pass.1 = f32[32,32,1024]{2,1,0:T(8,128)} custom-call(bf16[16,8,4096]{2,1,0:T(8,128)(2,1)} %q_hbm.3, bf16[8,8,4096]{2,1,0:T(8,128)(2,1)} %bitcast.78, bf16[4096,1024]{1,0:T(8,128)(2,1)} %w_hbm.3, f32[1,1024]{1,0:T(1,128)} %bitcast.83, f32[28,8,128]{2,1,0:T(8,128)} %pad.13.mask), custom_call_target="tpu_custom_call" | custom-call | tf_op jit(solution)/shard_map/loss_pass/pallas_call | solution.py:455
  297.5 1.5 slice_reduce_fusion
  298.9 1.4 bitcast_reduce_fusion
  300.3 1.8 fusion.29
  302.8 1.8 fusion
  305.1 1.2 convolution_bitcast_fusion.1
  306.9 1.4 maximum_bitcast_fusion
  308.4 1.9 copy.43
  310.3 1.3 reshape.198
  311.6 1.6 select_maximum_fusion
  313.8 90.4 %all-reduce.5.cloned.1.call-done = f32[520,64]{0,1:T(8,128)} async-done(((f32[520,64]{0,1:T(8,128)}), f32[520,64]{0,1:T(8,128)}) %all-reduce.5.cloned.1.call-update) | async-done | bytes 133136 | tf_op jit(solution)/shard_map/psum | solution.py:556
  404.1 0.9 fusion.11
  405.1 1.0 select_reduce_fusion
  406.7 0.9 subtract_multiply_fusion
  408.0 1.5 copy.46
  409.5 1.4 fusion.15
  411.9 1.4 convolution_add_fusion.1
  413.3 1.9 convolution_add_fusion
  415.3 2.5 pad_maximum_fusion.drep
  417.8 422.3 %grad_pass.1 = (bf16[4096,1024]{1,0:T(8,128)(2,1)}, f32[8,1024]{1,0:T(8,128)}, bf16[24,8,4096]{2,1,0:T(8,128)(2,1)}) custom-call(bf16[16,8,4096]{2,1,0:T(8,128)(2,1)} %q_hbm.3, bf16[8,8,4096]{2,1,0:T(8,128)(2,1)} %bitcast.79, bf16[4096,1024]{1,0:T(8,128)(2,1)} %w_hbm.3, f32[1,1024]{1,0:T(1,128)} %bitcast.84, f32[28,8,128]{2,1,0:T(8,128)} %pad.13.mask, ...), custom_call_target="tpu_custom_call" | custom-call | tf_op jit(solution)/shard_map/grad_pass/pallas_call | solution.py:485
  840.0 1.9 slice.60
  841.9 2.3 slice.59
  844.2 1.4 reduce_sum.89
  845.6 1.3 fusion.30
  848.7 7.8 copy.57
  (41 shorter events, 6.5 us)
Async XLA Ops:
  7.2 397.0 %all-reduce.5.cloned.1.call-start = ((), (), s32[]{:S(2)}) async-start(), calls=%async_computation | async-start | bytes 327680 | tf_op jit(solution)/shard_map/psum | solution.py:556
  11.8 35.7 %copy-start.3 = (s32[32]{0:T(128)}, s32[32]{0:T(128)S(1)}, u32[]{:S(2)}) copy-start(s32[32]{0:T(128)S(1)} %add.119) | copy-start | bytes 388
  45.0 0.7 copy-start.1
  297.5 5.3 copy-start
  298.9 5.7 copy-start.4
  302.2 11.1 %copy-start.2 = (s32[32,26,8]{1,2,0:T(8,128)S(1)}, s32[32,26,8]{1,2,0:T(8,128)}, u32[]{:S(2)}) copy-start(s32[32,26,8]{1,2,0:T(8,128)} %copy-done.1) | copy-start | bytes 79876
Sparse Core Ops, SparseCore 0:
  313.4 90.6 all-reduce.4

commit v2 on v1

v2 whole, which is shorter than its diff:
```python
import functools
import math

import jax
import jax.numpy as jnp
import numpy as np
from jax import lax
from jax.experimental import pallas as pl
from jax.experimental.pallas import tpu as pltpu
from jax.sharding import PartitionSpec as P

MESH = pl.DeviceIdType.MESH
F32 = jnp.float32
BF16 = jnp.bfloat16
VMEM_LIMIT = 67043328
HIGHEST = lax.Precision.HIGHEST


class Geometry:
    def __init__(self, n_group, rows, hidden, vocab, unit):
        self.side = math.isqrt(n_group // 2)
        self.nd = 2 * (self.side.bit_length() - 1)
        self.chips = 1 << self.nd
        assert self.side == 4 and self.chips * 2 == n_group
        self.rows = rows
        self.first = self.nd + rows
        self.steps = self.first + rows
        self.unit = unit
        self.slab = 2 * unit
        self.tokens = self.slab * self.chips
        self.half = hidden // 2
        self.width = self.half // self.nd
        self.vocab = vocab

    def hops(self, rel):
        return bin(rel).count("1")

    def slot(self, rel, lane):
        return ((rel >> lane) | (rel << (self.nd - lane))) & (self.chips - 1)

    def device(self, me, rel, core):
        chip = lax.div(me, 2)
        x, y = lax.rem(chip, self.side), lax.div(chip, self.side)
        if rel & 1:
            x = x + 1 - 2 * lax.rem(x, 2)
        if rel & 2:
            x = self.side - 1 - x
        if rel & 4:
            y = y + 1 - 2 * lax.rem(y, 2)
        if rel & 8:
            y = self.side - 1 - y
        return {"tp": (y * self.side + x) * 2 + core}

    def peer(self, me, dim, core):
        return self.device(me, 1 << dim, core)


def entry_barrier(peers):
    barrier = pltpu.get_barrier_semaphore()
    for device in peers:
        pl.semaphore_signal(barrier, inc=1, device_id=device, device_id_type=MESH)
    pl.semaphore_wait(barrier, len(peers))


class Gather:
    def __init__(self, geo, me, xo, xs, stage, ownx, sems):
        (self.ici_send, self.ici_recv, self.share_send, self.share_recv, self.piece_send, self.piece_recv,
         self.free_ici, self.free_piece, self.free_xs) = sems
        self.geo, self.xo, self.xs, self.stage, self.ownx = geo, xo, xs, stage, ownx
        self.core = lax.rem(me, 2)
        self.sib = {"tp": me + 1 - 2 * self.core}
        self.cross = [geo.peer(me, dim, 1 - self.core) for dim in range(geo.nd)]

    def ici(self, lane, pos):
        count = (1 << pos) * self.geo.slab
        return pltpu.make_async_remote_copy(
            src_ref=self.xs.at[lane, pl.ds(0, count)], dst_ref=self.xo.at[lane, pl.ds(count, count)],
            send_sem=self.ici_send.at[lane, pos], recv_sem=self.ici_recv.at[lane, pos],
            device_id=self.cross[(lane + pos) % self.geo.nd], device_id_type=MESH)

    def share(self, lane):
        return pltpu.make_async_remote_copy(
            src_ref=self.xo.at[lane], dst_ref=self.xs.at[lane],
            send_sem=self.share_send.at[lane], recv_sem=self.share_recv.at[lane],
            device_id=self.sib, device_id_type=MESH)

    def piece(self, lane, row):
        width = self.geo.width
        return pltpu.make_async_remote_copy(
            src_ref=self.ownx.at[1, row, :, pl.ds(lane * width, width)], dst_ref=self.stage.at[lane],
            send_sem=self.piece_send.at[lane], recv_sem=self.piece_recv.at[lane],
            device_id=self.sib, device_id_type=MESH)

    def arrive(self, s, lane):
        geo = self.geo
        width = geo.width

        row = lax.rem(s, geo.rows)
        self.piece(lane, row).wait()
        mine = self.ownx[0, row, :, lane * width:(lane + 1) * width].astype(F32)
        theirs = self.stage[lane].astype(F32)
        first = jnp.where(self.core == 0, mine, theirs)
        second = jnp.where(self.core == 0, theirs, mine)
        self.xo[lane, 0:geo.slab, :] = jnp.concatenate([first, second], axis=0).astype(BF16)

        @pl.when(s > 0)
        def _():
            for pos in range(geo.nd):
                self.ici(lane, pos).wait_recv()
            pl.semaphore_wait(self.free_xs.at[lane], 1)

        self.share(lane).start()

    def release_own(self, s, lane):
        geo = self.geo
        self.share(lane).wait_send()

        @pl.when(s < geo.steps - 1)
        def _():
            for pos in range(geo.nd):
                pl.semaphore_signal(self.free_ici.at[lane, pos], inc=1,
                                    device_id=self.cross[(lane + pos) % geo.nd], device_id_type=MESH)
            pl.semaphore_signal(self.free_piece.at[lane], inc=1, device_id=self.sib, device_id_type=MESH)

    def forward(self, s, lane):
        geo = self.geo

        @pl.when(s < geo.steps - 1)
        def _():
            pl.semaphore_wait(self.free_piece.at[lane], 1)
            self.piece(lane, lax.rem(s + 1, geo.rows)).start()
            for pos in reversed(range(geo.nd)):
                pl.semaphore_wait(self.free_ici.at[lane, pos], 1)
                self.ici(lane, pos).start()

    def release_sib(self, s, lane):
        geo = self.geo

        @pl.when(s < geo.steps - 1)
        def _():
            for pos in range(geo.nd):
                self.ici(lane, pos).wait_send()
            pl.semaphore_signal(self.free_xs.at[lane], inc=1, device_id=self.sib, device_id_type=MESH)

    def tokens_of(self, ref, lane):
        geo = self.geo
        if lane == 0:
            return ref[lane]
        places = [geo.slot(rel, lane) * geo.slab for rel in range(geo.chips)]
        return jnp.concatenate([ref[lane, at:at + geo.slab, :] for at in places], axis=0)


def gather_scratch(geo):
    nd = geo.nd
    lane = pltpu.VMEM((nd, geo.tokens, geo.width), BF16)
    bufs = [lane, lane, pltpu.VMEM((nd, geo.unit, geo.width), BF16),
            pltpu.VMEM((2, geo.rows, geo.unit, geo.half), BF16)]
    dma, reg = pltpu.SemaphoreType.DMA, pltpu.SemaphoreType.REGULAR
    sems = [dma((nd, nd)), dma((nd, nd)), dma((nd,)), dma((nd,)), dma((nd,)), dma((nd,)),
            reg((nd, nd)), reg((nd,)), reg((nd,))]
    return bufs, sems


def start_loads(geo, core, q_hbm, d_hbm, w_hbm, ownx, wv, own_sem, w_sem):
    n_q, n_d = q_hbm.shape[0], d_hbm.shape[0]
    own_loads, w_loads = [], []
    for plane in range(2):
        column = pl.multiple_of((core if plane == 0 else 1 - core) * geo.half, geo.half)
        own_loads.append(pltpu.make_async_copy(
            q_hbm.at[:, :, pl.ds(column, geo.half)], ownx.at[plane, pl.ds(0, n_q)], own_sem.at[2 * plane]))
        own_loads.append(pltpu.make_async_copy(
            d_hbm.at[:, :, pl.ds(column, geo.half)], ownx.at[plane, pl.ds(n_q, n_d)], own_sem.at[2 * plane + 1]))
        for lane in range(geo.nd):
            w_loads.append(pltpu.make_async_copy(
                w_hbm.at[pl.ds(pl.multiple_of(column + lane * geo.width, geo.width), geo.width), :],
                wv.at[plane, lane], w_sem.at[plane, lane]))
    for copy in own_loads + w_loads:
        copy.start()
    return own_loads, w_loads


def all_peers(geo, me):
    core = lax.rem(me, 2)
    found = [(0, 1 - core, geo.device(me, 0, 1 - core))]
    for rel in range(1, geo.chips):
        for other in range(2):
            found.append((rel, other, geo.device(me, rel, other)))
    return found


def fused_kernel(geo, const, q_hbm, d_hbm, w_hbm, bias, mrow, pos_ref, place, doc_place, pick,
                 loss_ref, gw_hbm, gb, gh_hbm,
                 xo, xs, stage, ownx, wv, wt, acc, z, dz, dzt, dho, sibout, sibin, dlo, dhi, m1, m2, m3,
                 r1, r2, r3, r4, ost, gout, early, rep, rd, drd, mall, mt, sbuf, pall, gmine, gall,
                 own_sem, w_sem, sd_send, sd_recv, rs_send, rs_recv, out_send, out_recv,
                 wout_sem, hout_sem, ex_send, ex_recv, *sems):
    nd, slab, unit, width, steps, rows, first = (geo.nd, geo.slab, geo.unit, geo.width, geo.steps, geo.rows,
                                                 geo.first)
    n_q, n_d, lam_q, lam_d, tau, q_batch, d_batch = const
    slots = 2 * geo.chips
    me = lax.axis_index("tp")
    net = Gather(geo, me, xo, xs, stage, ownx, sems)
    core = net.core
    same = [geo.peer(me, dim, core) for dim in range(nd)]
    peers = all_peers(geo, me)
    own_loads, w_loads = start_loads(geo, core, q_hbm, d_hbm, w_hbm, ownx, wv, own_sem, w_sem)
    xo[...] = jnp.zeros_like(xo)
    entry_barrier([device for _, _, device in peers])
    for copy in own_loads:
        copy.wait()
    for lane in range(nd):
        net.piece(lane, 0).start()

    def broadcast(kind, src_of, dst):
        return [pltpu.make_async_remote_copy(
            src_ref=src_of(2 * rel + other), dst_ref=dst.at[2 * rel + core],
            send_sem=ex_send.at[kind, i], recv_sem=ex_recv.at[kind, 2 * rel + core], device_id=device,
            device_id_type=MESH) for i, (rel, other, device) in enumerate(peers)]

    def arrivals(kind, dst):
        return [pltpu.make_async_remote_copy(
            src_ref=dst.at[2 * rel + other], dst_ref=dst.at[2 * rel + other],
            send_sem=ex_send.at[kind, i], recv_sem=ex_recv.at[kind, 2 * rel + other], device_id=device,
            device_id_type=MESH) for i, (rel, other, device) in enumerate(peers)]

    masks_out = broadcast(0, lambda slot: mrow, mall)
    for copy in masks_out:
        copy.start()
    mall[core] = mrow[...]
    gb[...] = jnp.zeros_like(gb)
    for ref in (dlo, m1, m2, m3):
        ref[...] = jnp.zeros_like(ref)

    def sib_dh(lane):
        return pltpu.make_async_remote_copy(
            src_ref=sibout.at[lane], dst_ref=sibin.at[lane], send_sem=sd_send.at[lane], recv_sem=sd_recv.at[lane],
            device_id=net.sib, device_id_type=MESH)

    def rs_copy(stage_no, lane, s):
        parity, ring = lax.rem(s, 2), lax.rem(s, 3)
        n_low = geo.tokens >> stage_no
        src = dhi.at[lane]
        if stage_no > 1:
            src = (m1, m2, m3)[stage_no - 2].at[ring, lane, pl.ds(n_low, n_low)]
        dst = (r1, r2, r3, r4)[stage_no - 1].at[parity, lane]
        return pltpu.make_async_remote_copy(
            src_ref=src, dst_ref=dst, send_sem=rs_send.at[stage_no - 1, lane],
            recv_sem=rs_recv.at[stage_no - 1, lane, parity],
            device_id=same[(lane + nd - stage_no) % nd], device_id_type=MESH)

    def out_copy(s):
        parity = lax.rem(s, 2)
        return pltpu.make_async_remote_copy(
            src_ref=ost.at[parity], dst_ref=gout.at[1, lax.rem(s - 9, rows)], send_sem=out_send.at[parity],
            recv_sem=out_recv.at[parity], device_id=net.sib, device_id_type=MESH)

    def merge(stage_no, lane, s, last, low):
        @pl.when(s < last)
        def _():
            rs_copy(stage_no, lane, s - 1).wait()
        got = (r1, r2, r3, r4)[stage_no - 1][lax.rem(s + 1, 2), lane].astype(F32)
        return jnp.where(s < last, got, 0.0) + low.astype(F32)

    def scatter(s):
        ring, back, prev = lax.rem(s, 3), lax.rem(s + 1, 3), lax.rem(s + 2, 3)
        low1, low2, low3, low4 = (geo.tokens >> k for k in range(1, 5))
        for lane in range(nd):
            cols = slice(lane * width, (lane + 1) * width)

            @pl.when((s >= first + 2) & (s <= steps + 2))
            def _():
                m1[ring, lane] = merge(1, lane, s, steps + 2, dlo[ring, lane]).astype(BF16)

            @pl.when((s >= first + 3) & (s <= steps + 4))
            def _():
                m2[ring, lane] = merge(2, lane, s, steps + 4, m1[back, lane, 0:low2]).astype(BF16)

            @pl.when((s >= first + 4) & (s <= steps + 6))
            def _():
                m3[ring, lane] = merge(3, lane, s, steps + 6, m2[back, lane, 0:low3]).astype(BF16)

            @pl.when((s >= first + 5) & (s <= steps + 8))
            def _():
                done = merge(4, lane, s, steps + 8, m3[back, lane, 0:low4])
                kept = lax.rem(s - first - 5, nd)

                @pl.when(s < first + 9)
                def _():
                    early[kept, lane] = done

                @pl.when(s >= first + 9)
                def _():
                    total = done + jnp.where(s >= steps + 5, early[kept, lane], 0.0)
                    one, two = total[0:unit], total[unit:slab]
                    gout[0, lax.rem(s - 9, rows), :, cols] = jnp.where(core == 0, one, two).astype(BF16)
                    ost[lax.rem(s, 2), :, cols] = jnp.where(core == 0, two, one).astype(BF16)

            @pl.when((s > first) & (s <= steps))
            def _():
                sib_dh(lane).wait()
                both = dho[lane] + sibin[lane].astype(F32)
                dlo[prev, lane] = both[0:low1].astype(BF16)
                dhi[lane] = both[low1:].astype(BF16)
                rs_copy(1, lane, s).start()

            @pl.when((s >= first + 2) & (s <= steps + 2))
            def _():
                rs_copy(2, lane, s).start()

            @pl.when((s >= first + 3) & (s <= steps + 4))
            def _():
                rs_copy(3, lane, s).start()

            @pl.when((s >= first + 4) & (s <= steps + 6))
            def _():
                rs_copy(4, lane, s).start()

        @pl.when((s >= first + 10) & (s <= steps + 8))
        def _():
            out_copy(s - 1).wait()

        @pl.when((s >= first + 9) & (s <= steps + 8))
        def _():
            out_copy(s).start()

    def own_part(s, lane):
        net.arrive(s, lane)

        @pl.when(s >= nd)
        def _():
            part = jnp.dot(net.tokens_of(xo, lane), wv[0, lane], preferred_element_type=F32)
            par = lax.rem(s, 2)
            if lane == 0:
                z[par] = part
            else:
                z[par] = z[par] + part

    def sib_part(s, lane):
        net.release_own(s, lane)
        net.share(lane).wait_recv()

        @pl.when(s >= nd)
        def _():
            par = lax.rem(s, 2)
            z[par] = z[par] + jnp.dot(net.tokens_of(xs, lane), wv[1, lane], preferred_element_type=F32)

    def reps(s):
        par = lax.rem(s, 2)
        for rel in range(geo.chips):
            logits = z[par, rel * slab:(rel + 1) * slab, :] + bias[...]
            active = jnp.log1p(jnp.maximum(logits, 0.0))
            row = lax.rem(s - geo.hops(rel), rows)
            for cr in range(2):
                at = 2 * rel + cr
                part = active[cr * unit:(cr + 1) * unit, :] * mt[row, :, at:at + 1]
                rep[at, pl.ds(row, 1), :] = jnp.sum(part, axis=0, keepdims=True)

    def prepare(s):
        @pl.when(s == 1)
        def _():
            for copy in w_loads:
                copy.wait()
            for copy in arrivals(0, mall):
                copy.wait_recv()
            for copy in masks_out:
                copy.wait_send()
            table = jnp.concatenate([mall[i] for i in range(slots)], axis=0)
            table = jnp.concatenate([table, jnp.zeros((128 - slots, table.shape[1]), F32)], axis=0)
            mt[...] = table.T.reshape(mt.shape)

        @pl.when((s >= 1) & (s <= nd))
        def _():
            def turn(k, carry):
                acc[k] = jnp.zeros(acc.shape[1:], F32)
                wt[k] = wv[lax.div(k, nd), lax.rem(k, nd)].T
                return carry

            lax.fori_loop(2 * (s - 1), 2 * s, turn, 0)

    def loss_step(s, carry):
        prepare(s)
        for lane in range(nd):
            @pl.when(s > 0)
            def _():
                net.release_sib(s - 1, lane)

            own_part(s, lane)
            if lane == 0:
                @pl.when(s > 0)
                def _():
                    net.forward(s - 1, nd - 1)

                @pl.when(s > nd)
                def _():
                    reps(s - 1)
            else:
                net.forward(s, lane - 1)
            sib_part(s, lane)
        return carry

    def softmax():
        chunk = 8
        parts = slots // chunk
        pieces = rep[:, n_q:rows, :].reshape((slots * (rows - n_q), geo.vocab))
        rd[...] = jnp.dot(pick[...], pieces, precision=HIGHEST, preferred_element_type=F32)

        def score(c, q_sum):
            at = pl.ds(c * chunk, chunk)
            reps_c = rep[at, 0:n_q, :].reshape((chunk * n_q, geo.vocab))
            part = lax.dot_general(reps_c, rd[...], (((1,), (1,)), ((), ())), precision=HIGHEST,
                                   preferred_element_type=F32)
            part = jnp.dot(part, doc_place[...], precision=HIGHEST, preferred_element_type=F32)
            sbuf[at] = part.reshape((chunk, n_q, part.shape[1]))
            return q_sum + jnp.sum(reps_c, axis=0, keepdims=True)

        q_sum = lax.fori_loop(0, parts, score, jnp.zeros((1, geo.vocab), F32))
        scores_out = broadcast(1, lambda slot: sbuf.at[slot], pall)
        for copy in scores_out:
            copy.start()
        pall[core] = sbuf[core]
        q_mean = q_sum / q_batch
        d_mean = jnp.sum(rd[...], axis=0, keepdims=True) / d_batch
        reg = (lam_q * jnp.sum(q_mean * q_mean, axis=1, keepdims=True)
               + lam_d * jnp.sum(d_mean * d_mean, axis=1, keepdims=True))
        for copy in arrivals(1, pall):
            copy.wait_recv()
        total = pall[0]
        for i in range(1, slots):
            total = total + pall[i]
        scores = total / tau
        lane_no = lax.broadcasted_iota(jnp.int32, scores.shape, 1)
        target = lane_no == pos_ref[...]
        masked = jnp.where(lane_no < d_batch, scores, -jnp.inf)
        top = jnp.max(masked, axis=1, keepdims=True)
        log_norm = jnp.log(jnp.sum(jnp.exp(masked - top), axis=1, keepdims=True)) + top
        hit = jnp.sum(jnp.where(target, scores, 0.0), axis=1, keepdims=True)
        mine = jnp.sum(log_norm - hit, axis=0, keepdims=True) / q_batch + reg
        grad = (jnp.exp(masked - log_norm) - target.astype(F32)) / (q_batch * tau)
        gmine[0:n_q, :] = grad
        gmine[n_q:, :] = jnp.broadcast_to(mine, (gmine.shape[0] - n_q, grad.shape[1]))
        grads_out = broadcast(2, lambda slot: gmine, gall)
        for copy in grads_out:
            copy.start()
        gall[core] = gmine[...]
        drd[...] = jnp.broadcast_to((2.0 * lam_d / d_batch) * d_mean, drd.shape)
        for copy in arrivals(2, gall):
            copy.wait_recv()
        by_device = jnp.zeros((1, place.shape[1]), F32)
        for i in range(slots):
            by_device = by_device + gall[i, n_q:n_q + 1, :] * place[i:i + 1, :]
        loss_ref[...] = jnp.broadcast_to(jnp.sum(by_device, axis=1, keepdims=True), loss_ref.shape)

        def back(c, carry):
            at = pl.ds(c * chunk, chunk)
            grad_c = gall[at, 0:n_q, :].reshape((chunk * n_q, gall.shape[2]))
            grad_c = lax.dot_general(grad_c, doc_place[...], (((1,), (1,)), ((), ())), precision=HIGHEST,
                                     preferred_element_type=F32)
            reps_c = rep[at, 0:n_q, :].reshape((chunk * n_q, geo.vocab))
            drd[...] += lax.dot_general(grad_c, reps_c, (((0,), (0,)), ((), ())), precision=HIGHEST,
                                        preferred_element_type=F32)
            drq = jnp.dot(grad_c, rd[...], precision=HIGHEST, preferred_element_type=F32)
            drq = drq + (2.0 * lam_q / q_batch) * q_mean
            rep[at, 0:n_q, :] = drq.reshape((chunk, n_q, geo.vocab))
            return carry

        lax.fori_loop(0, parts, back, 0)
        spread = lax.dot_general(pick[...], drd[...], (((0,), (0,)), ((), ())), precision=HIGHEST,
                                 preferred_element_type=F32)
        rep[:, n_q:rows, :] = spread.reshape((slots, rows - n_q, geo.vocab))
        for copy in scores_out + grads_out:
            copy.wait_send()

    def logits_grad(s):
        total = gb[...]
        for rel in range(geo.chips):
            logits = z[0, rel * slab:(rel + 1) * slab, :] + bias[...]
            slope = jnp.where(logits > 0.0, 1.0 / (1.0 + jnp.maximum(logits, 0.0)), 0.0)
            row = lax.rem(s - geo.hops(rel), rows)
            parts = []
            for cr in range(2):
                at = 2 * rel + cr
                grad_row = rep[at, pl.ds(row, 1), :]
                part = grad_row * slope[cr * unit:(cr + 1) * unit, :] * mt[row, :, at:at + 1]
                total = total + part
                parts.append(part)
            dz[rel * slab:(rel + 1) * slab, :] = jnp.concatenate(parts, axis=0).astype(BF16)
        gb[...] = total
        dzt[...] = dz[...].T

    def grad_step(s):
        def sib_dot(lane):
            net.share(lane).wait_recv()
            z[0] += jnp.dot(net.tokens_of(xs, lane), wv[1, lane], preferred_element_type=F32)

        for lane in range(nd):
            net.release_sib(s - 1, lane)
            net.arrive(s, lane)
            part = jnp.dot(net.tokens_of(xo, lane), wv[0, lane], preferred_element_type=F32)
            if lane == 0:
                z[0] = part
            else:
                z[0] += part
                sib_dot(lane - 1)
        sib_dot(nd - 1)
        logits_grad(s)
        for lane in range(nd):
            acc[lane] += jnp.dot(dzt[...], net.tokens_of(xo, lane), preferred_element_type=F32)
            net.release_own(s, lane)
        for lane in range(nd):
            acc[nd + lane] += jnp.dot(dzt[...], net.tokens_of(xs, lane), preferred_element_type=F32)
            if lane >= 1:
                net.forward(s, lane - 1)
        for lane in range(nd):
            part = jnp.dot(dz[...], wt[nd + lane], preferred_element_type=F32)
            for rel in range(geo.chips):
                at = geo.slot(rel, lane) * slab
                sibout[lane, at:at + slab, :] = part[rel * slab:(rel + 1) * slab, :].astype(BF16)
            sib_dh(lane).start()
            if lane == 0:
                net.forward(s, nd - 1)
        for lane in range(nd):
            part = jnp.dot(dz[...], wt[lane], preferred_element_type=F32)
            for rel in range(geo.chips):
                at = geo.slot(rel, lane) * slab
                dho[lane, at:at + slab, :] = part[rel * slab:(rel + 1) * slab, :]

    def wout(k):
        plane, lane = lax.div(k, nd), lax.rem(k, nd)
        half_no = core + plane - 2 * core * plane
        column = half_no * geo.half + lane * width
        return pltpu.make_async_copy(
            wv.at[plane, lane], gw_hbm.at[pl.ds(pl.multiple_of(column, width), width), :], wout_sem.at[k])

    def body(s, carry):
        scatter(s)

        @pl.when(s < steps)
        def _():
            grad_step(s)

        @pl.when((s >= steps) & (s < steps + 2 * nd))
        def _():
            k = s - steps
            wv[lax.div(k, nd), lax.rem(k, nd)] = acc[k].astype(BF16).T
            wout(k).start()
        return carry

    lax.fori_loop(0, first, loss_step, 0)
    net.forward(first - 1, nd - 1)
    reps(first - 1)
    softmax()
    lax.fori_loop(first, steps + 9, body, 0)
    out_copy(steps + 8).wait()
    stores = []
    for plane in range(2):
        column = pl.multiple_of((core if plane == 0 else 1 - core) * geo.half, geo.half)
        stores.append(pltpu.make_async_copy(gout.at[plane], gh_hbm.at[:, :, pl.ds(column, geo.half)],
                                            hout_sem.at[plane]))
    for copy in stores:
        copy.start()
    for copy in stores:
        copy.wait()
    for k in range(2 * nd):
        wout(k).wait()


def call_fused(geo, const, q_rows, d_rows, w_head, bias, mrow, positive, place, doc_place, pick):
    bufs, sems = gather_scratch(geo)
    dma = pltpu.SemaphoreType.DMA
    nd, tok, width, vocab, rows = geo.nd, geo.tokens, geo.width, geo.vocab, geo.rows
    n_q, docs, slots = const[0], doc_place.shape[0], 2 * geo.chips
    lanes = doc_place.shape[1]
    tile = n_q + 8
    hbm, vmem = pl.BlockSpec(memory_space=pl.ANY), pl.BlockSpec(memory_space=pltpu.VMEM)
    scratch = bufs + [
        pltpu.VMEM((2, nd, width, vocab), BF16), pltpu.VMEM((2 * nd, vocab, width), BF16),
        pltpu.VMEM((2 * nd, vocab, width), F32), pltpu.VMEM((2, tok, vocab), F32), pltpu.VMEM((tok, vocab), BF16),
        pltpu.VMEM((vocab, tok), BF16), pltpu.VMEM((nd, tok, width), F32), pltpu.VMEM((nd, tok, width), BF16),
        pltpu.VMEM((nd, tok, width), BF16), pltpu.VMEM((3, nd, tok // 2, width), BF16),
        pltpu.VMEM((nd, tok // 2, width), BF16), pltpu.VMEM((3, nd, tok // 2, width), BF16),
        pltpu.VMEM((3, nd, tok // 4, width), BF16), pltpu.VMEM((3, nd, tok // 8, width), BF16),
        pltpu.VMEM((2, nd, tok // 2, width), BF16), pltpu.VMEM((2, nd, tok // 4, width), BF16),
        pltpu.VMEM((2, nd, tok // 8, width), BF16), pltpu.VMEM((2, nd, tok // 16, width), BF16),
        pltpu.VMEM((2, geo.unit, geo.half), BF16), pltpu.VMEM((2, rows, geo.unit, geo.half), BF16),
        pltpu.VMEM((nd, nd, geo.slab, width), F32),
        pltpu.VMEM((slots, rows, vocab), F32), pltpu.VMEM((docs, vocab), F32), pltpu.VMEM((docs, vocab), F32),
        pltpu.VMEM((slots,) + mrow.shape, F32), pltpu.VMEM((mrow.shape[1] // geo.unit, geo.unit, 128), F32),
        pltpu.VMEM((slots, n_q, lanes), F32), pltpu.VMEM((slots, n_q, lanes), F32),
        pltpu.VMEM((tile, lanes), F32), pltpu.VMEM((slots, tile, lanes), F32),
        dma((4,)), dma((2, nd)), dma((nd,)), dma((nd,)), dma((4, nd)), dma((4, nd, 2)), dma((2,)), dma((2,)),
        dma((2 * nd,)), dma((2,)), dma((3, slots)), dma((3, slots))] + sems
    return pl.pallas_call(
        functools.partial(fused_kernel, geo, const),
        name="lexical_head",
        out_shape=[jax.ShapeDtypeStruct((1, 128), F32), jax.ShapeDtypeStruct(w_head.shape, BF16),
                   jax.ShapeDtypeStruct((geo.unit, vocab), F32),
                   jax.ShapeDtypeStruct((rows, geo.unit, 2 * geo.half), BF16)],
        in_specs=[hbm, hbm, hbm] + [vmem] * 6,
        out_specs=[vmem, hbm, vmem, hbm],
        scratch_shapes=scratch,
        compiler_params=pltpu.CompilerParams(collective_id=0, has_side_effects=True, vmem_limit_bytes=VMEM_LIMIT),
    )(q_rows, d_rows, w_head, bias, mrow, positive, place, doc_place, pick)


def solution(mesh):
    n_group = mesh.shape['tp']
    row_spec = P(('dp', 'tp'))
    mask_spec = P(('dp', 'tp'), None)
    hid_spec = P(('dp', 'tp'), None, None)

    def local_step(q_hidden, d_hidden, q_mask, d_mask, positive, w_head, b_head):
        hidden_size, vocab_loc = w_head.shape
        vocab_size = vocab_loc * n_group
        n_q, q_len, _ = q_hidden.shape
        n_d, d_len, _ = d_hidden.shape
        pieces = d_len // q_len
        q_batch, d_batch = n_q * n_group, n_d * n_group
        tau = q_len * math.sqrt(vocab_size * d_len) / 16.0
        lam_q = 4.0 / (vocab_size * q_len * q_len)
        lam_d = 4.0 / (vocab_size * d_len * d_len)
        rows = n_q + n_d * pieces
        geo = Geometry(n_group, rows, hidden_size, vocab_loc, q_len)
        side, slots = geo.side, 2 * geo.chips
        lanes = max(128, d_batch)

        me = lax.axis_index('tp')
        slot = jnp.arange(slots)
        chip, rel = me // 2, slot // 2
        step_x, step_y = rel % side, rel // side
        chip_of = (((chip // side) ^ step_y ^ (step_y >> 1)) * side + ((chip % side) ^ step_x ^ (step_x >> 1)))
        device_of = chip_of * 2 + slot % 2
        place = (device_of[:, None] == jnp.arange(lanes)[None, :]).astype(F32)
        doc_of = (device_of[None, :] * n_d + jnp.arange(n_d)[:, None]).reshape((n_d * slots,))
        doc_place = (doc_of[:, None] == jnp.arange(lanes)[None, :]).astype(F32)
        doc_row = np.arange(n_d * slots)
        unit_row = np.arange(slots * n_d * pieces)
        pick = ((doc_row[:, None] % slots == unit_row[None, :] // (n_d * pieces))
                & (doc_row[:, None] // slots == unit_row[None, :] % (n_d * pieces) // pieces)).astype(np.float32)

        own_mask = jnp.concatenate([q_mask.reshape((-1,)), d_mask.reshape((-1,))]).astype(F32)
        mrow = jnp.pad(own_mask, (0, -own_mask.shape[0] % 128)).reshape((1, -1))
        const = (n_q, n_d, lam_q, lam_d, tau, float(q_batch), float(d_batch))
        loss, grad_w, grad_b, grad_h = call_fused(
            geo, const, q_hidden, d_hidden.reshape((n_d * pieces, q_len, hidden_size)), w_head,
            b_head.reshape((1, vocab_loc)), mrow, positive.reshape((n_q, 1)), place, doc_place, jnp.asarray(pick))
        return (loss[0, 0:1], grad_w, jnp.sum(grad_b, axis=0), grad_h[:n_q], grad_h[n_q:].reshape(d_hidden.shape))

    return jax.shard_map(local_step, mesh=mesh,
                         in_specs=(hid_spec, hid_spec, mask_spec, mask_spec, row_spec, P(None, 'tp'), P('tp')),
                         out_specs=(P('dp'), P('dp', 'tp'), row_spec, hid_spec, hid_spec),
                         check_vma=False)
```

time: 865 us -> 666 us (0.77)
  waiting for transfers between devices: 90.4 us -> 0 us
  blocking collectives: 32.4 us -> 0 us
  Pallas kernels: 672 us -> 644 us
  other arithmetic: 17.8 us -> 2.76 us
  between operations: 17.3 us -> 2.53 us
  local copies, waits for them, and re-layouts: 25.4 us -> 15.5 us
  matrix products: 8.85 us -> 0 us
    psum x1 -> x0, waiting for transfers between devices: 90.4 us -> none  [local_step(): summed = lax.psum(jnp.concatenate([score_part, reg_part], axis=0), 'tp')]
    all_gather x1 -> x0, blocking collectives: 32.4 us -> none  [local_step(): all_ints = lax.all_gather(own_ints, 'tp')]
    pallas_call x2 -> x1, Pallas kernels: 672 us -> 644 us  [call_fused(): pl.pallas_call(functools.partial(fused_kernel, geo, const), name='lexical...]
    dot_general x8 -> x0, matrix products: 8.85 us -> none  [the longest x2 1.87 us: local_step(): jnp.einsum('erfi,je,kf->rjik', grad_part, place, place, precision=HIGHEST)]
  transfers between devices with their start and end apart: 1 -> 0, of which waited for: 1 -> 0; matrix products, arithmetic and copies ran while one was open for 0% -> 0% of each run, Pallas kernels for 0% -> 0%
where the time goes in v2:
time: 666 us; the launch traced here: 665 us
  Pallas kernels  644 us (97%)
  local copies, waits for them, and re-layouts  15.5 us (2%)
    pallas_call x1, Pallas kernels, call_fused(): pl.pallas_call(functools.partial(fused_kernel, geo, const), name='lexical...  644 us

profile of v2, /device:TPU:97, one launch (start us, length us, event | category | flops | bytes accessed | tf_op | source)
XLA Modules:
  0.0 665.2 jit_solution(376382012307464004)
XLA Ops:
  0.7 0.1 add.104
  0.8 0.8 reshape.162
  1.5 0.8 copy.15
  2.3 0.1 reshape.161
  2.4 0.6 pad.4
  3.0 1.3 copy.16.pos_ref
  4.3 0.7 fusion.1.place
  5.0 0.7 fusion.doc_place
  5.7 644.4 %lexical_head.1 = (f32[1,128]{1,0:T(1,128)}, bf16[4096,1024]{1,0:T(8,128)(2,1)}, f32[8,1024]{1,0:T(8,128)}, bf16[24,8,4096]{2,1,0:T(8,128)(2,1)}) custom-call(bf16[16,8,4096]{2,1,0:T(8,128)(2,1)} %q_hbm.1, bf16[8,8,4096]{2,1,0:T(8,128)(2,1)} %bitcast.7, bf16[4096,1024]{1,0:T(8,128)(2,1)} %w_hbm.1, f32[1,1024]{1,0:T(1,128)} %bitcast.9, f32[1,256]{1,0:T(1,128)} %bitcast.10, ...), custom_call_target="tpu_custom_call" | custom-call | tf_op jit(solution)/shard_map/lexical_head/pallas_call | solution.py:592
  650.1 1.4 reduce_sum.9
  651.4 1.9 slice.11
  653.3 2.3 slice.10
  656.3 7.8 %copy.20 = bf16[4096,1024]{1,0:T(8,128)(2,1)} copy(bf16[4096,1024]{1,0:T(8,128)(2,1)} %get-tuple-element.21) | data formatting | bytes 16777216
  (3 shorter events, 0.0 us)

commit v3 on v2

--- a/solution.py
+++ b/solution.py
@@ -63,120 +63,85 @@
 
 
 class Gather:
-    def __init__(self, geo, me, xo, xs, stage, ownx, sems):
-        (self.ici_send, self.ici_recv, self.share_send, self.share_recv, self.piece_send, self.piece_recv,
-         self.free_ici, self.free_piece, self.free_xs) = sems
-        self.geo, self.xo, self.xs, self.stage, self.ownx = geo, xo, xs, stage, ownx
+    def __init__(self, geo, me, x, stage, ownx, sems):
+        (self.ici_send, self.ici_recv, self.piece_send, self.piece_recv, self.free_ici, self.free_piece) = sems
+        self.geo, self.x, self.stage, self.ownx = geo, x, stage, ownx
         self.core = lax.rem(me, 2)
         self.sib = {"tp": me + 1 - 2 * self.core}
-        self.cross = [geo.peer(me, dim, 1 - self.core) for dim in range(geo.nd)]
-
-    def ici(self, lane, pos):
+        self.same = [geo.peer(me, dim, self.core) for dim in range(geo.nd)]
+
+    def ici(self, s, lane, pos):
         count = (1 << pos) * self.geo.slab
+        here, there = lax.rem(s, 2), lax.rem(s + 1, 2)
         return pltpu.make_async_remote_copy(
-            src_ref=self.xs.at[lane, pl.ds(0, count)], dst_ref=self.xo.at[lane, pl.ds(count, count)],
-            send_sem=self.ici_send.at[lane, pos], recv_sem=self.ici_recv.at[lane, pos],
-            device_id=self.cross[(lane + pos) % self.geo.nd], device_id_type=MESH)
-
-    def share(self, lane):
+            src_ref=self.x.at[here, lane, pl.ds(0, count)], dst_ref=self.x.at[there, lane, pl.ds(count, count)],
+            send_sem=self.ici_send.at[lane, pos, there], recv_sem=self.ici_recv.at[lane, pos, there],
+            device_id=self.same[(lane + pos) % self.geo.nd], device_id_type=MESH)
+
+    def piece(self, s, lane):
+        width, parity = self.geo.width, lax.rem(s, 2)
         return pltpu.make_async_remote_copy(
-            src_ref=self.xo.at[lane], dst_ref=self.xs.at[lane],
-            send_sem=self.share_send.at[lane], recv_sem=self.share_recv.at[lane],
-            device_id=self.sib, device_id_type=MESH)
-
-    def piece(self, lane, row):
-        width = self.geo.width
-        return pltpu.make_async_remote_copy(
-            src_ref=self.ownx.at[1, row, :, pl.ds(lane * width, width)], dst_ref=self.stage.at[lane],
-            send_sem=self.piece_send.at[lane], recv_sem=self.piece_recv.at[lane],
-            device_id=self.sib, device_id_type=MESH)
+            src_ref=self.ownx.at[1, lax.rem(s, self.geo.rows), :, pl.ds(lane * width, width)],
+            dst_ref=self.stage.at[parity, lane], send_sem=self.piece_send.at[lane, parity],
+            recv_sem=self.piece_recv.at[lane, parity], device_id=self.sib, device_id_type=MESH)
 
     def arrive(self, s, lane):
         geo = self.geo
-        width = geo.width
-
-        row = lax.rem(s, geo.rows)
-        self.piece(lane, row).wait()
-        mine = self.ownx[0, row, :, lane * width:(lane + 1) * width].astype(F32)
-        theirs = self.stage[lane].astype(F32)
+        width, parity = geo.width, lax.rem(s, 2)
+        self.piece(s, lane).wait()
+        mine = self.ownx[0, lax.rem(s, geo.rows), :, lane * width:(lane + 1) * width].astype(F32)
+        theirs = self.stage[parity, lane].astype(F32)
         first = jnp.where(self.core == 0, mine, theirs)
         second = jnp.where(self.core == 0, theirs, mine)
-        self.xo[lane, 0:geo.slab, :] = jnp.concatenate([first, second], axis=0).astype(BF16)
+        self.x[parity, lane, 0:geo.slab, :] = jnp.concatenate([first, second], axis=0).astype(BF16)
 
         @pl.when(s > 0)
         def _():
             for pos in range(geo.nd):
-                self.ici(lane, pos).wait_recv()
-            pl.semaphore_wait(self.free_xs.at[lane], 1)
-
-        self.share(lane).start()
-
-    def release_own(self, s, lane):
+                self.ici(s - 1, lane, pos).wait_recv()
+
+        @pl.when((s > 0) & (s < geo.steps - 1))
+        def _():
+            pl.semaphore_wait(self.free_piece.at[lane], 1)
+            for pos in range(geo.nd):
+                pl.semaphore_wait(self.free_ici.at[lane, pos], 1)
+
+        @pl.when(s < geo.steps - 1)
+        def _():
+            for pos in reversed(range(geo.nd)):
+                self.ici(s, lane, pos).start()
+            self.piece(s + 1, lane).start()
+
+    def release(self, s, lane):
         geo = self.geo
-        self.share(lane).wait_send()
 
         @pl.when(s < geo.steps - 1)
+        def _():
+            for pos in range(geo.nd):
+                self.ici(s, lane, pos).wait_send()
+
+        @pl.when(s < geo.steps - 2)
         def _():
             for pos in range(geo.nd):
                 pl.semaphore_signal(self.free_ici.at[lane, pos], inc=1,
-                                    device_id=self.cross[(lane + pos) % geo.nd], device_id_type=MESH)
+                                    device_id=self.same[(lane + pos) % geo.nd], device_id_type=MESH)
             pl.semaphore_signal(self.free_piece.at[lane], inc=1, device_id=self.sib, device_id_type=MESH)
 
-    def forward(self, s, lane):
-        geo = self.geo
-
-        @pl.when(s < geo.steps - 1)
-        def _():
-            pl.semaphore_wait(self.free_piece.at[lane], 1)
-            self.piece(lane, lax.rem(s + 1, geo.rows)).start()
-            for pos in reversed(range(geo.nd)):
-                pl.semaphore_wait(self.free_ici.at[lane, pos], 1)
-                self.ici(lane, pos).start()
-
-    def release_sib(self, s, lane):
-        geo = self.geo
-
-        @pl.when(s < geo.steps - 1)
-        def _():
-            for pos in range(geo.nd):
-                self.ici(lane, pos).wait_send()
-            pl.semaphore_signal(self.free_xs.at[lane], inc=1, device_id=self.sib, device_id_type=MESH)
-
-    def tokens_of(self, ref, lane):
-        geo = self.geo
+    def tokens(self, s, lane):
+        geo, parity = self.geo, lax.rem(s, 2)
         if lane == 0:
-            return ref[lane]
+            return self.x[parity, lane]
         places = [geo.slot(rel, lane) * geo.slab for rel in range(geo.chips)]
-        return jnp.concatenate([ref[lane, at:at + geo.slab, :] for at in places], axis=0)
+        return jnp.concatenate([self.x[parity, lane, at:at + geo.slab, :] for at in places], axis=0)
 
 
 def gather_scratch(geo):
     nd = geo.nd
-    lane = pltpu.VMEM((nd, geo.tokens, geo.width), BF16)
-    bufs = [lane, lane, pltpu.VMEM((nd, geo.unit, geo.width), BF16),
+    bufs = [pltpu.VMEM((2, nd, geo.tokens, geo.width), BF16), pltpu.VMEM((2, nd, geo.unit, geo.width), BF16),
             pltpu.VMEM((2, geo.rows, geo.unit, geo.half), BF16)]
     dma, reg = pltpu.SemaphoreType.DMA, pltpu.SemaphoreType.REGULAR
-    sems = [dma((nd, nd)), dma((nd, nd)), dma((nd,)), dma((nd,)), dma((nd,)), dma((nd,)),
-            reg((nd, nd)), reg((nd,)), reg((nd,))]
+    sems = [dma((nd, nd, 2)), dma((nd, nd, 2)), dma((nd, 2)), dma((nd, 2)), reg((nd, nd)), reg((nd,))]
     return bufs, sems
-
-
-def start_loads(geo, core, q_hbm, d_hbm, w_hbm, ownx, wv, own_sem, w_sem):
-    n_q, n_d = q_hbm.shape[0], d_hbm.shape[0]
-    own_loads, w_loads = [], []
-    for plane in range(2):
-        column = pl.multiple_of((core if plane == 0 else 1 - core) * geo.half, geo.half)
-        own_loads.append(pltpu.make_async_copy(
-            q_hbm.at[:, :, pl.ds(column, geo.half)], ownx.at[plane, pl.ds(0, n_q)], own_sem.at[2 * plane]))
-        own_loads.append(pltpu.make_async_copy(
-            d_hbm.at[:, :, pl.ds(column, geo.half)], ownx.at[plane, pl.ds(n_q, n_d)], own_sem.at[2 * plane + 1]))
-        for lane in range(geo.nd):
-            w_loads.append(pltpu.make_async_copy(
-                w_hbm.at[pl.ds(pl.multiple_of(column + lane * geo.width, geo.width), geo.width), :],
-                wv.at[plane, lane], w_sem.at[plane, lane]))
-    for copy in own_loads + w_loads:
-        copy.start()
-    return own_loads, w_loads
 
 
 def all_peers(geo, me):
@@ -190,26 +155,44 @@
 
 def fused_kernel(geo, const, q_hbm, d_hbm, w_hbm, bias, mrow, pos_ref, place, doc_place, pick,
                  loss_ref, gw_hbm, gb, gh_hbm,
-                 xo, xs, stage, ownx, wv, wt, acc, z, dz, dzt, dho, sibout, sibin, dlo, dhi, m1, m2, m3,
+                 x, stage, ownx, wv, wt, acc, zo, zs, zr, dz, dzt, dlo, dhi, m1, m2, m3,
                  r1, r2, r3, r4, ost, gout, early, rep, rd, drd, mall, mt, sbuf, pall, gmine, gall,
-                 own_sem, w_sem, sd_send, sd_recv, rs_send, rs_recv, out_send, out_recv,
-                 wout_sem, hout_sem, ex_send, ex_recv, *sems):
+                 own_sem, w_sem, wx_send, wx_recv, z_send, z_recv, dz_send, dz_recv, rs_send, rs_recv,
+                 out_send, out_recv, wout_sem, wo_send, wo_recv, hout_sem, ex_send, ex_recv, *sems):
     nd, slab, unit, width, steps, rows, first = (geo.nd, geo.slab, geo.unit, geo.width, geo.steps, geo.rows,
                                                  geo.first)
     n_q, n_d, lam_q, lam_d, tau, q_batch, d_batch = const
-    slots = 2 * geo.chips
+    slots, vocab = 2 * geo.chips, geo.vocab
     me = lax.axis_index("tp")
-    net = Gather(geo, me, xo, xs, stage, ownx, sems)
-    core = net.core
-    same = [geo.peer(me, dim, core) for dim in range(nd)]
+    net = Gather(geo, me, x, stage, ownx, sems)
+    core, same = net.core, net.same
     peers = all_peers(geo, me)
-    own_loads, w_loads = start_loads(geo, core, q_hbm, d_hbm, w_hbm, ownx, wv, own_sem, w_sem)
-    xo[...] = jnp.zeros_like(xo)
+    half_at = [pl.multiple_of(core * geo.half, geo.half), pl.multiple_of((1 - core) * geo.half, geo.half)]
+
+    n_dp = d_hbm.shape[0]
+    own_loads = []
+    for half in range(2):
+        cols = pl.ds(half_at[half], geo.half)
+        own_loads.append(pltpu.make_async_copy(q_hbm.at[:, :, cols], ownx.at[half, pl.ds(0, n_q)],
+                                               own_sem.at[2 * half]))
+        own_loads.append(pltpu.make_async_copy(d_hbm.at[:, :, cols], ownx.at[half, pl.ds(n_q, n_dp)],
+                                               own_sem.at[2 * half + 1]))
+    w_loads, w_cross = [], []
+    for lane in range(nd):
+        here = pl.ds(pl.multiple_of(half_at[0] + lane * width, width), width)
+        there = pl.ds(pl.multiple_of(half_at[1] + lane * width, width), width)
+        w_loads.append(pltpu.make_async_copy(w_hbm.at[here, :], wv.at[lane, :, pl.ds(0, vocab)], w_sem.at[lane]))
+        w_cross.append(pltpu.make_async_remote_copy(
+            src_ref=w_hbm.at[there, :], dst_ref=wv.at[lane, :, pl.ds(vocab, vocab)], send_sem=wx_send.at[lane],
+            recv_sem=wx_recv.at[lane], device_id=net.sib, device_id_type=MESH))
+    for copy in own_loads + w_loads:
+        copy.start()
+    x[...] = jnp.zeros_like(x)
     entry_barrier([device for _, _, device in peers])
     for copy in own_loads:
         copy.wait()
     for lane in range(nd):
-        net.piece(lane, 0).start()
+        net.piece(0, lane).start()
 
     def broadcast(kind, src_of, dst):
         return [pltpu.make_async_remote_copy(
@@ -228,13 +211,24 @@
         copy.start()
     mall[core] = mrow[...]
     gb[...] = jnp.zeros_like(gb)
+    for copy in w_cross:
+        copy.start()
     for ref in (dlo, m1, m2, m3):
         ref[...] = jnp.zeros_like(ref)
 
-    def sib_dh(lane):
+    def z_copy(s):
+        parity = lax.rem(s, 2)
         return pltpu.make_async_remote_copy(
-            src_ref=sibout.at[lane], dst_ref=sibin.at[lane], send_sem=sd_send.at[lane], recv_sem=sd_recv.at[lane],
+            src_ref=zs.at[parity], dst_ref=zr.at[parity], send_sem=z_send.at[parity], recv_sem=z_recv.at[parity],
             device_id=net.sib, device_id_type=MESH)
+
+    def dz_copies():
+        return [pltpu.make_async_remote_copy(
+            src_ref=dzt.at[pl.ds(0, vocab)], dst_ref=dzt.at[pl.ds(vocab, vocab)], send_sem=dz_send.at[0],
+            recv_sem=dz_recv.at[0], device_id=net.sib, device_id_type=MESH),
+            pltpu.make_async_remote_copy(
+                src_ref=dz.at[:, pl.ds(0, vocab)], dst_ref=dz.at[:, pl.ds(vocab, vocab)], send_sem=dz_send.at[1],
+                recv_sem=dz_recv.at[1], device_id=net.sib, device_id_type=MESH)]
 
     def rs_copy(stage_no, lane, s):
         parity, ring = lax.rem(s, 2), lax.rem(s, 3)
@@ -262,7 +256,7 @@
         return jnp.where(s < last, got, 0.0) + low.astype(F32)
 
     def scatter(s):
-        ring, back, prev = lax.rem(s, 3), lax.rem(s + 1, 3), lax.rem(s + 2, 3)
+        ring, back = lax.rem(s, 3), lax.rem(s + 1, 3)
         low1, low2, low3, low4 = (geo.tokens >> k for k in range(1, 5))
         for lane in range(nd):
             cols = slice(lane * width, (lane + 1) * width)
@@ -282,27 +276,18 @@
             @pl.when((s >= first + 5) & (s <= steps + 8))
             def _():
                 done = merge(4, lane, s, steps + 8, m3[back, lane, 0:low4])
-                kept = lax.rem(s - first - 5, nd)
-
                 @pl.when(s < first + 9)
                 def _():
-                    early[kept, lane] = done
+                    early[lax.rem(s - first - 5, nd), lane] = done
 
                 @pl.when(s >= first + 9)
                 def _():
+                    kept = lax.rem(s - first - 5 + nd - rows % nd, nd)
                     total = done + jnp.where(s >= steps + 5, early[kept, lane], 0.0)
                     one, two = total[0:unit], total[unit:slab]
                     gout[0, lax.rem(s - 9, rows), :, cols] = jnp.where(core == 0, one, two).astype(BF16)
                     ost[lax.rem(s, 2), :, cols] = jnp.where(core == 0, two, one).astype(BF16)
 
-            @pl.when((s > first) & (s <= steps))
-            def _():
-                sib_dh(lane).wait()
-                both = dho[lane] + sibin[lane].astype(F32)
-                dlo[prev, lane] = both[0:low1].astype(BF16)
-                dhi[lane] = both[low1:].astype(BF16)
-                rs_copy(1, lane, s).start()
-
             @pl.when((s >= first + 2) & (s <= steps + 2))
             def _():
                 rs_copy(2, lane, s).start()
@@ -323,31 +308,22 @@
         def _():
             out_copy(s).start()
 
-    def own_part(s, lane):
-        net.arrive(s, lane)
-
-        @pl.when(s >= nd)
-        def _():
-            part = jnp.dot(net.tokens_of(xo, lane), wv[0, lane], preferred_element_type=F32)
-            par = lax.rem(s, 2)
+    def logits_part(s, lane):
+        parity = lax.rem(s, 2)
+        tokens = net.tokens(s, lane)
+        for ref, at in ((zs, vocab), (zo, 0)):
+            part = jnp.dot(tokens, wv[lane, :, at:at + vocab], preferred_element_type=F32)
             if lane == 0:
-                z[par] = part
+                ref[parity] = part
             else:
-                z[par] = z[par] + part
-
-    def sib_part(s, lane):
-        net.release_own(s, lane)
-        net.share(lane).wait_recv()
-
-        @pl.when(s >= nd)
-        def _():
-            par = lax.rem(s, 2)
-            z[par] = z[par] + jnp.dot(net.tokens_of(xs, lane), wv[1, lane], preferred_element_type=F32)
+                ref[parity] = ref[parity] + part
 
     def reps(s):
-        par = lax.rem(s, 2)
+        parity = lax.rem(s, 2)
+        z_copy(s).wait()
         for rel in range(geo.chips):
-            logits = z[par, rel * slab:(rel + 1) * slab, :] + bias[...]
+            span = slice(rel * slab, (rel + 1) * slab)
+            logits = zo[parity, span, :] + zr[parity, span, :] + bias[...]
             active = jnp.log1p(jnp.maximum(logits, 0.0))
             row = lax.rem(s - geo.hops(rel), rows)
             for cr in range(2):
@@ -368,34 +344,44 @@
             table = jnp.concatenate([table, jnp.zeros((128 - slots, table.shape[1]), F32)], axis=0)
             mt[...] = table.T.reshape(mt.shape)
 
-        @pl.when((s >= 1) & (s <= nd))
-        def _():
-            def turn(k, carry):
-                acc[k] = jnp.zeros(acc.shape[1:], F32)
-                wt[k] = wv[lax.div(k, nd), lax.rem(k, nd)].T
+        @pl.when(s == 2)
+        def _():
+            for copy in w_cross:
+                copy.wait()
+
+        @pl.when((s >= 2) & (s < 2 + nd))
+        def _():
+            def turn(part, carry):
+                span = pl.ds(pl.multiple_of(part * vocab, vocab), vocab)
+                acc[s - 2, span, :] = jnp.zeros((vocab, width), F32)
+                wt[s - 2, span, :] = wv[s - 2, :, span].T
                 return carry
 
-            lax.fori_loop(2 * (s - 1), 2 * s, turn, 0)
+            lax.fori_loop(0, 2, turn, 0)
 
     def loss_step(s, carry):
         prepare(s)
         for lane in range(nd):
-            @pl.when(s > 0)
-            def _():
-                net.release_sib(s - 1, lane)
-
-            own_part(s, lane)
-            if lane == 0:
+            net.arrive(s, lane)
+
+            @pl.when(s >= nd)
+            def _():
+                logits_part(s, lane)
+
+            if lane >= 2:
+                net.release(s, lane - 2)
+            else:
                 @pl.when(s > 0)
                 def _():
-                    net.forward(s - 1, nd - 1)
-
+                    net.release(s - 1, lane + nd - 2)
+            if lane == 1:
                 @pl.when(s > nd)
                 def _():
                     reps(s - 1)
-            else:
-                net.forward(s, lane - 1)
-            sib_part(s, lane)
+
+        @pl.when(s >= nd)
+        def _():
+            z_copy(s).start()
         return carry
 
     def softmax():
@@ -471,97 +457,99 @@
             copy.wait_send()
 
     def logits_grad(s):
+        parity = lax.rem(s, 2)
+        z_copy(s).wait()
         total = gb[...]
         for rel in range(geo.chips):
-            logits = z[0, rel * slab:(rel + 1) * slab, :] + bias[...]
-            slope = jnp.where(logits > 0.0, 1.0 / (1.0 + jnp.maximum(logits, 0.0)), 0.0)
+            span = slice(rel * slab, (rel + 1) * slab)
+            logits = zo[parity, span, :] + zr[parity, span, :] + bias[...]
+            inverse = 1.0 / (1.0 + logits)
             row = lax.rem(s - geo.hops(rel), rows)
             parts = []
             for cr in range(2):
                 at = 2 * rel + cr
-                grad_row = rep[at, pl.ds(row, 1), :]
-                part = grad_row * slope[cr * unit:(cr + 1) * unit, :] * mt[row, :, at:at + 1]
-                total = total + part
-                parts.append(part)
-            dz[rel * slab:(rel + 1) * slab, :] = jnp.concatenate(parts, axis=0).astype(BF16)
+                part = slice(cr * unit, (cr + 1) * unit)
+                grad_row = rep[at, pl.ds(row, 1), :] * inverse[part, :]
+                grad_row = jnp.where(logits[part, :] > 0.0, grad_row, 0.0) * mt[row, :, at:at + 1]
+                total = total + grad_row
+                parts.append(grad_row)
+            dz[span, 0:vocab] = jnp.concatenate(parts, axis=0).astype(BF16)
         gb[...] = total
-        dzt[...] = dz[...].T
-
-    def grad_step(s):
-        def sib_dot(lane):
-            net.share(lane).wait_recv()
-            z[0] += jnp.dot(net.tokens_of(xs, lane), wv[1, lane], preferred_element_type=F32)
-
+        dzt[0:vocab, :] = dz[:, 0:vocab].T
+
+    def grad_step(s, carry):
         for lane in range(nd):
-            net.release_sib(s - 1, lane)
             net.arrive(s, lane)
-            part = jnp.dot(net.tokens_of(xo, lane), wv[0, lane], preferred_element_type=F32)
-            if lane == 0:
-                z[0] = part
-            else:
-                z[0] += part
-                sib_dot(lane - 1)
-        sib_dot(nd - 1)
+            logits_part(s, lane)
+        z_copy(s).start()
+        scatter(s + 1)
         logits_grad(s)
+        copies = dz_copies()
+        for copy in copies:
+            copy.start()
         for lane in range(nd):
-            acc[lane] += jnp.dot(dzt[...], net.tokens_of(xo, lane), preferred_element_type=F32)
-            net.release_own(s, lane)
+            acc[lane, 0:vocab, :] += jnp.dot(dzt[0:vocab, :], net.tokens(s, lane), preferred_element_type=F32)
+        for copy in copies:
+            copy.wait()
         for lane in range(nd):
-            acc[nd + lane] += jnp.dot(dzt[...], net.tokens_of(xs, lane), preferred_element_type=F32)
-            if lane >= 1:
-                net.forward(s, lane - 1)
-        for lane in range(nd):
-            part = jnp.dot(dz[...], wt[nd + lane], preferred_element_type=F32)
-            for rel in range(geo.chips):
-                at = geo.slot(rel, lane) * slab
-                sibout[lane, at:at + slab, :] = part[rel * slab:(rel + 1) * slab, :].astype(BF16)
-            sib_dh(lane).start()
-            if lane == 0:
-                net.forward(s, nd - 1)
+            acc[lane, vocab:, :] += jnp.dot(dzt[vocab:, :], net.tokens(s, lane), preferred_element_type=F32)
+        ring = lax.rem(s, 3)
         for lane in range(nd):
             part = jnp.dot(dz[...], wt[lane], preferred_element_type=F32)
             for rel in range(geo.chips):
                 at = geo.slot(rel, lane) * slab
-                dho[lane, at:at + slab, :] = part[rel * slab:(rel + 1) * slab, :]
-
-    def wout(k):
-        plane, lane = lax.div(k, nd), lax.rem(k, nd)
-        half_no = core + plane - 2 * core * plane
-        column = half_no * geo.half + lane * width
+                block = part[rel * slab:(rel + 1) * slab, :].astype(BF16)
+                if at < geo.tokens // 2:
+                    dlo[ring, lane, at:at + slab, :] = block
+                else:
+                    dhi[lane, at - geo.tokens // 2:at - geo.tokens // 2 + slab, :] = block
+            rs_copy(1, lane, s + 1).start()
+            if lane >= 2:
+                net.release(s, 2 * lane - 4)
+                net.release(s, 2 * lane - 3)
+        return carry
+
+    def wout(lane):
         return pltpu.make_async_copy(
-            wv.at[plane, lane], gw_hbm.at[pl.ds(pl.multiple_of(column, width), width), :], wout_sem.at[k])
-
-    def body(s, carry):
+            wv.at[lane, :, pl.ds(0, vocab)],
+            gw_hbm.at[pl.ds(pl.multiple_of(half_at[0] + lane * width, width), width), :], wout_sem.at[lane])
+
+    def wout_cross(lane):
+        return pltpu.make_async_remote_copy(
+            src_ref=wv.at[lane, :, pl.ds(vocab, vocab)],
+            dst_ref=gw_hbm.at[pl.ds(pl.multiple_of(half_at[0] + lane * width, width), width), :],
+            send_sem=wo_send.at[lane], recv_sem=wo_recv.at[lane], device_id=net.sib, device_id_type=MESH)
+
+    def tail_step(s, carry):
         scatter(s)
 
-        @pl.when(s < steps)
-        def _():
-            grad_step(s)
-
-        @pl.when((s >= steps) & (s < steps + 2 * nd))
-        def _():
-            k = s - steps
-            wv[lax.div(k, nd), lax.rem(k, nd)] = acc[k].astype(BF16).T
-            wout(k).start()
+        @pl.when(s <= steps + nd)
+        def _():
+            lane = s - steps - 1
+            for part in range(2):
+                span = slice(part * vocab, (part + 1) * vocab)
+                wv[lane, :, span] = acc[lane, span, :].astype(BF16).T
+            wout(lane).start()
+            wout_cross(lane).start()
         return carry
 
     lax.fori_loop(0, first, loss_step, 0)
-    net.forward(first - 1, nd - 1)
+    for lane in range(2, nd):
+        net.release(first - 1, lane)
     reps(first - 1)
     softmax()
-    lax.fori_loop(first, steps + 9, body, 0)
+    lax.fori_loop(first, steps, grad_step, 0)
+    lax.fori_loop(steps + 1, steps + 9, tail_step, 0)
     out_copy(steps + 8).wait()
-    stores = []
-    for plane in range(2):
-        column = pl.multiple_of((core if plane == 0 else 1 - core) * geo.half, geo.half)
-        stores.append(pltpu.make_async_copy(gout.at[plane], gh_hbm.at[:, :, pl.ds(column, geo.half)],
-                                            hout_sem.at[plane]))
+    stores = [pltpu.make_async_copy(gout.at[half], gh_hbm.at[:, :, pl.ds(half_at[half], geo.half)], hout_sem.at[half])
+              for half in range(2)]
     for copy in stores:
         copy.start()
     for copy in stores:
         copy.wait()
-    for k in range(2 * nd):
-        wout(k).wait()
+    for lane in range(nd):
+        wout(lane).wait()
+        wout_cross(lane).wait()
 
 
 def call_fused(geo, const, q_rows, d_rows, w_head, bias, mrow, positive, place, doc_place, pick):
@@ -572,13 +560,14 @@
     lanes = doc_place.shape[1]
     tile = n_q + 8
     hbm, vmem = pl.BlockSpec(memory_space=pl.ANY), pl.BlockSpec(memory_space=pltpu.VMEM)
+    logit = pltpu.VMEM((2, tok, vocab), F32)
     scratch = bufs + [
-        pltpu.VMEM((2, nd, width, vocab), BF16), pltpu.VMEM((2 * nd, vocab, width), BF16),
-        pltpu.VMEM((2 * nd, vocab, width), F32), pltpu.VMEM((2, tok, vocab), F32), pltpu.VMEM((tok, vocab), BF16),
-        pltpu.VMEM((vocab, tok), BF16), pltpu.VMEM((nd, tok, width), F32), pltpu.VMEM((nd, tok, width), BF16),
-        pltpu.VMEM((nd, tok, width), BF16), pltpu.VMEM((3, nd, tok // 2, width), BF16),
-        pltpu.VMEM((nd, tok // 2, width), BF16), pltpu.VMEM((3, nd, tok // 2, width), BF16),
-        pltpu.VMEM((3, nd, tok // 4, width), BF16), pltpu.VMEM((3, nd, tok // 8, width), BF16),
+        pltpu.VMEM((nd, width, 2 * vocab), BF16), pltpu.VMEM((nd, 2 * vocab, width), BF16),
+        pltpu.VMEM((nd, 2 * vocab, width), F32), logit, logit, logit,
+        pltpu.VMEM((tok, 2 * vocab), BF16), pltpu.VMEM((2 * vocab, tok), BF16),
+        pltpu.VMEM((3, nd, tok // 2, width), BF16), pltpu.VMEM((nd, tok // 2, width), BF16),
+        pltpu.VMEM((3, nd, tok // 2, width), BF16), pltpu.VMEM((3, nd, tok // 4, width), BF16),
+        pltpu.VMEM((3, nd, tok // 8, width), BF16),
         pltpu.VMEM((2, nd, tok // 2, width), BF16), pltpu.VMEM((2, nd, tok // 4, width), BF16),
         pltpu.VMEM((2, nd, tok // 8, width), BF16), pltpu.VMEM((2, nd, tok // 16, width), BF16),
         pltpu.VMEM((2, geo.unit, geo.half), BF16), pltpu.VMEM((2, rows, geo.unit, geo.half), BF16),
@@ -587,8 +576,9 @@
         pltpu.VMEM((slots,) + mrow.shape, F32), pltpu.VMEM((mrow.shape[1] // geo.unit, geo.unit, 128), F32),
         pltpu.VMEM((slots, n_q, lanes), F32), pltpu.VMEM((slots, n_q, lanes), F32),
         pltpu.VMEM((tile, lanes), F32), pltpu.VMEM((slots, tile, lanes), F32),
-        dma((4,)), dma((2, nd)), dma((nd,)), dma((nd,)), dma((4, nd)), dma((4, nd, 2)), dma((2,)), dma((2,)),
-        dma((2 * nd,)), dma((2,)), dma((3, slots)), dma((3, slots))] + sems
+        dma((4,)), dma((nd,)), dma((nd,)), dma((nd,)), dma((2,)), dma((2,)), dma((2,)), dma((2,)),
+        dma((4, nd)), dma((4, nd, 2)), dma((2,)), dma((2,)), dma((nd,)), dma((nd,)), dma((nd,)), dma((2,)),
+        dma((3, slots)), dma((3, slots))] + sems
     return pl.pallas_call(
         functools.partial(fused_kernel, geo, const),
         name="lexical_head",

time: 666 us -> 579 us (0.87)
  Pallas kernels: 644 us -> 558 us
    pallas_call x1, Pallas kernels: 644 us -> 558 us  [call_fused(): pl.pallas_call(functools.partial(fused_kernel, geo, const), name='lexical...]
where the time goes in v3:
time: 579 us
  Pallas kernels  558 us (96%)
  local copies, waits for them, and re-layouts  15.5 us (3%)
    pallas_call x1, Pallas kernels, call_fused(): pl.pallas_call(functools.partial(fused_kernel, geo, const), name='lexical...  558 us

profile of v3, /device:TPU:97, one launch (start us, length us, event | category | flops | bytes accessed | tf_op | source)
XLA Modules:
  0.0 578.5 jit_solution(3488586691525854946)
XLA Ops:
  0.7 0.1 add.104
  0.8 0.8 reshape.162
  1.5 0.8 copy.15
  2.3 0.1 reshape.161
  2.4 0.6 pad.4
  3.0 1.3 copy.16.pos_ref
  4.3 0.7 fusion.1.place
  5.0 0.7 fusion.doc_place
  5.7 557.8 %lexical_head.1 = (f32[1,128]{1,0:T(1,128)}, bf16[4096,1024]{1,0:T(8,128)(2,1)}, f32[8,1024]{1,0:T(8,128)}, bf16[24,8,4096]{2,1,0:T(8,128)(2,1)}) custom-call(bf16[16,8,4096]{2,1,0:T(8,128)(2,1)} %q_hbm.1, bf16[8,8,4096]{2,1,0:T(8,128)(2,1)} %bitcast.7, bf16[4096,1024]{1,0:T(8,128)(2,1)} %w_hbm.1, f32[1,1024]{1,0:T(1,128)} %bitcast.9, f32[1,256]{1,0:T(1,128)} %bitcast.10, ...), custom_call_target="tpu_custom_call" | custom-call | tf_op jit(solution)/shard_map/lexical_head/pallas_call | solution.py:582
  563.4 1.4 reduce_sum.9
  564.8 1.9 slice.11
  566.7 2.3 slice.10
  569.7 7.8 %copy.20 = bf16[4096,1024]{1,0:T(8,128)(2,1)} copy(bf16[4096,1024]{1,0:T(8,128)(2,1)} %get-tuple-element.21) | data formatting | bytes 16777216
  (3 shorter events, 0.0 us)

commit v4 on v3

--- a/solution.py
+++ b/solution.py
@@ -68,7 +68,17 @@
         self.geo, self.x, self.stage, self.ownx = geo, x, stage, ownx
         self.core = lax.rem(me, 2)
         self.sib = {"tp": me + 1 - 2 * self.core}
-        self.same = [geo.peer(me, dim, self.core) for dim in range(geo.nd)]
+        dims = [geo.peer(me, dim, self.core)["tp"] for dim in range(geo.nd)]
+        turn = geo.nd // 2
+        self.same = [{"tp": dims[d] + self.core * (dims[(d + turn) % geo.nd] - dims[d])} for d in range(geo.nd)]
+
+    def place(self, rel, lane):
+        geo = self.geo
+        one = geo.slot(rel, lane) * geo.slab
+        two = geo.slot(rel, (lane + geo.nd // 2) % geo.nd) * geo.slab
+        if one == two:
+            return pl.ds(one, geo.slab)
+        return pl.ds(pl.multiple_of(one + self.core * (two - one), geo.slab), geo.slab)
 
     def ici(self, s, lane, pos):
         count = (1 << pos) * self.geo.slab
@@ -85,7 +95,7 @@
             dst_ref=self.stage.at[parity, lane], send_sem=self.piece_send.at[lane, parity],
             recv_sem=self.piece_recv.at[lane, parity], device_id=self.sib, device_id_type=MESH)
 
-    def arrive(self, s, lane):
+    def inject(self, s, lane):
         geo = self.geo
         width, parity = geo.width, lax.rem(s, 2)
         self.piece(s, lane).wait()
@@ -95,44 +105,87 @@
         second = jnp.where(self.core == 0, theirs, mine)
         self.x[parity, lane, 0:geo.slab, :] = jnp.concatenate([first, second], axis=0).astype(BF16)
 
-        @pl.when(s > 0)
-        def _():
+    def begin(self):
+        geo = self.geo
+
+        def first(lane, pos):
+            return pltpu.make_async_remote_copy(
+                src_ref=self.x.at[0, lane, pl.ds(0, geo.slab)],
+                dst_ref=self.x.at[1, lane, pl.ds((1 << pos) * geo.slab, geo.slab)],
+                send_sem=self.ici_send.at[lane, pos, 1], recv_sem=self.ici_recv.at[lane, pos, 1],
+                device_id=self.same[(lane + pos) % geo.nd], device_id_type=MESH)
+
+        for lane in range(geo.nd):
+            self.inject(0, lane)
+            for pos in range(geo.nd):
+                first(lane, pos).start()
+            self.piece(1, lane).start()
+        for lane in range(geo.nd):
+            for pos in range(geo.nd):
+                first(lane, pos).wait_send()
+            self.grant(lane)
+        for lane in range(geo.nd):
+            for pos in range(geo.nd):
+                first(lane, pos).wait_recv()
+
+    def arrive(self, s, lane, loss):
+        geo = self.geo
+        self.inject(s, lane)
+
+        def receive():
             for pos in range(geo.nd):
                 self.ici(s - 1, lane, pos).wait_recv()
 
-        @pl.when((s > 0) & (s < geo.steps - 1))
-        def _():
+        def send():
             pl.semaphore_wait(self.free_piece.at[lane], 1)
             for pos in range(geo.nd):
                 pl.semaphore_wait(self.free_ici.at[lane, pos], 1)
-
-        @pl.when(s < geo.steps - 1)
-        def _():
             for pos in reversed(range(geo.nd)):
                 self.ici(s, lane, pos).start()
             self.piece(s + 1, lane).start()
 
-    def release(self, s, lane):
+        if loss:
+            @pl.when(s > 1)
+            def _():
+                receive()
+
+            send()
+        else:
+            receive()
+
+            @pl.when(s < geo.steps - 1)
+            def _():
+                send()
+
+    def grant(self, lane):
         geo = self.geo
-
-        @pl.when(s < geo.steps - 1)
-        def _():
+        for pos in range(geo.nd):
+            pl.semaphore_signal(self.free_ici.at[lane, pos], inc=1,
+                                device_id=self.same[(lane + pos) % geo.nd], device_id_type=MESH)
+        pl.semaphore_signal(self.free_piece.at[lane], inc=1, device_id=self.sib, device_id_type=MESH)
+
+    def release(self, s, lane, loss):
+        geo = self.geo
+
+        def sent():
             for pos in range(geo.nd):
                 self.ici(s, lane, pos).wait_send()
 
-        @pl.when(s < geo.steps - 2)
-        def _():
-            for pos in range(geo.nd):
-                pl.semaphore_signal(self.free_ici.at[lane, pos], inc=1,
-                                    device_id=self.same[(lane + pos) % geo.nd], device_id_type=MESH)
-            pl.semaphore_signal(self.free_piece.at[lane], inc=1, device_id=self.sib, device_id_type=MESH)
+        if loss:
+            sent()
+            self.grant(lane)
+        else:
+            @pl.when(s < geo.steps - 1)
+            def _():
+                sent()
+
+            @pl.when(s < geo.steps - 2)
+            def _():
+                self.grant(lane)
 
     def tokens(self, s, lane):
         geo, parity = self.geo, lax.rem(s, 2)
-        if lane == 0:
-            return self.x[parity, lane]
-        places = [geo.slot(rel, lane) * geo.slab for rel in range(geo.chips)]
-        return jnp.concatenate([self.x[parity, lane, at:at + geo.slab, :] for at in places], axis=0)
+        return jnp.concatenate([self.x[parity, lane, self.place(rel, lane), :] for rel in range(geo.chips)], axis=0)
 
 
 def gather_scratch(geo):
@@ -155,7 +208,7 @@
 
 def fused_kernel(geo, const, q_hbm, d_hbm, w_hbm, bias, mrow, pos_ref, place, doc_place, pick,
                  loss_ref, gw_hbm, gb, gh_hbm,
-                 x, stage, ownx, wv, wt, acc, zo, zs, zr, dz, dzt, dlo, dhi, m1, m2, m3,
+                 x, stage, ownx, wv, wt, acc, zo, zs, zr, dz, dzt, dsum, m1, m2, m3,
                  r1, r2, r3, r4, ost, gout, early, rep, rd, drd, mall, mt, sbuf, pall, gmine, gall,
                  own_sem, w_sem, wx_send, wx_recv, z_send, z_recv, dz_send, dz_recv, rs_send, rs_recv,
                  out_send, out_recv, wout_sem, wo_send, wo_recv, hout_sem, ex_send, ex_recv, *sems):
@@ -213,27 +266,28 @@
     gb[...] = jnp.zeros_like(gb)
     for copy in w_cross:
         copy.start()
-    for ref in (dlo, m1, m2, m3):
+    for ref in (dsum, m1, m2, m3):
         ref[...] = jnp.zeros_like(ref)
 
-    def z_copy(s):
-        parity = lax.rem(s, 2)
+    part = vocab // 2
+
+    def z_copy(s, half):
+        parity, cols = lax.rem(s, 2), pl.ds(half * part, part)
         return pltpu.make_async_remote_copy(
-            src_ref=zs.at[parity], dst_ref=zr.at[parity], send_sem=z_send.at[parity], recv_sem=z_recv.at[parity],
+            src_ref=zs.at[parity, :, cols], dst_ref=zr.at[parity, :, cols], send_sem=z_send.at[parity, half],
+            recv_sem=z_recv.at[parity, half], device_id=net.sib, device_id_type=MESH)
+
+    def dz_copy(half, turned):
+        here, there = pl.ds(half * part, part), pl.ds(vocab + half * part, part)
+        src, dst = (dzt.at[here], dzt.at[there]) if turned else (dz.at[:, here], dz.at[:, there])
+        return pltpu.make_async_remote_copy(
+            src_ref=src, dst_ref=dst, send_sem=dz_send.at[half, int(turned)], recv_sem=dz_recv.at[half, int(turned)],
             device_id=net.sib, device_id_type=MESH)
-
-    def dz_copies():
-        return [pltpu.make_async_remote_copy(
-            src_ref=dzt.at[pl.ds(0, vocab)], dst_ref=dzt.at[pl.ds(vocab, vocab)], send_sem=dz_send.at[0],
-            recv_sem=dz_recv.at[0], device_id=net.sib, device_id_type=MESH),
-            pltpu.make_async_remote_copy(
-                src_ref=dz.at[:, pl.ds(0, vocab)], dst_ref=dz.at[:, pl.ds(vocab, vocab)], send_sem=dz_send.at[1],
-                recv_sem=dz_recv.at[1], device_id=net.sib, device_id_type=MESH)]
 
     def rs_copy(stage_no, lane, s):
         parity, ring = lax.rem(s, 2), lax.rem(s, 3)
         n_low = geo.tokens >> stage_no
-        src = dhi.at[lane]
+        src = dsum.at[lax.rem(s + 2, 3), lane, pl.ds(n_low, n_low)]
         if stage_no > 1:
             src = (m1, m2, m3)[stage_no - 2].at[ring, lane, pl.ds(n_low, n_low)]
         dst = (r1, r2, r3, r4)[stage_no - 1].at[parity, lane]
@@ -263,7 +317,7 @@
 
             @pl.when((s >= first + 2) & (s <= steps + 2))
             def _():
-                m1[ring, lane] = merge(1, lane, s, steps + 2, dlo[ring, lane]).astype(BF16)
+                m1[ring, lane] = merge(1, lane, s, steps + 2, dsum[ring, lane, 0:low1]).astype(BF16)
 
             @pl.when((s >= first + 3) & (s <= steps + 4))
             def _():
@@ -320,7 +374,8 @@
 
     def reps(s):
         parity = lax.rem(s, 2)
-        z_copy(s).wait()
+        for half in range(2):
+            z_copy(s, half).wait()
         for rel in range(geo.chips):
             span = slice(rel * slab, (rel + 1) * slab)
             logits = zo[parity, span, :] + zr[parity, span, :] + bias[...]
@@ -351,8 +406,8 @@
 
         @pl.when((s >= 2) & (s < 2 + nd))
         def _():
-            def turn(part, carry):
-                span = pl.ds(pl.multiple_of(part * vocab, vocab), vocab)
+            def turn(half, carry):
+                span = pl.ds(pl.multiple_of(half * vocab, vocab), vocab)
                 acc[s - 2, span, :] = jnp.zeros((vocab, width), F32)
                 wt[s - 2, span, :] = wv[s - 2, :, span].T
                 return carry
@@ -362,18 +417,19 @@
     def loss_step(s, carry):
         prepare(s)
         for lane in range(nd):
-            net.arrive(s, lane)
+            if lane == nd - 1:
+                net.release(s, 0, True)
+            else:
+                @pl.when(s > 1)
+                def _():
+                    net.release(s - 1, lane + 1, True)
+
+            net.arrive(s, lane, True)
 
             @pl.when(s >= nd)
             def _():
                 logits_part(s, lane)
 
-            if lane >= 2:
-                net.release(s, lane - 2)
-            else:
-                @pl.when(s > 0)
-                def _():
-                    net.release(s - 1, lane + nd - 2)
             if lane == 1:
                 @pl.when(s > nd)
                 def _():
@@ -381,7 +437,8 @@
 
         @pl.when(s >= nd)
         def _():
-            z_copy(s).start()
+            for half in range(2):
+                z_copy(s, half).start()
         return carry
 
     def softmax():
@@ -456,57 +513,72 @@
         for copy in scores_out + grads_out:
             copy.wait_send()
 
-    def logits_grad(s):
+    def logit_sum(s, at):
+        total = jnp.dot(net.tokens(s, 0), wv[0, :, at:at + part], preferred_element_type=F32)
+        for lane in range(1, nd):
+            total += jnp.dot(net.tokens(s, lane), wv[lane, :, at:at + part], preferred_element_type=F32)
+        return total
+
+    def logits_grad(s, half):
         parity = lax.rem(s, 2)
-        z_copy(s).wait()
-        total = gb[...]
+        cols = slice(half * part, (half + 1) * part)
+        total = gb[:, cols]
         for rel in range(geo.chips):
             span = slice(rel * slab, (rel + 1) * slab)
-            logits = zo[parity, span, :] + zr[parity, span, :] + bias[...]
+            logits = zo[parity, span, cols] + zr[parity, span, cols] + bias[:, cols]
             inverse = 1.0 / (1.0 + logits)
             row = lax.rem(s - geo.hops(rel), rows)
             parts = []
             for cr in range(2):
                 at = 2 * rel + cr
-                part = slice(cr * unit, (cr + 1) * unit)
-                grad_row = rep[at, pl.ds(row, 1), :] * inverse[part, :]
-                grad_row = jnp.where(logits[part, :] > 0.0, grad_row, 0.0) * mt[row, :, at:at + 1]
+                tok = slice(cr * unit, (cr + 1) * unit)
+                grad_row = rep[at, pl.ds(row, 1), cols] * inverse[tok, :]
+                grad_row = jnp.where(logits[tok, :] > 0.0, grad_row, 0.0) * mt[row, :, at:at + 1]
                 total = total + grad_row
                 parts.append(grad_row)
-            dz[span, 0:vocab] = jnp.concatenate(parts, axis=0).astype(BF16)
-        gb[...] = total
-        dzt[0:vocab, :] = dz[:, 0:vocab].T
+            dz[span, cols] = jnp.concatenate(parts, axis=0).astype(BF16)
+        gb[:, cols] = total
+        dzt[cols, :] = dz[:, cols].T
+
+    def accumulate(s, at, count):
+        for lane in range(nd):
+            acc[lane, at:at + count, :] += jnp.dot(dzt[at:at + count, :], net.tokens(s, lane),
+                                                   preferred_element_type=F32)
 
     def grad_step(s, carry):
+        parity = lax.rem(s, 2)
         for lane in range(nd):
-            net.arrive(s, lane)
-            logits_part(s, lane)
-        z_copy(s).start()
+            net.arrive(s, lane, False)
+        for half in range(2):
+            zs[parity, :, half * part:(half + 1) * part] = logit_sum(s, vocab + half * part)
+            z_copy(s, half).start()
+        zo[parity, :, 0:part] = logit_sum(s, 0)
+        z_copy(s, 0).wait()
+        logits_grad(s, 0)
+        zo[parity, :, part:vocab] = logit_sum(s, part)
+        dz_copy(0, True).start()
+        dz_copy(0, False).start()
+        z_copy(s, 1).wait()
+        logits_grad(s, 1)
+        accumulate(s, 0, part)
+        dz_copy(1, True).start()
+        dz_copy(1, False).start()
         scatter(s + 1)
-        logits_grad(s)
-        copies = dz_copies()
-        for copy in copies:
-            copy.start()
-        for lane in range(nd):
-            acc[lane, 0:vocab, :] += jnp.dot(dzt[0:vocab, :], net.tokens(s, lane), preferred_element_type=F32)
-        for copy in copies:
-            copy.wait()
-        for lane in range(nd):
-            acc[lane, vocab:, :] += jnp.dot(dzt[vocab:, :], net.tokens(s, lane), preferred_element_type=F32)
+        accumulate(s, part, part)
+        for half in range(2):
+            dz_copy(half, True).wait()
+        accumulate(s, vocab, vocab)
+        for half in range(2):
+            dz_copy(half, False).wait()
         ring = lax.rem(s, 3)
         for lane in range(nd):
-            part = jnp.dot(dz[...], wt[lane], preferred_element_type=F32)
+            block = jnp.dot(dz[...], wt[lane], preferred_element_type=F32).astype(BF16)
             for rel in range(geo.chips):
-                at = geo.slot(rel, lane) * slab
-                block = part[rel * slab:(rel + 1) * slab, :].astype(BF16)
-                if at < geo.tokens // 2:
-                    dlo[ring, lane, at:at + slab, :] = block
-                else:
-                    dhi[lane, at - geo.tokens // 2:at - geo.tokens // 2 + slab, :] = block
+                dsum[ring, lane, net.place(rel, lane), :] = block[rel * slab:(rel + 1) * slab, :]
             rs_copy(1, lane, s + 1).start()
             if lane >= 2:
-                net.release(s, 2 * lane - 4)
-                net.release(s, 2 * lane - 3)
+                net.release(s, 2 * lane - 4, False)
+                net.release(s, 2 * lane - 3, False)
         return carry
 
     def wout(lane):
@@ -526,16 +598,17 @@
         @pl.when(s <= steps + nd)
         def _():
             lane = s - steps - 1
-            for part in range(2):
-                span = slice(part * vocab, (part + 1) * vocab)
+            for half in range(2):
+                span = slice(half * vocab, (half + 1) * vocab)
                 wv[lane, :, span] = acc[lane, span, :].astype(BF16).T
             wout(lane).start()
             wout_cross(lane).start()
         return carry
 
-    lax.fori_loop(0, first, loss_step, 0)
-    for lane in range(2, nd):
-        net.release(first - 1, lane)
+    net.begin()
+    lax.fori_loop(1, first, loss_step, 0)
+    for lane in range(1, nd):
+        net.release(first - 1, lane, True)
     reps(first - 1)
     softmax()
     lax.fori_loop(first, steps, grad_step, 0)
@@ -565,7 +638,7 @@
         pltpu.VMEM((nd, width, 2 * vocab), BF16), pltpu.VMEM((nd, 2 * vocab, width), BF16),
         pltpu.VMEM((nd, 2 * vocab, width), F32), logit, logit, logit,
         pltpu.VMEM((tok, 2 * vocab), BF16), pltpu.VMEM((2 * vocab, tok), BF16),
-        pltpu.VMEM((3, nd, tok // 2, width), BF16), pltpu.VMEM((nd, tok // 2, width), BF16),
+        pltpu.VMEM((3, nd, tok, width), BF16),
         pltpu.VMEM((3, nd, tok // 2, width), BF16), pltpu.VMEM((3, nd, tok // 4, width), BF16),
         pltpu.VMEM((3, nd, tok // 8, width), BF16),
         pltpu.VMEM((2, nd, tok // 2, width), BF16), pltpu.VMEM((2, nd, tok // 4, width), BF16),
@@ -576,7 +649,7 @@
         pltpu.VMEM((slots,) + mrow.shape, F32), pltpu.VMEM((mrow.shape[1] // geo.unit, geo.unit, 128), F32),
         pltpu.VMEM((slots, n_q, lanes), F32), pltpu.VMEM((slots, n_q, lanes), F32),
         pltpu.VMEM((tile, lanes), F32), pltpu.VMEM((slots, tile, lanes), F32),
-        dma((4,)), dma((nd,)), dma((nd,)), dma((nd,)), dma((2,)), dma((2,)), dma((2,)), dma((2,)),
+        dma((4,)), dma((nd,)), dma((nd,)), dma((nd,)), dma((2, 2)), dma((2, 2)), dma((2, 2)), dma((2, 2)),
         dma((4, nd)), dma((4, nd, 2)), dma((2,)), dma((2,)), dma((nd,)), dma((nd,)), dma((nd,)), dma((2,)),
         dma((3, slots)), dma((3, slots))] + sems
     return pl.pallas_call(

time: 579 us -> 525 us (0.907)
  Pallas kernels: 558 us -> 503 us
    pallas_call x1, Pallas kernels: 558 us -> 503 us  [call_fused(): pl.pallas_call(functools.partial(fused_kernel, geo, const), name='lexical...]
where the time goes in v4:
time: 525 us; the launch traced here: 524 us
  Pallas kernels  503 us (96%)
  local copies, waits for them, and re-layouts  15.5 us (3%)
    pallas_call x1, Pallas kernels, call_fused(): pl.pallas_call(functools.partial(fused_kernel, geo, const), name='lexical...  503 us

profile of v4, /device:TPU:97, one launch (start us, length us, event | category | flops | bytes accessed | tf_op | source)
XLA Modules:
  0.0 524.1 jit_solution(5891559536310220132)
XLA Ops:
  0.7 0.1 add.104
  0.8 0.8 reshape.162
  1.5 0.8 copy.15
  2.3 0.1 reshape.161
  2.4 0.6 pad.4
  3.0 1.3 copy.16.pos_ref
  4.3 0.7 fusion.1.place
  5.0 0.7 fusion.doc_place
  5.7 503.3 %lexical_head.1 = (f32[1,128]{1,0:T(1,128)}, bf16[4096,1024]{1,0:T(8,128)(2,1)}, f32[8,1024]{1,0:T(8,128)}, bf16[24,8,4096]{2,1,0:T(8,128)(2,1)}) custom-call(bf16[16,8,4096]{2,1,0:T(8,128)(2,1)} %q_hbm.1, bf16[8,8,4096]{2,1,0:T(8,128)(2,1)} %bitcast.7, bf16[4096,1024]{1,0:T(8,128)(2,1)} %w_hbm.1, f32[1,1024]{1,0:T(1,128)} %bitcast.9, f32[1,256]{1,0:T(1,128)} %bitcast.10, ...), custom_call_target="tpu_custom_call" | custom-call | tf_op jit(solution)/shard_map/lexical_head/pallas_call | solution.py:655
  509.0 1.4 reduce_sum.9
  510.4 1.9 slice.11
  512.2 2.3 slice.10
  515.2 7.8 %copy.20 = bf16[4096,1024]{1,0:T(8,128)(2,1)} copy(bf16[4096,1024]{1,0:T(8,128)(2,1)} %get-tuple-element.21) | data formatting | bytes 16777216
  (3 shorter events, 0.0 us)

commit v5 on v4

v5 whole, which is shorter than its diff:
```python
import functools
import math

import jax
import jax.numpy as jnp
import numpy as np
from jax import lax
from jax.experimental import pallas as pl
from jax.experimental.pallas import tpu as pltpu
from jax.sharding import PartitionSpec as P

MESH = pl.DeviceIdType.MESH
F32 = jnp.float32
BF16 = jnp.bfloat16
VMEM_LIMIT = 67043328
PAIR = range(2)
HIGHEST = lax.Precision.HIGHEST


def parity(s):
    return lax.rem(s, 2)


def ring(s):
    return lax.rem(s, 3)


def sum_rows(x):
    return jnp.sum(x, axis=0, keepdims=True)


def sum_lanes(x):
    return jnp.sum(x, axis=1, keepdims=True)


def exact_dot(a, b, dims=(((1,), (0,)), ((), ()))):
    return lax.dot_general(a, b, dims, precision=HIGHEST, preferred_element_type=F32)


TURNED = (((1,), (1,)), ((), ()))
FIRST = (((0,), (0,)), ((), ()))


class Geometry:
    def __init__(self, n_group, rows, hidden, vocab, unit):
        self.side = math.isqrt(n_group // 2)
        self.nd = 2 * (self.side.bit_length() - 1)
        self.chips = 1 << self.nd
        assert self.side == 4 and self.chips * 2 == n_group
        self.rows = rows
        self.first = self.nd + rows
        self.steps = self.first + rows
        self.unit = unit
        self.slab = 2 * unit
        self.tokens = self.slab * self.chips
        self.half = hidden // 2
        self.width = self.half // self.nd
        self.vocab = vocab

    def hops(self, rel):
        return bin(rel).count("1")

    def slot(self, rel, lane):
        return ((rel >> lane) | (rel << (self.nd - lane))) & (self.chips - 1)

    def device(self, me, rel, core):
        chip = lax.div(me, 2)
        x, y = lax.rem(chip, self.side), lax.div(chip, self.side)
        at = [x, y]
        for dim in range(self.nd):
            if rel >> dim & 1:
                axis, wide = divmod(dim, len(at))
                at[axis] = self.side - 1 - at[axis] if wide else at[axis] + 1 - 2 * lax.rem(at[axis], 2)
        x, y = at
        return {"tp": (y * self.side + x) * 2 + core}

    def peer(self, me, dim, core):
        return self.device(me, 1 << dim, core)


def entry_barrier(peers):
    barrier = pltpu.get_barrier_semaphore()
    for device in peers:
        pl.semaphore_signal(barrier, inc=1, device_id=device, device_id_type=MESH)
    pl.semaphore_wait(barrier, len(peers))


class Gather:
    def __init__(self, geo, me, x, stage, ownx, sems):
        (self.ici_send, self.ici_recv, self.piece_send, self.piece_recv, self.free_ici, self.free_piece) = sems
        self.geo, self.x, self.stage, self.ownx = geo, x, stage, ownx
        self.core = lax.rem(me, 2)
        self.sib = {"tp": me + 1 - 2 * self.core}
        dims = [geo.peer(me, dim, self.core)["tp"] for dim in range(geo.nd)]
        turn = geo.nd // 2
        self.same = [{"tp": dims[d] + self.core * (dims[(d + turn) % geo.nd] - dims[d])} for d in range(geo.nd)]

    def place(self, rel, lane):
        geo = self.geo
        one = geo.slot(rel, lane) * geo.slab
        two = geo.slot(rel, (lane + geo.nd // 2) % geo.nd) * geo.slab
        if one == two:
            return pl.ds(one, geo.slab)
        return pl.ds(pl.multiple_of(one + self.core * (two - one), geo.slab), geo.slab)

    def ici(self, s, lane, pos):
        count = (1 << pos) * self.geo.slab
        here, there = parity(s), parity(s + 1)
        return pltpu.make_async_remote_copy(
            src_ref=self.x.at[here, lane, pl.ds(0, count)], dst_ref=self.x.at[there, lane, pl.ds(count, count)],
            send_sem=self.ici_send.at[lane, pos, there], recv_sem=self.ici_recv.at[lane, pos, there],
            device_id=self.same[(lane + pos) % self.geo.nd], device_id_type=MESH)

    def piece(self, s, lane):
        width = self.geo.width
        return pltpu.make_async_remote_copy(
            src_ref=self.ownx.at[1, lax.rem(s, self.geo.rows), :, pl.ds(lane * width, width)],
            dst_ref=self.stage.at[parity(s), lane], send_sem=self.piece_send.at[lane, parity(s)],
            recv_sem=self.piece_recv.at[lane, parity(s)], device_id=self.sib, device_id_type=MESH)

    def inject(self, s, lane):
        geo = self.geo
        width = geo.width
        self.piece(s, lane).wait()
        mine = self.ownx[0, lax.rem(s, geo.rows), :, lane * width:(lane + 1) * width].astype(F32)
        theirs = self.stage[parity(s), lane].astype(F32)
        first = jnp.where(self.core == 0, mine, theirs)
        second = jnp.where(self.core == 0, theirs, mine)
        self.x[parity(s), lane, :geo.slab, :] = jnp.concatenate([first, second], axis=0).astype(BF16)

    def begin(self):
        geo = self.geo
        for lane in range(geo.nd):
            self.inject(0, lane)
            for pos in range(geo.nd):
                self.first(lane, pos).start()
            self.piece(1, lane).start()

    def begun(self):
        geo = self.geo
        for lane in range(geo.nd):
            for pos in range(geo.nd):
                self.first(lane, pos).wait_send()
            self.grant(lane)
        for lane in range(geo.nd):
            for pos in range(geo.nd):
                self.first(lane, pos).wait_recv()

    def first(self, lane, pos):
        geo = self.geo
        return pltpu.make_async_remote_copy(
            src_ref=self.x.at[0, lane, pl.ds(0, geo.slab)],
            dst_ref=self.x.at[1, lane, pl.ds((1 << pos) * geo.slab, geo.slab)],
            send_sem=self.ici_send.at[lane, pos, 1], recv_sem=self.ici_recv.at[lane, pos, 1],
            device_id=self.same[(lane + pos) % geo.nd], device_id_type=MESH)

    def arrive(self, s, lane, loss):
        geo = self.geo
        self.inject(s, lane)

        def receive():
            for pos in range(geo.nd):
                self.ici(s - 1, lane, pos).wait_recv()

        def credits():
            pl.semaphore_wait(self.free_piece.at[lane], 1)
            for pos in range(geo.nd):
                pl.semaphore_wait(self.free_ici.at[lane, pos], 1)

        def send():
            for pos in reversed(range(geo.nd)):
                self.ici(s, lane, pos).start()
            self.piece(s + 1, lane).start()

        if loss:
            @pl.when(s > 1)
            def _():
                receive()

            credits()
            send()
        else:
            receive()
            credits()

            @pl.when(s < geo.steps - 1)
            def _():
                send()

    def grant(self, lane):
        geo = self.geo
        for pos in range(geo.nd):
            pl.semaphore_signal(self.free_ici.at[lane, pos], inc=1,
                                device_id=self.same[(lane + pos) % geo.nd], device_id_type=MESH)
        pl.semaphore_signal(self.free_piece.at[lane], inc=1, device_id=self.sib, device_id_type=MESH)

    def release(self, s, lane, loss):
        geo = self.geo

        def sent():
            for pos in range(geo.nd):
                self.ici(s, lane, pos).wait_send()

        if loss:
            sent()
            self.grant(lane)
        else:
            @pl.when(s < geo.steps - 1)
            def _():
                sent()
                self.grant(lane)

    def tokens(self, s, lane):
        geo = self.geo
        return jnp.concatenate([self.x[parity(s), lane, self.place(rel, lane), :] for rel in range(geo.chips)], axis=0)


def gather_scratch(geo):
    nd = geo.nd
    bufs = [pltpu.VMEM((2, nd, geo.tokens, geo.width), BF16), pltpu.VMEM((2, nd, geo.unit, geo.width), BF16),
            pltpu.VMEM((2, geo.rows, geo.unit, geo.half), BF16)]
    dma, reg = pltpu.SemaphoreType.DMA, pltpu.SemaphoreType.REGULAR
    sems = [dma((nd, nd, 2)), dma((nd, nd, 2)), dma((nd, 2)), dma((nd, 2)), reg((nd, nd)), reg((nd,))]
    return bufs, sems


def all_peers(geo, me):
    core = lax.rem(me, 2)
    found = [(0, 1 - core, geo.device(me, 0, 1 - core))]
    for rel in range(1, geo.chips):
        for other in PAIR:
            found.append((rel, other, geo.device(me, rel, other)))
    return found


def fused_kernel(geo, const, q_hbm, d_hbm, w_hbm, bias, mrow, pos_ref, place, doc_place, pick,
                 loss_ref, gw_hbm, gb_ref, gq_hbm, gd_hbm,
                 x, stage, ownx, wv, wt, acc, zo, zs, zr, dz, dzt, dsum, m1, m2, m3,
                 r1, r2, r3, r4, x2, x3, x4, ost, gout, early, last, gb, rep, rd, drd, mall, mt, sbuf, pall, gmine, gall,
                 lmine, lall,
                 own_sem, w_sem, wx_send, wx_recv, z_send, z_recv, dz_send, dz_recv, rs_send, rs_recv, fl_send, fl_recv,
                 out_send, out_recv, wout_sem, wo_send, wo_recv, hout_sem, ex_send, ex_recv, *sems):
    nd, slab, unit, width, steps, rows, first = (geo.nd, geo.slab, geo.unit, geo.width, geo.steps, geo.rows,
                                                 geo.first)
    n_q, n_d, lam_q, lam_d, tau, q_batch, d_batch = const
    slots, vocab = 2 * geo.chips, geo.vocab
    me = lax.axis_index("tp")
    net = Gather(geo, me, x, stage, ownx, sems)
    core, same = net.core, net.same
    peers = all_peers(geo, me)
    half_at = [pl.multiple_of(core * geo.half, geo.half), pl.multiple_of((1 - core) * geo.half, geo.half)]

    n_dp = d_hbm.shape[0]
    own_loads = []
    for half in PAIR:
        cols = pl.ds(half_at[half], geo.half)
        own_loads.append(pltpu.make_async_copy(q_hbm.at[:, :, cols], ownx.at[half, pl.ds(0, n_q)],
                                               own_sem.at[2 * half]))
        own_loads.append(pltpu.make_async_copy(d_hbm.at[:, :, cols], ownx.at[half, pl.ds(n_q, n_dp)],
                                               own_sem.at[2 * half + 1]))
    w_loads, w_cross = [], []
    for lane in range(nd):
        here = pl.ds(pl.multiple_of(half_at[0] + lane * width, width), width)
        there = pl.ds(pl.multiple_of(half_at[1] + lane * width, width), width)
        w_loads.append(pltpu.make_async_copy(w_hbm.at[here, :], wv.at[lane, :, pl.ds(0, vocab)], w_sem.at[lane]))
        w_cross.append(pltpu.make_async_remote_copy(
            src_ref=w_hbm.at[there, :], dst_ref=wv.at[lane, :, pl.ds(vocab, vocab)], send_sem=wx_send.at[lane],
            recv_sem=wx_recv.at[lane], device_id=net.sib, device_id_type=MESH))
    for copy in own_loads + w_loads:
        copy.start()
    entry_barrier([device for _, _, device in peers])
    for copy in own_loads:
        copy.wait()
    for lane in range(nd):
        net.piece(0, lane).start()
    net.begin()

    def broadcast(kind, src_of, dst):
        return [pltpu.make_async_remote_copy(
            src_ref=src_of(2 * rel + other), dst_ref=dst.at[2 * rel + core],
            send_sem=ex_send.at[kind, i], recv_sem=ex_recv.at[kind, 2 * rel + core], device_id=device,
            device_id_type=MESH) for i, (rel, other, device) in enumerate(peers)]

    def arrivals(kind, dst):
        return [pltpu.make_async_remote_copy(
            src_ref=dst.at[2 * rel + other], dst_ref=dst.at[2 * rel + other],
            send_sem=ex_send.at[kind, i], recv_sem=ex_recv.at[kind, 2 * rel + other], device_id=device,
            device_id_type=MESH) for i, (rel, other, device) in enumerate(peers)]

    masks_out = broadcast(0, lambda slot: mrow, mall)
    for copy in masks_out:
        copy.start()
    mall[core] = mrow[...]
    for copy in w_cross:
        copy.start()
    gb[...] = jnp.zeros_like(gb)
    for ref in (dsum, m1, m2, m3, dz):
        ref[...] = jnp.zeros_like(ref)

    part = vocab // 2

    def z_copy(s, half):
        cols = pl.ds(half * part, part)
        return pltpu.make_async_remote_copy(
            src_ref=zs.at[parity(s), :, cols], dst_ref=zr.at[parity(s), :, cols], send_sem=z_send.at[parity(s), half],
            recv_sem=z_recv.at[parity(s), half], device_id=net.sib, device_id_type=MESH)

    def dz_copy(s, half, turned):
        here, there = pl.ds(half * part, part), pl.ds(vocab + half * part, part)
        src, dst = dzt.at[here], dzt.at[there]
        if not turned:
            src, dst = dz.at[parity(s), :, here], dz.at[parity(s), :, there]
        return pltpu.make_async_remote_copy(
            src_ref=src, dst_ref=dst, send_sem=dz_send.at[half, int(turned)], recv_sem=dz_recv.at[half, int(turned)],
            device_id=net.sib, device_id_type=MESH)

    def rs_copy(stage_no, lane, s):
        n_low = geo.tokens >> stage_no
        src = dsum.at[ring(s + 2), lane, pl.ds(n_low, n_low)]
        if stage_no > 1:
            src = (m1, m2, m3)[stage_no - 2].at[ring(s), lane, pl.ds(n_low, n_low)]
        dst = (r1, r2, r3, r4)[stage_no - 1].at[parity(s), lane]
        return pltpu.make_async_remote_copy(
            src_ref=src, dst_ref=dst, send_sem=rs_send.at[stage_no - 1, lane, parity(s)],
            recv_sem=rs_recv.at[stage_no - 1, lane, parity(s)],
            device_id=same[(lane + nd - stage_no) % nd], device_id_type=MESH)

    low = [geo.tokens >> k for k in range(5)]
    deep = (low[2] + low[4], low[2] + low[3], low[2] + low[3] + low[4])
    later = (2, 3, 4)
    tail, spare = (steps - 1) % 3, steps % 3

    def flush_copy(i, lane):
        src, dst, stage_no = (
            (dsum.at[tail, lane, pl.ds(low[2], low[2])], x2.at[lane], 2),
            (dsum.at[spare, lane, pl.ds(low[3], low[3])], x3.at[0, lane], 3),
            (dsum.at[tail, lane, pl.ds(low[3], low[3])], x3.at[1, lane], 3),
            (dsum.at[spare, lane, pl.ds(deep[0], low[4])], x4.at[0, lane], 4),
            (dsum.at[spare, lane, pl.ds(deep[2], low[4])], x4.at[1, lane], 4),
            (dsum.at[tail, lane, pl.ds(low[4], low[4])], x4.at[2, lane], 4))[i]
        return pltpu.make_async_remote_copy(
            src_ref=src, dst_ref=dst, send_sem=fl_send.at[i, lane], recv_sem=fl_recv.at[i, lane],
            device_id=same[(lane + nd - stage_no) % nd], device_id_type=MESH)

    def out_copy(s, at):
        return pltpu.make_async_remote_copy(
            src_ref=ost.at[at], dst_ref=gout.at[1, lax.rem(s - 9, rows)], send_sem=out_send.at[at],
            recv_sem=out_recv.at[at], device_id=net.sib, device_id_type=MESH)

    def emit(lane, s, total, at):
        cols = slice(lane * width, (lane + 1) * width)
        one, two = total[:unit], total[unit:slab]
        gout[0, lax.rem(s - 9, rows), :, cols] = jnp.where(core == 0, one, two).astype(BF16)
        ost[at, :, cols] = jnp.where(core == 0, two, one).astype(BF16)

    def merged(stage_no, lane, s, mine):
        got = (r1, r2, r3, r4)[stage_no - 1][parity(s + 1), lane].astype(F32)
        return got + mine.astype(F32)

    def merge_first(s):
        for lane in range(nd):
            rs_copy(1, lane, s - 1).wait()
        for lane in range(nd):
            m1[ring(s), lane] = merged(1, lane, s, dsum[ring(s), lane, :low[1]]).astype(BF16)

    def merge_rest(s):
        back = ring(s + 1)
        for lane in range(nd):
            for stage_no in later:
                rs_copy(stage_no, lane, s - 1).wait()
        for lane in range(nd):
            m2[ring(s), lane] = merged(2, lane, s, m1[back, lane, :low[2]]).astype(BF16)
            m3[ring(s), lane] = merged(3, lane, s, m2[back, lane, :low[3]]).astype(BF16)
            last[lane] = merged(4, lane, s, m3[back, lane, :low[4]])

    def finish(s):
        @pl.when((s >= first + 5) & (s < first + 9))
        def _():
            early[lax.rem(s - first - 5, nd)] = last[...]

        @pl.when(s >= first + 9)
        def _():
            for lane in range(nd):
                emit(lane, s, last[lane], parity(s))

        @pl.when(s >= first + 10)
        def _():
            out_copy(s - 1, parity(s + 1)).wait()

        @pl.when(s >= first + 9)
        def _():
            out_copy(s, parity(s)).start()

    def start_rest(s):
        for lane in range(nd):
            rs_copy(3, lane, s).start()
            rs_copy(4, lane, s).start()

    def logits_part(s, lane):
        tokens = net.tokens(s, lane)
        for ref, at in ((zs, vocab), (zo, 0)):
            part = jnp.dot(tokens, wv[lane, :, at:at + vocab], preferred_element_type=F32)
            if lane == 0:
                ref[parity(s)] = part
            else:
                ref[parity(s)] = ref[parity(s)] + part

    def reps(s):
        for half in PAIR:
            z_copy(s, half).wait()
        for rel in range(geo.chips):
            span = slice(rel * slab, (rel + 1) * slab)
            logits = zo[parity(s), span, :] + zr[parity(s), span, :] + bias[...]
            active = jnp.log1p(jnp.maximum(logits, 0.0))
            row = lax.rem(s - geo.hops(rel), rows)
            for cr in PAIR:
                at = 2 * rel + cr
                part = active[cr * unit:(cr + 1) * unit, :] * mt[row, :, at:at + 1]
                rep[at, pl.ds(row, 1), :] = sum_rows(part)

    def prepare(s):
        @pl.when(s == 1)
        def _():
            for copy in w_loads:
                copy.wait()
            for copy in arrivals(0, mall):
                copy.wait_recv()
            for copy in masks_out:
                copy.wait_send()
            table = jnp.concatenate([mall[i] for i in range(slots)], axis=0)
            table = jnp.concatenate([table, jnp.zeros((128 - slots, table.shape[1]), F32)], axis=0)
            mt[...] = table.T.reshape(mt.shape)

        @pl.when(s == 2)
        def _():
            for copy in w_cross:
                copy.wait()

        @pl.when((s >= 2) & (s < 2 + nd))
        def _():
            def turn(half, carry):
                span = pl.ds(pl.multiple_of(half * vocab, vocab), vocab)
                acc[s - 2, span, :] = jnp.zeros((vocab, width), F32)
                wt[s - 2, span, :] = wv[s - 2, :, span].T
                return carry

            lax.fori_loop(0, 2, turn, 0)

    def loss_step(s, carry):
        prepare(s)
        for lane in range(nd):
            if lane == nd - 1:
                net.release(s, 0, True)
            else:
                @pl.when(s > 1)
                def _():
                    net.release(s - 1, lane + 1, True)

            net.arrive(s, lane, True)

            @pl.when(s >= nd)
            def _():
                logits_part(s, lane)

            if lane == 1:
                @pl.when(s > nd)
                def _():
                    reps(s - 1)

        @pl.when(s >= nd)
        def _():
            for half in PAIR:
                z_copy(s, half).start()
        return carry

    def softmax():
        chunk = 16
        hq = n_q // 2
        shift = loss_ref.shape[1] // 2
        parts = slots // chunk
        pieces = rep[:, n_q:rows, :].reshape((slots * (rows - n_q), geo.vocab))
        rd[...] = exact_dot(pick[...], pieces)

        def score(c, q_sum):
            at = pl.ds(c * chunk, chunk)
            reps_c = rep[at, :n_q, :].reshape((chunk * n_q, geo.vocab))
            part = exact_dot(reps_c, rd[...], TURNED)
            part = exact_dot(part, doc_place[...])
            part = part.reshape((chunk, n_q, part.shape[1]))
            sbuf[at] = part[:, :hq] + pltpu.roll(part[:, hq:], shift, 2)
            return q_sum + sum_rows(reps_c)

        q_sum = lax.fori_loop(0, parts, score, jnp.zeros((1, geo.vocab), F32))
        scores_out = broadcast(1, lambda slot: sbuf.at[slot], pall)
        for copy in scores_out:
            copy.start()
        pall[core] = sbuf[core]
        q_mean = q_sum / q_batch
        d_mean = sum_rows(rd[...]) / d_batch
        reg = (lam_q * sum_lanes(q_mean * q_mean)
               + lam_d * sum_lanes(d_mean * d_mean))
        for copy in arrivals(1, pall):
            copy.wait_recv()
        total = pall[0]
        for i in range(1, slots):
            total = total + pall[i]
        scores = jnp.concatenate([total, pltpu.roll(total, shift, 1)], axis=0) / tau
        lane_no = lax.broadcasted_iota(jnp.int32, scores.shape, 1)
        target = lane_no == pos_ref[...]
        masked = jnp.where(lane_no < d_batch, scores, -jnp.inf)
        top = jnp.max(masked, axis=1, keepdims=True)
        log_norm = jnp.log(sum_lanes(jnp.exp(masked - top))) + top
        hit = sum_lanes(jnp.where(target, scores, 0.0))
        mine = sum_rows(log_norm - hit) / q_batch + reg
        grad = (jnp.exp(masked - log_norm) - target.astype(F32)) / (q_batch * tau)
        gmine[...] = grad[:hq] + pltpu.roll(grad[hq:], shift, 1)
        lmine[...] = jnp.broadcast_to(mine, lmine.shape)
        grads_out = broadcast(2, lambda slot: gmine, gall)
        for copy in grads_out:
            copy.start()
        losses_out = broadcast(3, lambda slot: lmine, lall)
        for copy in losses_out:
            copy.start()
        gall[core] = gmine[...]
        lall[core] = lmine[...]
        drd[...] = jnp.broadcast_to((2.0 * lam_d / d_batch) * d_mean, drd.shape)
        for copy in arrivals(2, gall):
            copy.wait_recv()

        def back(c, carry):
            at = pl.ds(c * chunk, chunk)
            grad_c = gall[at]
            grad_c = jnp.concatenate([grad_c, pltpu.roll(grad_c, shift, 2)], axis=1).reshape((chunk * n_q, 2 * shift))
            grad_c = exact_dot(grad_c, doc_place[...], TURNED)
            reps_c = rep[at, :n_q, :].reshape((chunk * n_q, geo.vocab))
            drd[...] += exact_dot(grad_c, reps_c, FIRST)
            drq = exact_dot(grad_c, rd[...])
            drq = drq + (2.0 * lam_q / q_batch) * q_mean
            rep[at, :n_q, :] = drq.reshape((chunk, n_q, geo.vocab))
            return carry

        lax.fori_loop(0, parts, back, 0)
        spread = exact_dot(pick[...], drd[...], FIRST)
        rep[:, n_q:rows, :] = spread.reshape((slots, rows - n_q, geo.vocab))
        for copy in arrivals(3, lall):
            copy.wait_recv()
        by_device = jnp.zeros((1, place.shape[1]), F32)
        for i in range(slots):
            by_device = by_device + lall[i] * place[i:i + 1, :]
        loss_ref[...] = jnp.broadcast_to(sum_lanes(by_device), loss_ref.shape)
        for copy in scores_out + grads_out + losses_out:
            copy.wait_send()

    def logit_sum(s, at):
        total = jnp.dot(net.tokens(s, 0), wv[0, :, at:at + part], preferred_element_type=F32)
        for lane in range(1, nd):
            total += jnp.dot(net.tokens(s, lane), wv[lane, :, at:at + part], preferred_element_type=F32)
        return total

    def logits_grad(s, half):
        cols = slice(half * part, (half + 1) * part)
        total = gb[:, cols]
        for rel in range(geo.chips):
            span = slice(rel * slab, (rel + 1) * slab)
            logits = zo[parity(s), span, cols] + zr[parity(s), span, cols] + bias[:, cols]
            inverse = 1.0 / (1.0 + logits)
            row = lax.rem(s - geo.hops(rel), rows)
            parts = []
            for cr in PAIR:
                at = 2 * rel + cr
                tok = slice(cr * unit, (cr + 1) * unit)
                grad_row = rep[at, pl.ds(row, 1), cols] * inverse[tok, :]
                grad_row = jnp.where(logits[tok, :] > 0.0, grad_row, 0.0) * mt[row, :, at:at + 1]
                total = total + grad_row
                parts.append(grad_row)
            dz[parity(s), span, cols] = jnp.concatenate(parts, axis=0).astype(BF16)
        gb[:, cols] = total
        dzt[cols, :] = dz[parity(s), :, cols].T

    def accumulate(s, at, count):
        for lane in range(nd):
            acc[lane, at:at + count, :] += jnp.dot(dzt[at:at + count, :], net.tokens(s, lane),
                                                   preferred_element_type=F32)

    def hidden_grad(s, lane):
        block = jnp.dot(dz[parity(s)], wt[lane], preferred_element_type=F32).astype(BF16)
        for rel in range(geo.chips):
            dsum[ring(s), lane, net.place(rel, lane), :] = block[rel * slab:(rel + 1) * slab, :]
        rs_copy(1, lane, s + 1).start()

    def grad_step(s, carry):
        for lane in range(nd):
            net.arrive(s, lane, False)
        for half in PAIR:
            zs[parity(s), :, half * part:(half + 1) * part] = logit_sum(s, vocab + half * part)
            z_copy(s, half).start()
        hidden_grad(s - 1, 0)
        zo[parity(s), :, :part] = logit_sum(s, 0)
        z_copy(s, 0).wait()
        logits_grad(s, 0)
        zo[parity(s), :, part:vocab] = logit_sum(s, part)
        dz_copy(s, 0, True).start()
        dz_copy(s, 0, False).start()
        z_copy(s, 1).wait()
        logits_grad(s, 1)
        accumulate(s, 0, part)
        dz_copy(s, 1, True).start()
        dz_copy(s, 1, False).start()
        hidden_grad(s - 1, 1)
        merge_rest(s)
        accumulate(s, part, part)
        finish(s)
        start_rest(s)
        for half in PAIR:
            dz_copy(s, half, True).wait()
        merge_first(s)
        accumulate(s, vocab, vocab)
        for lane in range(nd):
            net.release(s, lane, False)
            rs_copy(2, lane, s).start()
        for lane in range(2, nd):
            hidden_grad(s - 1, lane)
        for half in PAIR:
            dz_copy(s, half, False).wait()
        return carry

    def wout(lane):
        return pltpu.make_async_copy(
            wv.at[lane, :, pl.ds(0, vocab)],
            gw_hbm.at[pl.ds(pl.multiple_of(half_at[0] + lane * width, width), width), :], wout_sem.at[lane])

    def wout_cross(lane):
        return pltpu.make_async_remote_copy(
            src_ref=wv.at[lane, :, pl.ds(vocab, vocab)],
            dst_ref=gw_hbm.at[pl.ds(pl.multiple_of(half_at[0] + lane * width, width), width), :],
            send_sem=wo_send.at[lane], recv_sem=wo_recv.at[lane], device_id=net.sib, device_id_type=MESH)

    def store_weights(lane):
        for half in PAIR:
            span = slice(half * vocab, (half + 1) * vocab)
            wv[lane, :, span] = acc[lane, span, :].astype(BF16).T
        wout(lane).start()
        wout_cross(lane).start()

    def flush():
        end = steps
        merge_rest(end)
        finish(end)
        start_rest(end)
        merge_first(end)
        for lane in range(nd):
            rs_copy(2, lane, end).start()
            hidden_grad(end - 1, lane)
        store_weights(0)

        end += 1
        merge_rest(end)
        finish(end)
        start_rest(end)
        merge_first(end)
        for lane in range(nd):
            rs_copy(2, lane, end).start()
            flush_copy(0, lane).start()

        end += 1
        for lane in range(nd):
            for stage_no in later:
                rs_copy(stage_no, lane, end - 1).wait()
            flush_copy(0, lane).wait()
        for lane in range(nd):
            m3[ring(end), lane] = merged(3, lane, end, m2[ring(end + 1), lane, :low[3]]).astype(BF16)
            m2[ring(end), lane] = merged(2, lane, end, m1[ring(end + 1), lane, :low[2]]).astype(BF16)
            last[lane] = merged(4, lane, end, m3[ring(end + 1), lane, :low[4]])
            dsum[spare, lane, :low[2], :] = (x2[lane].astype(F32)
                                          + m1[ring(end + 2), lane, :low[2]].astype(F32)).astype(BF16)
            rs_copy(3, lane, end).start()
            rs_copy(4, lane, end).start()
            flush_copy(1, lane).start()
            flush_copy(2, lane).start()
        finish(end)
        store_weights(1)

        end += 1
        for lane in range(nd):
            for stage_no in range(3, 5):
                rs_copy(stage_no, lane, end - 1).wait()
            flush_copy(1, lane).wait()
            flush_copy(2, lane).wait()
        for lane in range(nd):
            last[lane] = merged(4, lane, end, m3[ring(end + 1), lane, :low[4]])
            m3[ring(end), lane] = merged(3, lane, end, m2[ring(end + 1), lane, :low[3]]).astype(BF16)
            dsum[spare, lane, low[2]:deep[1], :] = (
                x3[0, lane].astype(F32) + m2[ring(end + 2), lane, :low[3]].astype(F32)).astype(BF16)
            dsum[spare, lane, deep[1]:low[1], :] = (
                x3[1, lane].astype(F32) + dsum[spare, lane, :low[3], :].astype(F32)).astype(BF16)
            rs_copy(4, lane, end).start()
            for i in range(3, 6):
                flush_copy(i, lane).start()
        finish(end)
        store_weights(2)

        end += 1
        for lane in range(nd):
            rs_copy(4, lane, end - 1).wait()
            for i in range(3, 6):
                flush_copy(i, lane).wait()
        for lane in range(nd):
            own3 = (m3[ring(end + 1), lane, :low[4]], m3[ring(end + 2), lane, :low[4]],
                    dsum[spare, lane, low[2]:deep[0], :],
                    dsum[spare, lane, deep[1]:deep[2], :])
            got4 = (r4[parity(end + 1), lane], x4[0, lane], x4[1, lane], x4[2, lane])
            for i in range(nd + 1):
                total = dsum[tail, lane, :low[4], :].astype(F32)
                if i < nd:
                    total = got4[i].astype(F32) + own3[i].astype(F32)
                if i > 0:
                    total = total + early[i - 1, lane]
                emit(lane, end + i, total, 2 + i)
        out_copy(end - 1, parity(end - 1)).wait()
        for i in range(nd + 1):
            out_copy(end + i, 2 + i).start()
        store_weights(3)
        for i in range(nd + 1):
            out_copy(end + i, 2 + i).wait()

    net.begun()
    lax.fori_loop(1, first, loss_step, 0)
    for lane in range(1, nd):
        net.release(first - 1, lane, True)
    for lane in range(nd):
        for stage_no in range(1, 5):
            rs_copy(stage_no, lane, first - 1).start()
    reps(first - 1)
    softmax()
    lax.fori_loop(first, steps, grad_step, 0)
    flush()
    gb_ref[...] = sum_rows(gb[...])
    stores = []
    for half in PAIR:
        cols = pl.ds(half_at[half], geo.half)
        stores.append(pltpu.make_async_copy(gout.at[half, pl.ds(0, n_q)], gq_hbm.at[:, :, cols], hout_sem.at[half, 0]))
        stores.append(pltpu.make_async_copy(gout.at[half, pl.ds(n_q, n_dp)], gd_hbm.at[:, :, cols],
                                            hout_sem.at[half, 1]))
    for copy in stores:
        copy.start()
    for copy in stores:
        copy.wait()
    for lane in range(nd):
        wout(lane).wait()
        wout_cross(lane).wait()


def call_fused(geo, const, q_rows, d_rows, w_head, bias, mrow, positive, place, doc_place, pick):
    bufs, sems = gather_scratch(geo)
    dma = pltpu.SemaphoreType.DMA
    nd, tok, width, vocab, rows = geo.nd, geo.tokens, geo.width, geo.vocab, geo.rows
    n_q, docs, slots = const[0], doc_place.shape[0], 2 * geo.chips
    lanes = doc_place.shape[1]
    hq = n_q // 2
    hbm, vmem = pl.BlockSpec(memory_space=pl.ANY), pl.BlockSpec(memory_space=pltpu.VMEM)
    logit = pltpu.VMEM((2, tok, vocab), F32)
    scratch = bufs + [
        pltpu.VMEM((nd, width, 2 * vocab), BF16), pltpu.VMEM((nd, 2 * vocab, width), BF16),
        pltpu.VMEM((nd, 2 * vocab, width), F32), logit, logit, logit,
        pltpu.VMEM((2, tok, 2 * vocab), BF16), pltpu.VMEM((2 * vocab, tok), BF16),
        pltpu.VMEM((3, nd, tok, width), BF16),
        pltpu.VMEM((3, nd, tok // 2, width), BF16), pltpu.VMEM((3, nd, tok // 4, width), BF16),
        pltpu.VMEM((3, nd, tok // 8, width), BF16),
        pltpu.VMEM((2, nd, tok // 2, width), BF16), pltpu.VMEM((2, nd, tok // 4, width), BF16),
        pltpu.VMEM((2, nd, tok // 8, width), BF16), pltpu.VMEM((2, nd, tok // 16, width), BF16),
        pltpu.VMEM((nd, tok // 4, width), BF16), pltpu.VMEM((2, nd, tok // 8, width), BF16),
        pltpu.VMEM((3, nd, tok // 16, width), BF16),
        pltpu.VMEM((nd + 3, geo.unit, geo.half), BF16), pltpu.VMEM((2, rows, geo.unit, geo.half), BF16),
        pltpu.VMEM((nd, nd, geo.slab, width), F32), pltpu.VMEM((nd, geo.slab, width), F32),
        pltpu.VMEM((geo.unit, vocab), F32),
        pltpu.VMEM((slots, rows, vocab), F32), pltpu.VMEM((docs, vocab), F32), pltpu.VMEM((docs, vocab), F32),
        pltpu.VMEM((slots,) + mrow.shape, F32), pltpu.VMEM((mrow.shape[1] // geo.unit, geo.unit, 128), F32),
        pltpu.VMEM((slots, hq, lanes), F32), pltpu.VMEM((slots, hq, lanes), F32),
        pltpu.VMEM((hq, lanes), F32), pltpu.VMEM((slots, hq, lanes), F32),
        pltpu.VMEM((1, lanes), F32), pltpu.VMEM((slots, 1, lanes), F32),
        dma((4,)), dma((nd,)), dma((nd,)), dma((nd,)), dma((2, 2)), dma((2, 2)), dma((2, 2)), dma((2, 2)),
        dma((4, nd, 2)), dma((4, nd, 2)), dma((6, nd)), dma((6, nd)), dma((nd + 3,)), dma((nd + 3,)), dma((nd,)), dma((nd,)),
        dma((nd,)), dma((2, 2)), dma((4, slots)), dma((4, slots))] + sems
    return pl.pallas_call(
        functools.partial(fused_kernel, geo, const),
        name="lexical_head",
        out_shape=[jax.ShapeDtypeStruct((1, lanes), F32), jax.ShapeDtypeStruct(w_head.shape, BF16),
                   jax.ShapeDtypeStruct((1, vocab), F32), jax.ShapeDtypeStruct(q_rows.shape, BF16),
                   jax.ShapeDtypeStruct(d_rows.shape, BF16)],
        in_specs=[hbm, hbm, hbm] + [vmem] * 6,
        out_specs=[vmem, hbm, vmem, hbm, hbm],
        scratch_shapes=scratch,
        compiler_params=pltpu.CompilerParams(collective_id=0, has_side_effects=True, vmem_limit_bytes=VMEM_LIMIT),
    )(q_rows, d_rows, w_head, bias, mrow, positive, place, doc_place, pick)


def solution(mesh):
    n_group = mesh.shape['tp']
    row_spec = P(('dp', 'tp'))
    mask_spec = P(('dp', 'tp'), None)
    hid_spec = P(('dp', 'tp'), None, None)

    def local_step(q_hidden, d_hidden, q_mask, d_mask, positive, w_head, b_head):
        hidden_size, vocab_loc = w_head.shape
        vocab_size = vocab_loc * n_group
        n_q, q_len, _ = q_hidden.shape
        n_d, d_len, _ = d_hidden.shape
        pieces = d_len // q_len
        q_batch, d_batch = n_q * n_group, n_d * n_group
        tau = q_len * math.sqrt(vocab_size * d_len) / 16.0
        lam_q = 4.0 / (vocab_size * q_len * q_len)
        lam_d = 4.0 / (vocab_size * d_len * d_len)
        rows = n_q + n_d * pieces
        geo = Geometry(n_group, rows, hidden_size, vocab_loc, q_len)
        side, slots = geo.side, 2 * geo.chips
        lanes = max(128, 2 * d_batch)

        me = lax.axis_index('tp')
        slot = jnp.arange(slots)
        chip, rel = me // 2, slot // 2
        step_x, step_y = rel % side, rel // side
        chip_of = (((chip // side) ^ step_y ^ (step_y >> 1)) * side + ((chip % side) ^ step_x ^ (step_x >> 1)))
        device_of = chip_of * 2 + slot % 2
        place = jax.nn.one_hot(device_of, lanes, dtype=F32)
        doc_of = jnp.add.outer(jnp.arange(n_d), device_of * n_d).reshape((n_d * slots,))
        doc_place = jax.nn.one_hot(doc_of, lanes, dtype=F32)
        pick = np.concatenate([np.kron(np.eye(slots), np.repeat(row, pieces)) for row in np.eye(n_d)])

        own_mask = jnp.concatenate([q_mask.reshape((-1,)), d_mask.reshape((-1,))]).astype(F32)
        mrow = jnp.pad(own_mask, (0, -own_mask.shape[0] % 128)).reshape((1, -1))
        const = (n_q, n_d, lam_q, lam_d, tau, float(q_batch), float(d_batch))
        loss, grad_w, grad_b, grad_q, grad_d = call_fused(
            geo, const, q_hidden, d_hidden.reshape((n_d * pieces, q_len, hidden_size)), w_head,
            b_head.reshape((1, vocab_loc)), mrow, positive.reshape((n_q, 1)), place, doc_place, jnp.asarray(pick, F32))
        return (loss[0, 0:1], grad_w, grad_b.reshape((vocab_loc,)), grad_q, grad_d.reshape(d_hidden.shape))

    return jax.shard_map(local_step, mesh=mesh,
                         in_specs=(hid_spec, hid_spec, mask_spec, mask_spec, row_spec, P(None, 'tp'), P('tp')),
                         out_specs=(P('dp'), P('dp', 'tp'), row_spec, hid_spec, hid_spec),
                         check_vma=False)
```

time: 525 us -> 497 us (0.947)
  Pallas kernels: 503 us -> 479 us
    pallas_call x1, Pallas kernels: 503 us -> 479 us  [call_fused(): pl.pallas_call(functools.partial(fused_kernel, geo, const), name='lexical...]
    unnamed x2 -> x11, local copies, waits for them, and re-layouts: 8.51 us -> 11 us
where the time goes in v5:
time: 497 us
  Pallas kernels  479 us (96%)
  local copies, waits for them, and re-layouts  13.8 us (3%)
    pallas_call x1, Pallas kernels, call_fused(): pl.pallas_call(functools.partial(fused_kernel, geo, const), name='lexical...  479 us
    unnamed x11, local copies, waits for them, and re-layouts  11 us

profile of v5, /device:TPU:97, one launch (start us, length us, event | category | flops | bytes accessed | tf_op | source)
XLA Modules:
  0.0 497.1 jit_solution(6800408748762243414)
XLA Ops:
  0.7 0.1 add.111
  0.8 0.8 reshape.166
  1.5 0.8 copy.15
  2.3 0.1 reshape.165
  2.4 0.6 pad.4
  3.0 1.3 copy.16.pos_ref
  4.3 0.7 fusion.1.place
  5.0 0.7 fusion.doc_place
  5.7 479.5 %lexical_head.1 = (f32[1,128]{1,0:T(1,128)}, bf16[4096,1024]{1,0:T(8,128)(2,1)}, f32[1,1024]{1,0:T(1,128)}, bf16[16,8,4096]{2,1,0:T(8,128)(2,1)}, bf16[8,8,4096]{2,1,0:T(8,128)(2,1)}) custom-call(bf16[16,8,4096]{2,1,0:T(8,128)(2,1)} %q_hbm.1, bf16[8,8,4096]{2,1,0:T(8,128)(2,1)} %bitcast.8, bf16[4096,1024]{1,0:T(8,128)(2,1)} %w_hbm.1, f32[1,1024]{1,0:T(1,128)} %bitcast.10, ...), custom_call_target="tpu_custom_call" | custom-call | tf_op jit(solution)/shard_map/lexical_head/pallas_call | solution.py:784
  485.7 0.0 copy-start.2
  485.7 0.0 copy-start
  485.7 0.0 copy-start.1
  485.7 7.9 %copy.23 = bf16[4096,1024]{1,0:T(8,128)(2,1)} copy(bf16[4096,1024]{1,0:T(8,128)(2,1)} %get-tuple-element.23) | data formatting | bytes 16777216
  493.6 0.0 copy-done.2
  493.6 0.6 copy.24
  494.2 0.0 copy-done
  494.2 1.0 copy.25
  495.2 0.0 copy-done.1
  495.2 0.8 copy.26
  (3 shorter events, 0.0 us)
Async XLA Ops:
  485.7 7.9 %copy-start.2 = (f32[1,1024]{1,0:T(1,128)S(1)}, f32[1,1024]{1,0:T(1,128)}, u32[]{:S(2)}) copy-start(f32[1,1024]{1,0:T(1,128)} %get-tuple-element.12) | copy-start | bytes 12292
  485.7 8.5 %copy-start = (bf16[16,8,4096]{2,1,0:T(8,128)(2,1)S(1)}, bf16[16,8,4096]{2,1,0:T(8,128)(2,1)}, u32[]{:S(2)}) copy-start(bf16[16,8,4096]{2,1,0:T(8,128)(2,1)} %get-tuple-element.25) | copy-start | bytes 3145732
  485.7 9.5 %copy-start.1 = (bf16[8,8,4096]{2,1,0:T(8,128)(2,1)S(1)}, bf16[8,8,4096]{2,1,0:T(8,128)(2,1)}, u32[]{:S(2)}) copy-start(bf16[8,8,4096]{2,1,0:T(8,128)(2,1)} %get-tuple-element.14) | copy-start | bytes 1572868

commit v6 on v5

--- a/solution.py
+++ b/solution.py
@@ -158,34 +158,25 @@
         geo = self.geo
         self.inject(s, lane)
 
-        def receive():
-            for pos in range(geo.nd):
-                self.ici(s - 1, lane, pos).wait_recv()
-
-        def credits():
-            pl.semaphore_wait(self.free_piece.at[lane], 1)
-            for pos in range(geo.nd):
-                pl.semaphore_wait(self.free_ici.at[lane, pos], 1)
-
-        def send():
-            for pos in reversed(range(geo.nd)):
-                self.ici(s, lane, pos).start()
-            self.piece(s + 1, lane).start()
-
         if loss:
             @pl.when(s > 1)
             def _():
-                receive()
-
-            credits()
-            send()
+                self.receive(s, lane)
         else:
-            receive()
-            credits()
-
-            @pl.when(s < geo.steps - 1)
-            def _():
-                send()
+            self.receive(s, lane)
+        self.credits(lane)
+        for pos in reversed(range(geo.nd)):
+            self.ici(s, lane, pos).start()
+        self.piece(s + 1, lane).start()
+
+    def receive(self, s, lane):
+        for pos in range(self.geo.nd):
+            self.ici(s - 1, lane, pos).wait_recv()
+
+    def credits(self, lane):
+        pl.semaphore_wait(self.free_piece.at[lane], 1)
+        for pos in range(self.geo.nd):
+            pl.semaphore_wait(self.free_ici.at[lane, pos], 1)
 
     def grant(self, lane):
         geo = self.geo
@@ -194,21 +185,16 @@
                                 device_id=self.same[(lane + pos) % geo.nd], device_id_type=MESH)
         pl.semaphore_signal(self.free_piece.at[lane], inc=1, device_id=self.sib, device_id_type=MESH)
 
-    def release(self, s, lane, loss):
-        geo = self.geo
-
-        def sent():
-            for pos in range(geo.nd):
-                self.ici(s, lane, pos).wait_send()
-
-        if loss:
-            sent()
-            self.grant(lane)
-        else:
-            @pl.when(s < geo.steps - 1)
-            def _():
-                sent()
-                self.grant(lane)
+    def release(self, s, lane):
+        for pos in range(self.geo.nd):
+            self.ici(s, lane, pos).wait_send()
+        self.grant(lane)
+
+    def end(self, s):
+        for lane in range(self.geo.nd):
+            self.receive(s, lane)
+            self.credits(lane)
+            self.piece(s, lane).wait()
 
     def tokens(self, s, lane):
         geo = self.geo
@@ -233,7 +219,7 @@
     return found
 
 
-def fused_kernel(geo, const, q_hbm, d_hbm, w_hbm, bias, mrow, pos_ref, place, doc_place, pick,
+def fused_kernel(geo, const, q_hbm, d_hbm, w_hbm, bias, mrow, tables, pick,
                  loss_ref, gw_hbm, gb_ref, gq_hbm, gd_hbm,
                  x, stage, ownx, wv, wt, acc, zo, zs, zr, dz, dzt, dsum, m1, m2, m3,
                  r1, r2, r3, r4, x2, x3, x4, ost, gout, early, last, gb, rep, rd, drd, mall, mt, sbuf, pall, gmine, gall,
@@ -247,6 +233,8 @@
     me = lax.axis_index("tp")
     net = Gather(geo, me, x, stage, ownx, sems)
     core, same = net.core, net.same
+    docs = n_d * slots
+    place, doc_place, target = tables.at[:slots], tables.at[pl.ds(slots, docs)], tables.at[pl.ds(slots + docs, n_q)]
     peers = all_peers(geo, me)
     half_at = [pl.multiple_of(core * geo.half, geo.half), pl.multiple_of((1 - core) * geo.half, geo.half)]
 
@@ -450,11 +438,11 @@
         prepare(s)
         for lane in range(nd):
             if lane == nd - 1:
-                net.release(s, 0, True)
+                net.release(s, 0)
             else:
                 @pl.when(s > 1)
                 def _():
-                    net.release(s - 1, lane + 1, True)
+                    net.release(s - 1, lane + 1)
 
             net.arrive(s, lane, True)
 
@@ -506,13 +494,12 @@
             total = total + pall[i]
         scores = jnp.concatenate([total, pltpu.roll(total, shift, 1)], axis=0) / tau
         lane_no = lax.broadcasted_iota(jnp.int32, scores.shape, 1)
-        target = lane_no == pos_ref[...]
         masked = jnp.where(lane_no < d_batch, scores, -jnp.inf)
         top = jnp.max(masked, axis=1, keepdims=True)
         log_norm = jnp.log(sum_lanes(jnp.exp(masked - top))) + top
-        hit = sum_lanes(jnp.where(target, scores, 0.0))
+        hit = sum_lanes(target[...] * scores)
         mine = sum_rows(log_norm - hit) / q_batch + reg
-        grad = (jnp.exp(masked - log_norm) - target.astype(F32)) / (q_batch * tau)
+        grad = (jnp.exp(masked - log_norm) - target[...]) / (q_batch * tau)
         gmine[...] = grad[:hq] + pltpu.roll(grad[hq:], shift, 1)
         lmine[...] = jnp.broadcast_to(mine, lmine.shape)
         grads_out = broadcast(2, lambda slot: gmine, gall)
@@ -586,7 +573,6 @@
         block = jnp.dot(dz[parity(s)], wt[lane], preferred_element_type=F32).astype(BF16)
         for rel in range(geo.chips):
             dsum[ring(s), lane, net.place(rel, lane), :] = block[rel * slab:(rel + 1) * slab, :]
-        rs_copy(1, lane, s + 1).start()
 
     def grad_step(s, carry):
         for lane in range(nd):
@@ -595,6 +581,7 @@
             zs[parity(s), :, half * part:(half + 1) * part] = logit_sum(s, vocab + half * part)
             z_copy(s, half).start()
         hidden_grad(s - 1, 0)
+        rs_copy(1, 0, s).start()
         zo[parity(s), :, :part] = logit_sum(s, 0)
         z_copy(s, 0).wait()
         logits_grad(s, 0)
@@ -607,6 +594,7 @@
         dz_copy(s, 1, True).start()
         dz_copy(s, 1, False).start()
         hidden_grad(s - 1, 1)
+        rs_copy(1, 1, s).start()
         merge_rest(s)
         accumulate(s, part, part)
         finish(s)
@@ -616,10 +604,11 @@
         merge_first(s)
         accumulate(s, vocab, vocab)
         for lane in range(nd):
-            net.release(s, lane, False)
+            net.release(s, lane)
             rs_copy(2, lane, s).start()
         for lane in range(2, nd):
             hidden_grad(s - 1, lane)
+            rs_copy(1, lane, s).start()
         for half in PAIR:
             dz_copy(s, half, False).wait()
         return carry
@@ -644,13 +633,16 @@
 
     def flush():
         end = steps
+        for lane in range(nd):
+            hidden_grad(end - 1, lane)
         merge_rest(end)
-        finish(end)
+        for lane in range(nd):
+            rs_copy(1, lane, end).start()
         start_rest(end)
         merge_first(end)
         for lane in range(nd):
             rs_copy(2, lane, end).start()
-            hidden_grad(end - 1, lane)
+        finish(end)
         store_weights(0)
 
         end += 1
@@ -720,13 +712,14 @@
         for i in range(nd + 1):
             out_copy(end + i, 2 + i).start()
         store_weights(3)
+        net.end(steps)
         for i in range(nd + 1):
             out_copy(end + i, 2 + i).wait()
 
     net.begun()
     lax.fori_loop(1, first, loss_step, 0)
     for lane in range(1, nd):
-        net.release(first - 1, lane, True)
+        net.release(first - 1, lane)
     for lane in range(nd):
         for stage_no in range(1, 5):
             rs_copy(stage_no, lane, first - 1).start()
@@ -750,12 +743,11 @@
         wout_cross(lane).wait()
 
 
-def call_fused(geo, const, q_rows, d_rows, w_head, bias, mrow, positive, place, doc_place, pick):
+def call_fused(geo, const, q_rows, d_rows, w_head, bias, mrow, tables, pick):
     bufs, sems = gather_scratch(geo)
     dma = pltpu.SemaphoreType.DMA
     nd, tok, width, vocab, rows = geo.nd, geo.tokens, geo.width, geo.vocab, geo.rows
-    n_q, docs, slots = const[0], doc_place.shape[0], 2 * geo.chips
-    lanes = doc_place.shape[1]
+    n_q, (docs, _), slots, lanes = const[0], pick.shape, 2 * geo.chips, tables.shape[1]
     hq = n_q // 2
     hbm, vmem = pl.BlockSpec(memory_space=pl.ANY), pl.BlockSpec(memory_space=pltpu.VMEM)
     logit = pltpu.VMEM((2, tok, vocab), F32)
@@ -787,11 +779,43 @@
         out_shape=[jax.ShapeDtypeStruct((1, lanes), F32), jax.ShapeDtypeStruct(w_head.shape, BF16),
                    jax.ShapeDtypeStruct((1, vocab), F32), jax.ShapeDtypeStruct(q_rows.shape, BF16),
                    jax.ShapeDtypeStruct(d_rows.shape, BF16)],
-        in_specs=[hbm, hbm, hbm] + [vmem] * 6,
+        in_specs=[hbm, hbm, hbm] + [vmem] * 4,
         out_specs=[vmem, hbm, vmem, hbm, hbm],
         scratch_shapes=scratch,
         compiler_params=pltpu.CompilerParams(collective_id=0, has_side_effects=True, vmem_limit_bytes=VMEM_LIMIT),
-    )(q_rows, d_rows, w_head, bias, mrow, positive, place, doc_place, pick)
+    )(q_rows, d_rows, w_head, bias, mrow, tables, pick)
+
+
+def store_kernel(count, *refs):
+    sources, results, holds = refs[:count], refs[count:2 * count], refs[2 * count:3 * count]
+    read_sem, write_sem = refs[3 * count:]
+    reads, writes = [], []
+    for source, result, hold in zip(sources, results, holds):
+        for piece in range(hold.shape[0]):
+            span = pl.ds(piece * hold.shape[1], hold.shape[1])
+            at = len(reads)
+            reads.append(pltpu.make_async_copy(source.at[span], hold.at[piece], read_sem.at[at]))
+            writes.append(pltpu.make_async_copy(hold.at[piece], result.at[span], write_sem.at[at]))
+    for copy in reads:
+        copy.start()
+    for read, write in zip(reads, writes):
+        read.wait()
+        write.start()
+    for copy in writes:
+        copy.wait()
+
+
+def call_store(geo, *arrays):
+    pieces = [geo.chips // (1 + 3 * (x.ndim - 2)) for x in arrays]
+    holds = [pltpu.VMEM((n, x.shape[0] // n) + x.shape[1:], x.dtype) for n, x in zip(pieces, arrays)]
+    hbm = pl.BlockSpec(memory_space=pl.ANY)
+    dma = pltpu.SemaphoreType.DMA((sum(pieces),))
+    return pl.pallas_call(
+        functools.partial(store_kernel, len(arrays)), name="store_results",
+        out_shape=[jax.ShapeDtypeStruct(x.shape, x.dtype) for x in arrays],
+        in_specs=[hbm] * len(arrays), out_specs=[hbm] * len(arrays), scratch_shapes=holds + [dma, dma],
+        compiler_params=pltpu.CompilerParams(vmem_limit_bytes=VMEM_LIMIT),
+    )(*arrays)
 
 
 def solution(mesh):
@@ -821,9 +845,8 @@
         step_x, step_y = rel % side, rel // side
         chip_of = (((chip // side) ^ step_y ^ (step_y >> 1)) * side + ((chip % side) ^ step_x ^ (step_x >> 1)))
         device_of = chip_of * 2 + slot % 2
-        place = jax.nn.one_hot(device_of, lanes, dtype=F32)
         doc_of = jnp.add.outer(jnp.arange(n_d), device_of * n_d).reshape((n_d * slots,))
-        doc_place = jax.nn.one_hot(doc_of, lanes, dtype=F32)
+        tables = jax.nn.one_hot(jnp.concatenate([device_of, doc_of, positive]), lanes, dtype=F32)
         pick = np.concatenate([np.kron(np.eye(slots), np.repeat(row, pieces)) for row in np.eye(n_d)])
 
         own_mask = jnp.concatenate([q_mask.reshape((-1,)), d_mask.reshape((-1,))]).astype(F32)
@@ -831,7 +854,8 @@
         const = (n_q, n_d, lam_q, lam_d, tau, float(q_batch), float(d_batch))
         loss, grad_w, grad_b, grad_q, grad_d = call_fused(
             geo, const, q_hidden, d_hidden.reshape((n_d * pieces, q_len, hidden_size)), w_head,
-            b_head.reshape((1, vocab_loc)), mrow, positive.reshape((n_q, 1)), place, doc_place, jnp.asarray(pick, F32))
+            b_head.reshape((1, vocab_loc)), mrow, tables, jnp.asarray(pick, F32))
+        grad_w, grad_q, grad_d = call_store(geo, grad_w, grad_q, grad_d)
         return (loss[0, 0:1], grad_w, grad_b.reshape((vocab_loc,)), grad_q, grad_d.reshape(d_hidden.shape))
 
     return jax.shard_map(local_step, mesh=mesh,

time: 497 us -> 493 us (level)
  local copies, waits for them, and re-layouts: 13.8 us -> 3.51 us
  Pallas kernels: 479 us -> 485 us
    unnamed x11 -> x2, local copies, waits for them, and re-layouts: 11 us -> 2.02 us
    pallas_call x0 -> x1, Pallas kernels: none -> 7.86 us  [call_store(): pl.pallas_call(functools.partial(store_kernel, len(arrays)), name='store_...]
where the time goes in v6:
time: 493 us; the launch traced here: 492 us
  Pallas kernels  485 us (98%)
    pallas_call x1, Pallas kernels, call_fused(): pl.pallas_call(functools.partial(fused_kernel, geo, const), name='lexical...  477 us

profile of v6, /device:TPU:97, one launch (start us, length us, event | category | flops | bytes accessed | tf_op | source)
XLA Modules:
  0.0 492.4 jit_solution(13954787771130404659)
XLA Ops:
  0.7 0.1 add.84
  0.8 0.7 pad_add_fusion
  1.5 0.8 reshape.96
  2.3 0.8 copy.14
  3.0 0.1 reshape.95
  3.1 0.6 pad.4
  3.7 0.7 fusion.tables
  4.4 477.0 %lexical_head.1 = (f32[1,128]{1,0:T(1,128)}, bf16[4096,1024]{1,0:T(8,128)(2,1)}, f32[1,1024]{1,0:T(1,128)}, bf16[16,8,4096]{2,1,0:T(8,128)(2,1)}, bf16[8,8,4096]{2,1,0:T(8,128)(2,1)}) custom-call(bf16[16,8,4096]{2,1,0:T(8,128)(2,1)} %q_hbm.1, bf16[8,8,4096]{2,1,0:T(8,128)(2,1)} %bitcast.7, bf16[4096,1024]{1,0:T(8,128)(2,1)} %w_hbm.1, f32[1,1024]{1,0:T(1,128)} %bitcast.8, ...), custom_call_target="tpu_custom_call" | custom-call | tf_op jit(solution)/shard_map/lexical_head/pallas_call | solution.py:776
  481.4 7.9 %store_results.1 = (bf16[4096,1024]{1,0:T(8,128)(2,1)}, bf16[16,8,4096]{2,1,0:T(8,128)(2,1)}, bf16[8,8,4096]{2,1,0:T(8,128)(2,1)}) custom-call(bf16[4096,1024]{1,0:T(8,128)(2,1)} %get-tuple-element.14.refs_0_, bf16[16,8,4096]{2,1,0:T(8,128)(2,1)} %get-tuple-element.15.refs_1_, bf16[8,8,4096]{2,1,0:T(8,128)(2,1)} %get-tuple-element.16.refs_2_), custom_call_target="tpu_custom_call" | custom-call | tf_op jit(solution)/shard_map/store_results/pallas_call | solution.py:813
  490.0 1.3 copy.18
  (3 shorter events, 0.0 us)

commit v7 on v6

--- a/solution.py
+++ b/solution.py
@@ -513,6 +513,8 @@
         drd[...] = jnp.broadcast_to((2.0 * lam_d / d_batch) * d_mean, drd.shape)
         for copy in arrivals(2, gall):
             copy.wait_recv()
+        for lane in range(nd):
+            net.arrive(first, lane, False)
 
         def back(c, carry):
             at = pl.ds(c * chunk, chunk)
@@ -575,8 +577,6 @@
             dsum[ring(s), lane, net.place(rel, lane), :] = block[rel * slab:(rel + 1) * slab, :]
 
     def grad_step(s, carry):
-        for lane in range(nd):
-            net.arrive(s, lane, False)
         for half in PAIR:
             zs[parity(s), :, half * part:(half + 1) * part] = logit_sum(s, vocab + half * part)
             z_copy(s, half).start()
@@ -611,6 +611,11 @@
             rs_copy(1, lane, s).start()
         for half in PAIR:
             dz_copy(s, half, False).wait()
+
+        @pl.when(s < steps - 1)
+        def _():
+            for lane in range(nd):
+                net.arrive(s + 1, lane, False)
         return carry
 
     def wout(lane):
@@ -806,7 +811,7 @@
 
 
 def call_store(geo, *arrays):
-    pieces = [geo.chips // (1 + 3 * (x.ndim - 2)) for x in arrays]
+    pieces = [max(1, min(geo.chips, x.shape[0] // 2)) for x in arrays]
     holds = [pltpu.VMEM((n, x.shape[0] // n) + x.shape[1:], x.dtype) for n, x in zip(pieces, arrays)]
     hbm = pl.BlockSpec(memory_space=pl.ANY)
     dma = pltpu.SemaphoreType.DMA((sum(pieces),))
@@ -855,7 +860,7 @@
         loss, grad_w, grad_b, grad_q, grad_d = call_fused(
             geo, const, q_hidden, d_hidden.reshape((n_d * pieces, q_len, hidden_size)), w_head,
             b_head.reshape((1, vocab_loc)), mrow, tables, jnp.asarray(pick, F32))
-        grad_w, grad_q, grad_d = call_store(geo, grad_w, grad_q, grad_d)
+        loss, grad_w, grad_b, grad_q, grad_d = call_store(geo, loss, grad_w, grad_b, grad_q, grad_d)
         return (loss[0, 0:1], grad_w, grad_b.reshape((vocab_loc,)), grad_q, grad_d.reshape(d_hidden.shape))
 
     return jax.shard_map(local_step, mesh=mesh,

time: 493 us -> 490 us (level)
  no operation moved by 1% of the time
where the time goes in v7:
time: 490 us
  Pallas kernels  485 us (99%)
    pallas_call x1, Pallas kernels, call_fused(): pl.pallas_call(functools.partial(fused_kernel, geo, const), name='lexical...  477 us

profile of v7, /device:TPU:97, one launch (start us, length us, event | category | flops | bytes accessed | tf_op | source)
XLA Modules:
  0.0 489.5 jit_solution(11667143151855075899)
XLA Ops:
  0.7 0.1 add.84
  0.8 0.7 pad_add_fusion
  1.5 0.8 reshape.96
  2.3 0.8 copy.14
  3.0 0.1 reshape.95
  3.1 0.6 pad.4
  3.7 0.7 fusion.tables
  4.4 476.9 %lexical_head.1 = (f32[1,128]{1,0:T(1,128)}, bf16[4096,1024]{1,0:T(8,128)(2,1)}, f32[1,1024]{1,0:T(1,128)}, bf16[16,8,4096]{2,1,0:T(8,128)(2,1)}, bf16[8,8,4096]{2,1,0:T(8,128)(2,1)}) custom-call(bf16[16,8,4096]{2,1,0:T(8,128)(2,1)} %q_hbm.1, bf16[8,8,4096]{2,1,0:T(8,128)(2,1)} %bitcast.7, bf16[4096,1024]{1,0:T(8,128)(2,1)} %w_hbm.1, f32[1,1024]{1,0:T(1,128)} %bitcast.8, ...), custom_call_target="tpu_custom_call" | custom-call | tf_op jit(solution)/shard_map/lexical_head/pallas_call | solution.py:781
  481.3 8.0 %store_results.1 = (f32[1,128]{1,0:T(1,128)}, bf16[4096,1024]{1,0:T(8,128)(2,1)}, f32[1,1024]{1,0:T(1,128)}, bf16[16,8,4096]{2,1,0:T(8,128)(2,1)}, bf16[8,8,4096]{2,1,0:T(8,128)(2,1)}) custom-call(f32[1,128]{1,0:T(1,128)} %get-tuple-element.15.refs_0_, bf16[4096,1024]{1,0:T(8,128)(2,1)} %get-tuple-element.16.refs_1_, f32[1,1024]{1,0:T(1,128)} %get-tuple-element.17.refs_2_, ...), custom_call_target="tpu_custom_call" | custom-call | tf_op jit(solution)/shard_map/store_results/pallas_call | solution.py:818
  (3 shorter events, 0.0 us)
